TPU v7x, 256 devices: a whole 4x4x8 slice. The times are simulated.
256 devices in a mesh: grp: 4 (over y_hi, core), blk: 64 (over z, x, y_lo).
Axes of the slice: x: 4, y: 4 (y_hi: 2, y_lo: 2; y = y_hi * 2 + y_lo), z: 8, core: 2. Of those that a mesh axis runs over, the one named last changes fastest.
Arguments:
- primal: float32 [2097152], P(('blk', 'grp')), may hold values from -3 to 3
- dual: float32 [1048576], P(('blk', 'grp')), may hold values from -3 to 3
- objective: float32 [2097152], P(('blk', 'grp')), may hold values from -6 to 6
- lower: float32 [2097152], P(('blk', 'grp')), may hold values from -2 to -0.5
- upper: float32 [2097152], P(('blk', 'grp')), may hold values from 0.5 to 2
- bound_kind: int32 [2097152], P(('blk', 'grp')), may hold values from 0 to 3
- rhs: float32 [1048576], P(('blk', 'grp')), may hold values from -6 to 6
- row_kind: int32 [1048576], P(('blk', 'grp')), may hold values 0 or 1
- q_tiles: float32 [4, 256, 512, 512], P('grp', 'blk'), may hold values from -0.25 to 0.25
- q_index: int32 [4, 2, 256], P('grp', None, 'blk'), may hold values from 0 to 1023
- k_tiles: float32 [4, 384, 512, 512], P('grp', 'blk'), may hold values from -0.25 to 0.25
- k_rows: int32 [4, 384], P('grp', 'blk'), may hold values from 0 to 31
- k_cols: int32 [4, 384], P('grp', 'blk'), may hold values from 0 to 1023
Outputs:
- final_primal: float32 [2097152], P(('blk', 'grp'))
- final_dual: float32 [1048576], P(('blk', 'grp'))
- primal_weight: float32 [], replicated
Inputs may be any that keep to these rules, and one draw needn't show every extreme that they name: `q_index`: row and column tile indices of Hessian tiles, within the column group. `k_rows`: row tile within the tile's dual block. `bound_kind`: 0 free, 1 lower bound only, 2 both bounds, 3 upper bound only.
All inputs are finite; a program needn't handle non-finite values. No bound on the sum of `row_kind` on one device may be relied on, other than what follows from the above.
Results may differ from a plain program's by a relative error of at most 0.00017.
Values sent between devices are 32-bit elements; how exact they have to be, the bound alone decides.
No kernel may reach another device: no remote copies, remote signals or barrier semaphores. Data moves between devices by JAX's collectives and lax.ppermute only.
A program may use at most 64 MiB of HBM per device.

v0:
```python
import functools

import jax
import jax.numpy as jnp
from jax import lax
from jax.experimental import pallas as pl
from jax.experimental.pallas import tpu as pltpu
from jax.sharding import Mesh
from jax.sharding import PartitionSpec as P

BLK = ("blk_0", "blk_1", "blk_2")
GRP = ("grp_0", "grp_1")
BLK_GRP = ("blk_0", "blk_1", "blk_2", "grp_0", "grp_1")
EPSILON = 1e-06
STEP_SCALE = 0.5
F32, BF16, I32 = jnp.float32, jnp.bfloat16, jnp.int32

NB = 64
TILE = 512
LANES = 128
NQ, NK = 4, 6
NT = NQ + NK
EXTRA = 60
VMEM_LIMIT = 16 * 1024 * 1024


def iota(shape, dim):
    return lax.broadcasted_iota(I32, shape, dim)


def lane(rows=NB):
    return iota((rows, LANES), 1)


def slot_of(lanes):
    return (lanes >> 2) & 15


def split(v, n):
    parts = []
    for _ in range(n - 1):
        p = v.astype(BF16)
        parts.append(p)
        v = v - p.astype(F32)
    parts.append(v.astype(BF16))
    return parts


def dot(a, b):
    return jnp.dot(a, b, preferred_element_type=F32)


def spread(v):
    return jnp.transpose(jnp.concatenate([v, pltpu.roll(v, 64, 1)], axis=0))[:NB]


def total(v):
    return jnp.sum(jnp.sum(v, axis=0, keepdims=True), axis=1, keepdims=True)


def extra_of(msg):
    return total(jnp.where(lane() == EXTRA, msg, 0.0))


def with_extra(msg, value):
    return jnp.where(lane() == EXTRA, value, msg)


def along(v, idx):
    return jnp.take_along_axis(v, idx, axis=1)


def column(v, c):
    return jnp.broadcast_to(v[:, c : c + 1], v.shape)


def gather_tiles(ids, tables, picks):
    ln = lane()
    t_of = along(ids & 15, slot_of(ln))
    idx = (ln & 64) + t_of * 4 + (ln & 3)
    owner = ids >> 4
    msg = jnp.zeros((NB, LANES), F32)
    for which, table in enumerate(tables):
        slots = [j for j in range(NT) if picks[j] == which]
        if not slots:
            continue
        a, b, c = split(table, 3)
        right = jnp.concatenate([a, b, c, jnp.zeros_like(a)], axis=0)
        ones = []
        for j in slots:
            o = jnp.where((ln & 63) == column(owner, j), 1.0, 0.0).astype(BF16)
            ones.append(jnp.concatenate([o, o], axis=1))
        got = dot(jnp.concatenate(ones, axis=0), right)
        for n, j in enumerate(slots):
            msg = jnp.where(slot_of(ln) == j, along(got[n * NB : (n + 1) * NB], idx), msg)
    return msg


def scatter_tiles(msg, rows, hot):
    ln = lane()
    t_of = rows & 15
    high, low = [], []
    for j in range(NT):
        e = along(msg, (ln & 64) + j * 4 + (ln & 3))
        e = jnp.where(slot_of(ln) == column(t_of, j), e, 0.0)
        a, b = split(e, 2)
        high.append(a)
        low.append(b)
    return dot(hot, jnp.concatenate(high, axis=0)) + dot(hot, jnp.concatenate(low, axis=0))


def forward_tiles(tiles_ref, rows_ref, count, first):
    ln = lane()

    def one(t, out):
        base = t * TILE
        j = first + t
        vec = [rows_ref[pl.ds(4 * j + q, 1), :] for q in range(4)]
        for qo in range(4):
            for h in range(2):
                at = pl.ds(base + qo * 128 + h * 64, 64)
                p = tiles_ref[at, 0:128] * vec[0]
                for q in range(1, 4):
                    p = p + tiles_ref[at, q * 128 : (q + 1) * 128] * vec[q]
                s = jnp.sum(p, axis=1, keepdims=True)
                out = jnp.where(ln == h * 64 + 4 * j + qo, s, out)
        return out

    return lax.fori_loop(0, count, one, jnp.zeros((NB, LANES), F32))


def transposed_tiles(tiles_ref, cols, rows_ref, first):
    def one(t, cols):
        base = t * TILE
        acc = [jnp.zeros((8, LANES), F32) for _ in range(4)]
        for qo in range(4):
            for h in range(2):
                at = pl.ds(base + qo * 128 + h * 64, 64)
                v = column(cols, h * 64 + qo)
                for q in range(4):
                    p = tiles_ref[at, q * 128 : (q + 1) * 128] * v
                    acc[q] = acc[q] + jnp.sum(p.reshape(8, 8, LANES), axis=0)
        for q in range(4):
            rows_ref[pl.ds(4 * (first + t) + q, 1), :] = jnp.sum(acc[q], axis=0, keepdims=True)
        return pltpu.roll(cols, LANES - 4, 1)

    lax.fori_loop(0, NK, one, pltpu.roll(cols, LANES - 4 * first, 1))


def join(parts, part):
    low = (lane() & 32) == 0
    blocks = []
    for k in (0, 2):
        a, b = parts[k], parts[k + 1]
        if part == 0:
            blocks.append(jnp.where(low, a, pltpu.roll(b, 32, 1)))
        else:
            blocks.append(jnp.where(low, pltpu.roll(a, LANES - 32, 1), b))
    return jnp.concatenate(blocks, axis=1)


def dual_step(parts, hot, y, rhs, kind, step):
    high, low = [], []
    for p in parts:
        a, b = split(p, 2)
        high.append(a)
        low.append(b)
    extrap = dot(jnp.concatenate(high, axis=1), hot) + dot(jnp.concatenate(low, axis=1), hot)
    new = y + step * (rhs - extrap)
    new = jnp.where(kind == 1.0, jnp.maximum(new, 0.0), new)
    moved = new - y
    return new, total(moved * moved)


def new_weight(weight, dual_sq, primal_sq):
    return jnp.sqrt(weight * jnp.sqrt((dual_sq + EPSILON) / (primal_sq + EPSILON)))


def start_kernel(q_index, k_cols, primal, objective, lower, upper, bound_kind, out):
    kind = bound_kind[...]
    low = jnp.where((kind == 1) | (kind == 2), lower[...], -jnp.inf)
    high = jnp.where((kind == 2) | (kind == 3), upper[...], jnp.inf)
    for k, v in enumerate((primal[...], objective[...], low, high)):
        out[pl.ds(k, NB, stride=5), :] = spread(v)
    ln = lane(8)
    ids = jnp.zeros((8, LANES), F32)
    for j in range(NQ):
        ids = jnp.where(ln == j, q_index[1, j].astype(F32), ids)
        ids = jnp.where(ln == NT + j, q_index[0, j].astype(F32), ids)
    for j in range(NK):
        ids = jnp.where(ln == NQ + j, k_cols[0, j].astype(F32), ids)
    out[pl.ds(4, NB, stride=5), :] = jnp.broadcast_to(ids[:1], (NB, LANES))


def dual_start_kernel(k_rows, dual, rhs, row_kind, out):
    out[0:NB] = spread(jnp.concatenate([dual[...], rhs[...]], axis=0))
    ids = jnp.zeros((8, LANES), F32)
    ln = lane(8)
    for j in range(NK):
        ids = jnp.where(slot_of(ln) == NQ + j, k_rows[0, j].astype(F32), ids)
    kinds = spread(jnp.concatenate([row_kind[...].astype(F32), jnp.zeros((32, LANES), F32)], axis=0))
    out[NB : 2 * NB] = kinds
    out[2 * NB :] = ids


def first_gather_kernel(got, msg):
    ids = got[pl.ds(4, NB, stride=5), :].astype(I32)
    x = got[pl.ds(0, NB, stride=5), :]
    msg[...] = gather_tiles(ids, [x], [0] * NQ + [-1] * NK)


def tables_kernel(got, rows_out, hot_out):
    ids = got[pl.ds(4, NB, stride=5), :].astype(I32)
    ln = lane()
    rows = jnp.where(ln < NQ, pltpu.roll(ids, LANES - NT, 1), ids)
    rows_out[...] = rows
    owner = (rows >> 4).astype(F32)
    flat = jnp.transpose(jnp.concatenate([owner, owner], axis=0))
    sub = iota((NB, LANES), 0).astype(F32)
    l1 = lane(1)
    for c in range(NT // 2):
        row = jnp.where(l1 < 64, flat[2 * c : 2 * c + 1], flat[2 * c + 1 : 2 * c + 2])
        hot_out[:, c * LANES : (c + 1) * LANES] = jnp.where(sub == row, 1.0, 0.0).astype(BF16)


def dual_tables_kernel(me, p0, p1, p2, p3, y, rhs, kind, put, take):
    parts = [p0, p1, p2, p3]
    y[...] = join([p[0:NB] for p in parts], 0)
    rhs[...] = join([p[0:NB] for p in parts], 1)
    kind[...] = join([p[NB : 2 * NB] for p in parts], 0)
    mine = me[0]
    rel = []
    for p in parts:
        r = p[2 * NB :].astype(I32)
        rel.append((((r >> 3) ^ mine) << 3) | (r & 7))
    ln = lane(LANES)
    sub = iota((LANES, LANES), 0)
    sub_ok = (slot_of(sub) >= NQ) & (slot_of(sub) < NT)
    for p in range(4):
        r = jnp.transpose(jnp.broadcast_to(rel[p][:1].astype(F32), (LANES, LANES))).astype(I32)
        same = ((ln & 64) == (sub & 64)) & ((ln & 3) == (sub & 3)) & sub_ok
        for kk in range(2):
            tile = (2 * kk + ((ln >> 5) & 1)) * 8 + ((ln >> 2) & 7)
            hit = same & (tile == r)
            put[p * LANES : (p + 1) * LANES, kk * LANES : (kk + 1) * LANES] = jnp.where(hit, 1.0, 0.0).astype(BF16)
    r = jnp.broadcast_to(rel[0][:1], (LANES, LANES))
    lane_ok = (slot_of(ln) >= NQ) & (slot_of(ln) < NT)
    for kk in range(2):
        tile = (2 * kk + ((sub >> 5) & 1)) * 8 + ((sub >> 2) & 7)
        hit = ((ln & 64) == (sub & 64)) & ((ln & 3) == (sub & 3)) & lane_ok & (tile == r)
        take[kk * LANES : (kk + 1) * LANES, :] = jnp.where(hit, 1.0, 0.0).astype(BF16)


def take_rows(y, take):
    a, b = split(y, 2)
    return dot(a, take) + dot(b, take)


def transposed_kernel(y, take, tiles, out, rows):
    rows[...] = jnp.zeros((NB, LANES), F32)
    transposed_tiles(tiles, take_rows(y[...], take[...]), rows, NQ)
    out[...] = spread(rows[...])


def first_products_kernel(msg, trans, tiles, out, rows):
    rows[...] = spread(msg[...])
    out[...] = with_extra(forward_tiles(tiles, rows, NQ, 0) - trans[...], 0.0)


def primal_step(msg, rows, hot, got, x, weight):
    c = got[pl.ds(1, NB, stride=5), :]
    low = got[pl.ds(2, NB, stride=5), :]
    high = got[pl.ds(3, NB, stride=5), :]
    grad = scatter_tiles(msg, rows, hot) + c
    new = jnp.minimum(jnp.maximum(x - (STEP_SCALE / weight) * grad, low), high)
    moved = new - x
    return new, total(moved * moved)


def first_primal_kernel(msg, got, rows, hot, x_out, out):
    x = got[pl.ds(0, NB, stride=5), :]
    new, moved = primal_step(msg[...], rows[...], hot[...], got, x, jnp.ones((1, 1), F32))
    x_out[...] = new
    ids = got[pl.ds(4, NB, stride=5), :].astype(I32)
    out[...] = with_extra(gather_tiles(ids, [new, 2.0 * new - x], [0] * NQ + [1] * NK), moved)


def second_primal_kernel(msg, got, rows, hot, x_in, primal_sq, weight_out, out):
    x = x_in[...]
    m = msg[...]
    weight = new_weight(jnp.ones((1, 1), F32), extra_of(m), primal_sq[...])
    weight_out[...] = weight
    new, moved = primal_step(m, rows[...], hot[...], got, x, weight)
    ids = got[pl.ds(4, NB, stride=5), :].astype(I32)
    out[pl.ds(0, NB, stride=2), :] = with_extra(gather_tiles(ids, [2.0 * new - x], [-1] * NQ + [0] * NK), moved)
    out[pl.ds(1, NB, stride=2), :] = new


def constraint_kernel(msg, tiles, out, vec, rows):
    m = msg[...]
    rows[...] = spread(m)
    vec[...] = rows[...]
    out[...] = with_extra(forward_tiles(tiles, rows, NK, NQ), extra_of(m))


def last_constraint_kernel(msg, tiles, out, final, rows):
    m = msg[pl.ds(0, NB, stride=2), :]
    final[...] = spread(msg[pl.ds(1, NB, stride=2), :])
    rows[...] = spread(m)
    out[...] = with_extra(forward_tiles(tiles, rows, NK, NQ), extra_of(m))


def hessian_kernel(vec, tiles, out):
    out[...] = forward_tiles(tiles, vec, NQ, 0)


def primal_total(parts):
    s = parts[0][0:1, EXTRA : EXTRA + 1]
    for p in parts[1:]:
        s = s + p[0:1, EXTRA : EXTRA + 1]
    return s


def dual_kernel(p0, p1, p2, p3, put, take, y, rhs, kind, hess, tiles, y_out, primal_sq, out, rows):
    parts = [p[...] for p in (p0, p1, p2, p3)]
    new, moved = dual_step(parts, put[...], y[...], rhs[...], kind[...], STEP_SCALE)
    y_out[...] = new
    primal_sq[...] = primal_total(parts)
    rows[...] = jnp.zeros((NB, LANES), F32)
    transposed_tiles(tiles, take_rows(new, take[...]), rows, NQ)
    out[...] = with_extra(hess[...] - spread(rows[...]), moved)


def last_dual_kernel(p0, p1, p2, p3, put, y, rhs, kind, weight, dual_out, primal_sq, out):
    parts = [p[...] for p in (p0, p1, p2, p3)]
    new, moved = dual_step(parts, put[...], y[...], rhs[...], kind[...], STEP_SCALE * weight[...])
    primal_sq[...] = primal_total(parts)
    dual_out[...] = spread(new[:, :LANES])[:32]
    out[...] = jnp.broadcast_to(moved, (NB, LANES))


def last_kernel(msg, weight, primal_sq, out):
    dual_sq = jnp.sum(msg[:, 0:1], axis=0, keepdims=True)
    out[...] = new_weight(weight[...], dual_sq, primal_sq[...])


def call(kernel, outs, *args, smem=0, scratch=(), cost=0):
    v = pl.BlockSpec(memory_space=pltpu.VMEM)
    s = pl.BlockSpec(memory_space=pltpu.SMEM)
    shapes = [jax.ShapeDtypeStruct(*o) for o in outs]
    res = pl.pallas_call(
        kernel,
        out_shape=shapes,
        in_specs=[s] * smem + [v] * (len(args) - smem),
        out_specs=[v] * len(shapes),
        scratch_shapes=list(scratch),
        compiler_params=pltpu.CompilerParams(vmem_limit_bytes=VMEM_LIMIT),
        cost_estimate=pl.CostEstimate(flops=cost, bytes_accessed=cost, transcendentals=0) if cost else None,
    )(*args)
    return res[0] if len(outs) == 1 else res


ROWS = ((NB, LANES), F32)
ROWS_SCRATCH = (pltpu.VMEM((NB, LANES), F32),)


def exchange(rows):
    k = rows.shape[0] // NB
    out = lax.all_to_all(rows.reshape(NB, 1, k * LANES), BLK, 0, 0, tiled=True)
    return out.reshape(NB * k, LANES)


def over_group(rows):
    return [rows] + [lax.ppermute(rows, GRP, [(i, i ^ k) for i in range(4)]) for k in (1, 2, 3)]


def shards(primal, dual, objective, lower, upper, bound_kind, rhs, row_kind, q_tiles, q_index, k_tiles, k_rows, k_cols):
    hess = q_tiles.reshape(NQ * TILE, TILE)
    cons = k_tiles.reshape(NK * TILE, TILE)
    me = lax.axis_index(GRP).astype(I32).reshape(1)

    def wide(v):
        return v.reshape(-1, LANES)

    first = call(start_kernel, [((5 * NB, LANES), F32)], q_index[0], k_cols, wide(primal), wide(objective), wide(lower),
                 wide(upper), wide(bound_kind), smem=2)
    block = call(dual_start_kernel, [((2 * NB + 8, LANES), F32)], k_rows, wide(dual), wide(rhs), wide(row_kind), smem=1)
    parts = over_group(block)
    got = exchange(first)
    msg = call(first_gather_kernel, [ROWS], got)
    want = exchange(msg)
    rows, hot = call(tables_kernel, [((NB, LANES), I32), ((NB, NT * NB), BF16)], got, cost=10000000)
    wide_block = ((NB, 2 * LANES), F32)
    y, b, kind, put, take = call(
        dual_tables_kernel,
        [wide_block, wide_block, wide_block, ((4 * LANES, 2 * LANES), BF16), ((2 * LANES, LANES), BF16)],
        me, *parts, smem=1, cost=10000000)
    trans = call(transposed_kernel, [ROWS], y, take, cons, scratch=ROWS_SCRATCH, cost=10000000)
    grads = exchange(call(first_products_kernel, [ROWS], want, trans, hess, scratch=ROWS_SCRATCH))
    x, msg = call(first_primal_kernel, [ROWS, ROWS], grads, got, rows, hot)
    want = exchange(msg)
    prods, vec = call(constraint_kernel, [ROWS, ROWS], want, cons, scratch=ROWS_SCRATCH)
    parts = over_group(prods)
    hess_prod = call(hessian_kernel, [ROWS], vec, hess, cost=10000000)
    y, primal_sq, msg = call(dual_kernel, [wide_block, ((1, 1), F32), ROWS], *parts, put, take, y, b, kind, hess_prod, cons,
                             scratch=ROWS_SCRATCH)
    grads = exchange(msg)
    weight, both = call(second_primal_kernel, [((1, 1), F32), ((2 * NB, LANES), F32)], grads, got, rows, hot, x, primal_sq)
    want = exchange(both)
    prods, final = call(last_constraint_kernel, [ROWS, ROWS], want, cons, scratch=ROWS_SCRATCH)
    parts = over_group(prods)
    dual_out, primal_sq, msg = call(last_dual_kernel, [((32, LANES), F32), ((1, 1), F32), ROWS], *parts, put, y, b, kind, weight)
    weight = call(last_kernel, [((1, 1), F32)], exchange(msg), weight, primal_sq)
    return final.reshape(-1), dual_out.reshape(-1), weight.reshape(())


def solution(mesh):
    finer = Mesh(mesh.devices.reshape(2, 2, 8, 4, 2), ("grp_0", "grp_1", "blk_0", "blk_1", "blk_2"))
    placed = (P(BLK_GRP),) * 8 + (
        P(GRP, BLK, None, None),
        P(GRP, None, BLK),
        P(GRP, BLK, None, None),
        P(GRP, BLK),
        P(GRP, BLK),
    )
    return jax.shard_map(shards, mesh=finer, in_specs=placed, out_specs=(P(BLK_GRP), P(BLK_GRP), P()), check_vma=False)
```

profile of v0, /device:TPU:1, one launch (start us, length us, event | category | flops | bytes accessed | tf_op | source)
XLA Modules:
  0.0 153.4 jit_solution(10903360635907775203)
XLA Ops:
  5.8 1.4 shard_map.148
  7.1 13.5 %all-to-all-start = ((f32[64,1,640]{2,1,0:T(1,128)}), f32[64,1,640]{2,1,0:T(1,128)S(1)}, u32[]{:S(2)}, u32[]{:S(2)}) async-start(f32[64,1,640]{2,1,0:T(1,128)} %bitcast.6), calls=%async_computation | async-start | bytes 327680 | tf_op jit(solution)/shard_map/all_to_all | solution.py:369
  24.1 1.0 collective-permute-start
  25.2 2.6 %collective-permute-start.1 = (f32[136,128]{1,0:T(8,128)S(1)}, f32[136,128]{1,0:T(8,128)S(1)}, u32[]{:S(2)}, u32[]{:S(2)}) collective-permute-start(f32[136,128]{1,0:T(8,128)S(1)} %shard_map.150.p0), channel_id=1, source_target_pairs={{0,128},{64,192},{128,0},{192,64},{1,129},{65,193},{129,1},{193,65... | collective-permute-start | bytes 208904 | tf_op jit(solution)/shard_map/ppermute | solution.py:374
  28.4 2.2 %all-to-all-done = f32[64,1,640]{2,1,0:T(1,128)S(1)} async-done(((f32[64,1,640]{2,1,0:T(1,128)}), f32[64,1,640]{2,1,0:T(1,128)S(1)}, u32[]{:S(2)}, u32[]{:S(2)}) %all-to-all-start) | async-done | bytes 163872 | tf_op jit(solution)/shard_map/all_to_all | solution.py:369
  31.6 8.7 %all-to-all-start.1 = ((f32[64,1,128]{2,1,0:T(1,128)}), f32[64,1,128]{2,1,0:T(1,128)S(1)}, u32[]{:S(2)}, u32[]{:S(2)}) async-start(f32[64,1,128]{2,1,0:T(1,128)} %bitcast.9), calls=%async_computation.1 | async-start | bytes 65536 | tf_op jit(solution)/shard_map/all_to_all | solution.py:369
  40.6 2.8 %copy-done = f32[1,6,512,512]{3,2,1,0:T(8,128)S(1)} copy-done((f32[1,6,512,512]{3,2,1,0:T(8,128)S(1)}, f32[1,6,512,512]{3,2,1,0:T(8,128)}, u32[]{:S(2)}) %copy-start) | copy-done | bytes 6291480
  43.4 1.3 shard_map.152.trans
  44.7 4.9 %all-to-all-done.1 = f32[64,1,128]{2,1,0:T(1,128)S(1)} async-done(((f32[64,1,128]{2,1,0:T(1,128)}), f32[64,1,128]{2,1,0:T(1,128)S(1)}, u32[]{:S(2)}, u32[]{:S(2)}) %all-to-all-start.1) | async-done | bytes 32800 | tf_op jit(solution)/shard_map/all_to_all | solution.py:369
  49.6 2.2 %copy-done.2 = f32[1,4,512,512]{3,2,1,0:T(8,128)S(1)} copy-done((f32[1,4,512,512]{3,2,1,0:T(8,128)S(1)}, f32[1,4,512,512]{3,2,1,0:T(8,128)}, u32[]{:S(2)}) %copy-start.2) | copy-done | bytes 4194328
  51.8 1.3 shard_map.153
  53.1 5.8 %all-to-all-start.2 = ((f32[64,1,128]{2,1,0:T(1,128)}), f32[64,1,128]{2,1,0:T(1,128)S(1)}, u32[]{:S(2)}, u32[]{:S(2)}) async-start(f32[64,1,128]{2,1,0:T(1,128)} %bitcast.18), calls=%async_computation.2 | async-start | bytes 65536 | tf_op jit(solution)/shard_map/all_to_all | solution.py:369
  59.0 9.1 %all-to-all-done.2 = f32[64,1,128]{2,1,0:T(1,128)S(1)} async-done(((f32[64,1,128]{2,1,0:T(1,128)}), f32[64,1,128]{2,1,0:T(1,128)S(1)}, u32[]{:S(2)}, u32[]{:S(2)}) %all-to-all-start.2) | async-done | bytes 32800 | tf_op jit(solution)/shard_map/all_to_all | solution.py:369
  69.0 13.1 %all_to_all.35 = f32[64,1,128]{2,1,0:T(1,128)S(1)} all-to-all(f32[64,1,128]{2,1,0:T(1,128)S(1)} %bitcast.65), channel_id=1, replica_groups=mesh['grp_0'=2,'grp_1'=2,'blk_0'=8,'blk_1'=4,'blk_2'=2] {'blk_0','blk_1'..., dimensions={0} | all-to-all | bytes 65536 | tf_op jit(solution)/shard_map/all_to_all | solution.py:369
  82.2 2.8 %copy-done.1 = f32[1,6,512,512]{3,2,1,0:T(8,128)S(1)} copy-done((f32[1,6,512,512]{3,2,1,0:T(8,128)S(1)}, f32[1,6,512,512]{3,2,1,0:T(8,128)}, u32[]{:S(2)}) %copy-start.1) | copy-done | bytes 6291480
  85.0 1.1 shard_map.156
  86.1 3.3 %collective-permute-start.3 = (f32[64,128]{1,0:T(8,128)S(1)}, f32[64,128]{1,0:T(8,128)S(1)}, u32[]{:S(2)}, u32[]{:S(2)}) collective-permute-start(f32[64,128]{1,0:T(8,128)S(1)} %get-tuple-element.29.p0), channel_id=1, source_target_pairs={{0,64},{64,0},{128,192},{192,128},{1,65},{65,1},{129,193},{193,129... | collective-permute-start | bytes 98312 | tf_op jit(solution)/shard_map/ppermute | solution.py:374
  89.4 2.6 %collective-permute-start.4 = (f32[64,128]{1,0:T(8,128)S(1)}, f32[64,128]{1,0:T(8,128)S(1)}, u32[]{:S(2)}, u32[]{:S(2)}) collective-permute-start(f32[64,128]{1,0:T(8,128)S(1)} %get-tuple-element.29.p0), channel_id=1, source_target_pairs={{0,128},{64,192},{128,0},{192,64},{1,129},{65,193},{129,1},{193,65... | collective-permute-start | bytes 98312 | tf_op jit(solution)/shard_map/ppermute | solution.py:374
  92.6 2.2 %copy-done.3 = f32[1,4,512,512]{3,2,1,0:T(8,128)S(1)} copy-done((f32[1,4,512,512]{3,2,1,0:T(8,128)S(1)}, f32[1,4,512,512]{3,2,1,0:T(8,128)}, u32[]{:S(2)}) %copy-start.3) | copy-done | bytes 4194328
  95.4 1.5 collective-permute-done.5.p3
  96.9 1.9 %shard_map.158 = (f32[64,256]{1,0:T(8,128)S(1)}, f32[1,1]{1,0:T(1,128)}, f32[64,128]{1,0:T(8,128)S(1)}) custom-call(f32[64,128]{1,0:T(8,128)S(1)} %get-tuple-element.29.p0, f32[64,128]{1,0:T(8,128)S(1)} %collective-permute-done.3.p1, f32[64,128]{1,0:T(8,128)S(1)} %collective-permute-done.4.p2, f32[64,128]{1,0:T(8,128)S(1)} %collective-permute-done.5.p3, ...), custom_call_target="tpu_custom_call" | custom-call | tf_op jit(solution)/shard_map/pallas_call | solution.py:351
  98.8 13.1 %all_to_all.36 = f32[64,1,128]{2,1,0:T(1,128)S(1)} all-to-all(f32[64,1,128]{2,1,0:T(1,128)S(1)} %bitcast.64), channel_id=1, replica_groups=mesh['grp_0'=2,'grp_1'=2,'blk_0'=8,'blk_1'=4,'blk_2'=2] {'blk_0','blk_1'..., dimensions={0} | all-to-all | bytes 65536 | tf_op jit(solution)/shard_map/all_to_all | solution.py:369
  111.9 1.5 shard_map.159
  113.4 13.5 %all_to_all.37 = f32[64,1,256]{2,1,0:T(1,128)S(1)} all-to-all(f32[64,1,256]{2,1,0:T(1,128)S(1)} %bitcast.57), channel_id=1, replica_groups=mesh['grp_0'=2,'grp_1'=2,'blk_0'=8,'blk_1'=4,'blk_2'=2] {'blk_0','blk_1'..., dimensions={0} | all-to-all | bytes 131072 | tf_op jit(solution)/shard_map/all_to_all | solution.py:369
  126.9 1.5 %shard_map.160 = (f32[64,128]{1,0:T(8,128)S(1)}, f32[64,128]{1,0:T(8,128)}) custom-call(f32[128,128]{1,0:T(8,128)S(1)} %bitcast.51, f32[3072,512]{1,0:T(8,128)S(1)} %bitcast.44), custom_call_target="tpu_custom_call" | custom-call | tf_op jit(solution)/shard_map/pallas_call | solution.py:351
  128.4 2.7 %collective-permute-start.6 = (f32[64,128]{1,0:T(8,128)S(1)}, f32[64,128]{1,0:T(8,128)S(1)}, u32[]{:S(2)}, u32[]{:S(2)}) collective-permute-start(f32[64,128]{1,0:T(8,128)S(1)} %get-tuple-element.39.p0), channel_id=1, source_target_pairs={{0,64},{64,0},{128,192},{192,128},{1,65},{65,1},{129,193},{193,129... | collective-permute-start | bytes 98312 | tf_op jit(solution)/shard_map/ppermute | solution.py:374
  132.1 2.2 %collective-permute-start.8 = (f32[64,128]{1,0:T(8,128)S(1)}, f32[64,128]{1,0:T(8,128)S(1)}, u32[]{:S(2)}, u32[]{:S(2)}) collective-permute-start(f32[64,128]{1,0:T(8,128)S(1)} %get-tuple-element.39.p0), channel_id=1, source_target_pairs={{0,192},{64,128},{128,64},{192,0},{1,193},{65,129},{129,65},{193,1... | collective-permute-start | bytes 98312 | tf_op jit(solution)/shard_map/ppermute | solution.py:374
  134.3 1.1 collective-permute-done.7.p2
  135.4 1.5 collective-permute-done.8.p3
  136.9 1.6 %shard_map.161 = (f32[32,128]{1,0:T(8,128)}, f32[1,1]{1,0:T(1,128)}, f32[64,128]{1,0:T(8,128)S(1)}) custom-call(f32[64,128]{1,0:T(8,128)S(1)} %get-tuple-element.39.p0, f32[64,128]{1,0:T(8,128)S(1)} %collective-permute-done.6.p1, f32[64,128]{1,0:T(8,128)S(1)} %collective-permute-done.7.p2, f32[64,128]{1,0:T(8,128)S(1)} %collective-permute-done.8.p3, ...), custom_call_target="tpu_custom_call" | custom-call | tf_op jit(solution)/shard_map/pallas_call | solution.py:351
  138.5 13.1 %all_to_all.38 = f32[64,1,128]{2,1,0:T(1,128)S(1)} all-to-all(f32[64,1,128]{2,1,0:T(1,128)S(1)} %bitcast.63), channel_id=1, replica_groups=mesh['grp_0'=2,'grp_1'=2,'blk_0'=8,'blk_1'=4,'blk_2'=2] {'blk_0','blk_1'..., dimensions={0} | all-to-all | bytes 65536 | tf_op jit(solution)/shard_map/all_to_all | solution.py:369
  151.6 1.8 %shard_map.162 = f32[1,1]{1,0:T(1,128)} custom-call(f32[64,128]{1,0:T(8,128)S(1)} %bitcast.55, f32[1,1]{1,0:T(1,128)} %get-tuple-element.41.weight, f32[1,1]{1,0:T(1,128)} %get-tuple-element.44.primal_sq), custom_call_target="tpu_custom_call" | custom-call | tf_op jit(solution)/shard_map/pallas_call | solution.py:351
  (46 shorter events, 13.6 us)
Async XLA Ops:
  0.6 0.8 copy-start.4
  1.4 0.8 copy-start.5
  2.1 0.8 copy-start.6
  2.9 0.8 copy-start.7
  3.7 0.8 copy-start.8
  4.4 0.7 copy-start.12
  5.1 0.7 copy-start.13
  7.1 23.5 %all-to-all-start = ((f32[64,1,640]{2,1,0:T(1,128)}), f32[64,1,640]{2,1,0:T(1,128)S(1)}, u32[]{:S(2)}, u32[]{:S(2)}) async-start(f32[64,1,640]{2,1,0:T(1,128)} %bitcast.6), calls=%async_computation | async-start | bytes 327680 | tf_op jit(solution)/shard_map/all_to_all | solution.py:369
  20.6 0.7 copy-start.9
  21.4 0.7 copy-start.10
  22.1 0.7 copy-start.11
  22.8 0.7 copy-start.14
  24.1 16.2 %collective-permute-start = (f32[136,128]{1,0:T(8,128)S(1)}, f32[136,128]{1,0:T(8,128)S(1)}, u32[]{:S(2)}, u32[]{:S(2)}) collective-permute-start(f32[136,128]{1,0:T(8,128)S(1)} %shard_map.150.p0), channel_id=1, source_target_pairs={{0,64},{64,0},{128,192},{192,128},{1,65},{65,1},{129,193},{193,129... | collective-permute-start | bytes 208904 | tf_op jit(solution)/shard_map/ppermute | solution.py:374
  25.2 15.1 %collective-permute-start.1 = (f32[136,128]{1,0:T(8,128)S(1)}, f32[136,128]{1,0:T(8,128)S(1)}, u32[]{:S(2)}, u32[]{:S(2)}) collective-permute-start(f32[136,128]{1,0:T(8,128)S(1)} %shard_map.150.p0), channel_id=1, source_target_pairs={{0,128},{64,192},{128,0},{192,64},{1,129},{65,193},{129,1},{193,65... | collective-permute-start | bytes 208904 | tf_op jit(solution)/shard_map/ppermute | solution.py:374
  27.8 12.5 %collective-permute-start.2 = (f32[136,128]{1,0:T(8,128)S(1)}, f32[136,128]{1,0:T(8,128)S(1)}, u32[]{:S(2)}, u32[]{:S(2)}) collective-permute-start(f32[136,128]{1,0:T(8,128)S(1)} %shard_map.150.p0), channel_id=1, source_target_pairs={{0,192},{64,128},{128,64},{192,0},{1,193},{65,129},{129,65},{193,1... | collective-permute-start | bytes 208904 | tf_op jit(solution)/shard_map/ppermute | solution.py:374
  31.6 18.0 %all-to-all-start.1 = ((f32[64,1,128]{2,1,0:T(1,128)}), f32[64,1,128]{2,1,0:T(1,128)S(1)}, u32[]{:S(2)}, u32[]{:S(2)}) async-start(f32[64,1,128]{2,1,0:T(1,128)} %bitcast.9), calls=%async_computation.1 | async-start | bytes 65536 | tf_op jit(solution)/shard_map/all_to_all | solution.py:369
  40.6 2.8 %copy-start = (f32[1,6,512,512]{3,2,1,0:T(8,128)S(1)}, f32[1,6,512,512]{3,2,1,0:T(8,128)}, u32[]{:S(2)}) copy-start(f32[1,6,512,512]{3,2,1,0:T(8,128)} %param.23) | copy-start | bytes 18874372
  49.6 2.2 %copy-start.2 = (f32[1,4,512,512]{3,2,1,0:T(8,128)S(1)}, f32[1,4,512,512]{3,2,1,0:T(8,128)}, u32[]{:S(2)}) copy-start(f32[1,4,512,512]{3,2,1,0:T(8,128)} %param.21) | copy-start | bytes 12582916
  51.8 45.1 %slice-start = ((s8[6291456]{0:T(1024)(128)(4,1)}), s8[2097152]{0:T(1024)(128)(4,1)S(1)}, s32[]{:S(2)}) async-start(s8[6291456]{0:T(1024)(128)(4,1)} %bitcast.41), calls=%async_computation.7 | async-start | bytes 4194304
  53.1 15.0 %all-to-all-start.2 = ((f32[64,1,128]{2,1,0:T(1,128)}), f32[64,1,128]{2,1,0:T(1,128)S(1)}, u32[]{:S(2)}, u32[]{:S(2)}) async-start(f32[64,1,128]{2,1,0:T(1,128)} %bitcast.18), calls=%async_computation.2 | async-start | bytes 65536 | tf_op jit(solution)/shard_map/all_to_all | solution.py:369
  82.2 2.8 %copy-start.1 = (f32[1,6,512,512]{3,2,1,0:T(8,128)S(1)}, f32[1,6,512,512]{3,2,1,0:T(8,128)}, u32[]{:S(2)}) copy-start(f32[1,6,512,512]{3,2,1,0:T(8,128)} %param.23) | copy-start | bytes 18874372
  85.0 11.9 %slice-start.1 = ((s8[6291456]{0:T(1024)(128)(4,1)}), s8[4194304]{0:T(1024)(128)(4,1)S(1)}, s32[]{:S(2)}) async-start(s8[6291456]{0:T(1024)(128)(4,1)} %bitcast.41), calls=%async_computation.8 | async-start | bytes 8388608
  86.1 9.3 %collective-permute-start.3 = (f32[64,128]{1,0:T(8,128)S(1)}, f32[64,128]{1,0:T(8,128)S(1)}, u32[]{:S(2)}, u32[]{:S(2)}) collective-permute-start(f32[64,128]{1,0:T(8,128)S(1)} %get-tuple-element.29.p0), channel_id=1, source_target_pairs={{0,64},{64,0},{128,192},{192,128},{1,65},{65,1},{129,193},{193,129... | collective-permute-start | bytes 98312 | tf_op jit(solution)/shard_map/ppermute | solution.py:374
  89.4 6.0 %collective-permute-start.4 = (f32[64,128]{1,0:T(8,128)S(1)}, f32[64,128]{1,0:T(8,128)S(1)}, u32[]{:S(2)}, u32[]{:S(2)}) collective-permute-start(f32[64,128]{1,0:T(8,128)S(1)} %get-tuple-element.29.p0), channel_id=1, source_target_pairs={{0,128},{64,192},{128,0},{192,64},{1,129},{65,193},{129,1},{193,65... | collective-permute-start | bytes 98312 | tf_op jit(solution)/shard_map/ppermute | solution.py:374
  92.0 4.9 %collective-permute-start.5 = (f32[64,128]{1,0:T(8,128)S(1)}, f32[64,128]{1,0:T(8,128)S(1)}, u32[]{:S(2)}, u32[]{:S(2)}) collective-permute-start(f32[64,128]{1,0:T(8,128)S(1)} %get-tuple-element.29.p0), channel_id=1, source_target_pairs={{0,192},{64,128},{128,64},{192,0},{1,193},{65,129},{129,65},{193,1... | collective-permute-start | bytes 98312 | tf_op jit(solution)/shard_map/ppermute | solution.py:374
  92.6 2.2 %copy-start.3 = (f32[1,4,512,512]{3,2,1,0:T(8,128)S(1)}, f32[1,4,512,512]{3,2,1,0:T(8,128)}, u32[]{:S(2)}) copy-start(f32[1,4,512,512]{3,2,1,0:T(8,128)} %param.21) | copy-start | bytes 12582916
  128.4 5.8 %collective-permute-start.6 = (f32[64,128]{1,0:T(8,128)S(1)}, f32[64,128]{1,0:T(8,128)S(1)}, u32[]{:S(2)}, u32[]{:S(2)}) collective-permute-start(f32[64,128]{1,0:T(8,128)S(1)} %get-tuple-element.39.p0), channel_id=1, source_target_pairs={{0,64},{64,0},{128,192},{192,128},{1,65},{65,1},{129,193},{193,129... | collective-permute-start | bytes 98312 | tf_op jit(solution)/shard_map/ppermute | solution.py:374
  131.1 4.3 %collective-permute-start.7 = (f32[64,128]{1,0:T(8,128)S(1)}, f32[64,128]{1,0:T(8,128)S(1)}, u32[]{:S(2)}, u32[]{:S(2)}) collective-permute-start(f32[64,128]{1,0:T(8,128)S(1)} %get-tuple-element.39.p0), channel_id=1, source_target_pairs={{0,128},{64,192},{128,0},{192,64},{1,129},{65,193},{129,1},{193,65... | collective-permute-start | bytes 98312 | tf_op jit(solution)/shard_map/ppermute | solution.py:374
  132.1 4.8 %collective-permute-start.8 = (f32[64,128]{1,0:T(8,128)S(1)}, f32[64,128]{1,0:T(8,128)S(1)}, u32[]{:S(2)}, u32[]{:S(2)}) collective-permute-start(f32[64,128]{1,0:T(8,128)S(1)} %get-tuple-element.39.p0), channel_id=1, source_target_pairs={{0,192},{64,128},{128,64},{192,0},{1,193},{65,129},{129,65},{193,1... | collective-permute-start | bytes 98312 | tf_op jit(solution)/shard_map/ppermute | solution.py:374
where the time goes:
time: 154 us; the launch traced here: 153 us
  blocking collectives  52.8 us (34%)
  starting transfers between devices  44.6 us (29%)
  waiting for transfers between devices  20.3 us (13%)
  local copies, waits for them, and re-layouts  17.9 us (12%)
  Pallas kernels  16.9 us (11%)
    all_to_all x4, blocking collectives, exchange(): out = lax.all_to_all(rows.reshape(NB, 1, k * LANES), BLK, 0, 0, tiled=True)  52.8 us
    all_to_all x3, starting transfers between devices, exchange(): out = lax.all_to_all(rows.reshape(NB, 1, k * LANES), BLK, 0, 0, tiled=True)  28 us
    unnamed x34, local copies, waits for them, and re-layouts  17.9 us
    pallas_call x15, Pallas kernels, call(): pl.pallas_call(kernel, out_shape=shapes, in_specs=[s] * smem + [v] * (len...  16.9 us
    ppermute x9, starting transfers between devices, over_group(): lax.ppermute(rows, GRP, [(i, i ^ k) for i in range(4)])  16.7 us
    all_to_all x3, waiting for transfers between devices, exchange(): out = lax.all_to_all(rows.reshape(NB, 1, k * LANES), BLK, 0, 0, tiled=True)  16.2 us
    ppermute x9, waiting for transfers between devices, over_group(): lax.ppermute(rows, GRP, [(i, i ^ k) for i in range(4)])  4.1 us
  transfers between devices with their start and end apart: 12, of which 6 were waited for; matrix products, arithmetic and copies ran while one was open for 0% of the time, Pallas kernels for 3%

commit v1 on v0

--- a/solution.py
+++ b/solution.py
@@ -21,7 +21,8 @@
 NQ, NK = 4, 6
 NT = NQ + NK
 EXTRA = 60
-VMEM_LIMIT = 16 * 1024 * 1024
+VMEM_LIMIT = 8 * 1024 * 1024
+COST = 10000000000
 
 
 def iota(shape, dim):
@@ -113,15 +114,14 @@
     ln = lane()
 
     def one(t, out):
-        base = t * TILE
         j = first + t
         vec = [rows_ref[pl.ds(4 * j + q, 1), :] for q in range(4)]
         for qo in range(4):
             for h in range(2):
-                at = pl.ds(base + qo * 128 + h * 64, 64)
-                p = tiles_ref[at, 0:128] * vec[0]
+                at = pl.ds(qo * 128 + h * 64, 64)
+                p = tiles_ref[0, t, at, 0:128] * vec[0]
                 for q in range(1, 4):
-                    p = p + tiles_ref[at, q * 128 : (q + 1) * 128] * vec[q]
+                    p = p + tiles_ref[0, t, at, q * 128 : (q + 1) * 128] * vec[q]
                 s = jnp.sum(p, axis=1, keepdims=True)
                 out = jnp.where(ln == h * 64 + 4 * j + qo, s, out)
         return out
@@ -131,14 +131,13 @@
 
 def transposed_tiles(tiles_ref, cols, rows_ref, first):
     def one(t, cols):
-        base = t * TILE
         acc = [jnp.zeros((8, LANES), F32) for _ in range(4)]
         for qo in range(4):
             for h in range(2):
-                at = pl.ds(base + qo * 128 + h * 64, 64)
+                at = pl.ds(qo * 128 + h * 64, 64)
                 v = column(cols, h * 64 + qo)
                 for q in range(4):
-                    p = tiles_ref[at, q * 128 : (q + 1) * 128] * v
+                    p = tiles_ref[0, t, at, q * 128 : (q + 1) * 128] * v
                     acc[q] = acc[q] + jnp.sum(p.reshape(8, 8, LANES), axis=0)
         for q in range(4):
             rows_ref[pl.ds(4 * (first + t) + q, 1), :] = jnp.sum(acc[q], axis=0, keepdims=True)
@@ -176,40 +175,56 @@
     return jnp.sqrt(weight * jnp.sqrt((dual_sq + EPSILON) / (primal_sq + EPSILON)))
 
 
-def start_kernel(q_index, k_cols, primal, objective, lower, upper, bound_kind, out):
-    kind = bound_kind[...]
-    low = jnp.where((kind == 1) | (kind == 2), lower[...], -jnp.inf)
-    high = jnp.where((kind == 2) | (kind == 3), upper[...], jnp.inf)
-    for k, v in enumerate((primal[...], objective[...], low, high)):
-        out[pl.ds(k, NB, stride=5), :] = spread(v)
+def spread_two(v, w):
+    t = jnp.transpose(jnp.concatenate([v, w], axis=0))
+    low = lane() < 64
+    top, bottom = t[:NB], t[NB:]
+    return jnp.where(low, top, pltpu.roll(bottom, 64, 1)), jnp.where(low, pltpu.roll(top, 64, 1), bottom)
+
+
+def start_kernel(me, q_index, k_cols, k_rows, primal, objective, lower, upper, bound_kind, dual, rhs, row_kind, out, block, *scratch):
+    refs = (q_index, k_cols, k_rows, primal, objective, lower, upper, bound_kind, dual, rhs, row_kind)
+    sems = scratch[-1]
+    copies = [pltpu.make_async_copy(r, s, sems.at[i]) for i, (r, s) in enumerate(zip(refs, scratch))]
+    for c in copies:
+        c.start()
+    qi, kc, kr, p, ob, lo, up, bk, du, rh, rk = scratch[:-1]
+    for c in copies:
+        c.wait()
+    kind = bk[...]
+    low = jnp.where((kind == 1) | (kind == 2), lo[...], -jnp.inf)
+    high = jnp.where((kind == 2) | (kind == 3), up[...], jnp.inf)
+    a, b = spread_two(p[...], ob[...])
+    c, d = spread_two(low, high)
+    for k, v in enumerate((a, b, c, d)):
+        out[pl.ds(k, NB, stride=5), :] = v
     ln = lane(8)
     ids = jnp.zeros((8, LANES), F32)
     for j in range(NQ):
-        ids = jnp.where(ln == j, q_index[1, j].astype(F32), ids)
-        ids = jnp.where(ln == NT + j, q_index[0, j].astype(F32), ids)
+        ids = jnp.where(ln == j, qi[1, j].astype(F32), ids)
+        ids = jnp.where(ln == NT + j, qi[0, j].astype(F32), ids)
     for j in range(NK):
-        ids = jnp.where(ln == NQ + j, k_cols[0, j].astype(F32), ids)
+        ids = jnp.where(ln == NQ + j, kc[0, j].astype(F32), ids)
     out[pl.ds(4, NB, stride=5), :] = jnp.broadcast_to(ids[:1], (NB, LANES))
-
-
-def dual_start_kernel(k_rows, dual, rhs, row_kind, out):
-    out[0:NB] = spread(jnp.concatenate([dual[...], rhs[...]], axis=0))
+    a, b = spread_two(
+        jnp.concatenate([du[...], rh[...]], axis=0),
+        jnp.concatenate([rk[...].astype(F32), jnp.zeros((32, LANES), F32)], axis=0),
+    )
+    block[0:NB] = a
+    block[NB : 2 * NB] = b
     ids = jnp.zeros((8, LANES), F32)
-    ln = lane(8)
     for j in range(NK):
-        ids = jnp.where(slot_of(ln) == NQ + j, k_rows[0, j].astype(F32), ids)
-    kinds = spread(jnp.concatenate([row_kind[...].astype(F32), jnp.zeros((32, LANES), F32)], axis=0))
-    out[NB : 2 * NB] = kinds
-    out[2 * NB :] = ids
-
-
-def first_gather_kernel(got, msg):
+        ids = jnp.where(slot_of(ln) == NQ + j, kr[0, j].astype(F32), ids)
+    block[2 * NB :] = jnp.where(ln == 0, me[0].astype(F32), ids)
+
+
+def first_gather_kernel(got, p1, p2, p3, msg):
     ids = got[pl.ds(4, NB, stride=5), :].astype(I32)
     x = got[pl.ds(0, NB, stride=5), :]
     msg[...] = gather_tiles(ids, [x], [0] * NQ + [-1] * NK)
 
 
-def tables_kernel(got, rows_out, hot_out):
+def primal_tables(got, rows_out, hot_out):
     ids = got[pl.ds(4, NB, stride=5), :].astype(I32)
     ln = lane()
     rows = jnp.where(ln < NQ, pltpu.roll(ids, LANES - NT, 1), ids)
@@ -223,12 +238,11 @@
         hot_out[:, c * LANES : (c + 1) * LANES] = jnp.where(sub == row, 1.0, 0.0).astype(BF16)
 
 
-def dual_tables_kernel(me, p0, p1, p2, p3, y, rhs, kind, put, take):
-    parts = [p0, p1, p2, p3]
+def dual_tables(parts, y, rhs, kind, put, take):
     y[...] = join([p[0:NB] for p in parts], 0)
     rhs[...] = join([p[0:NB] for p in parts], 1)
     kind[...] = join([p[NB : 2 * NB] for p in parts], 0)
-    mine = me[0]
+    mine = jnp.broadcast_to(parts[0][2 * NB :, 0:1], (8, LANES)).astype(I32)
     rel = []
     for p in parts:
         r = p[2 * NB :].astype(I32)
@@ -256,15 +270,14 @@
     return dot(a, take) + dot(b, take)
 
 
-def transposed_kernel(y, take, tiles, out, rows):
+def first_products_kernel(msg, got, p0, p1, p2, p3, hess, cons, y, rhs, kind, put, take, rows_out, hot_out, out, rows):
+    primal_tables(got, rows_out, hot_out)
+    dual_tables([p0, p1, p2, p3], y, rhs, kind, put, take)
+    rows[...] = spread(msg[...])
+    first = forward_tiles(hess, rows, NQ, 0)
     rows[...] = jnp.zeros((NB, LANES), F32)
-    transposed_tiles(tiles, take_rows(y[...], take[...]), rows, NQ)
-    out[...] = spread(rows[...])
-
-
-def first_products_kernel(msg, trans, tiles, out, rows):
-    rows[...] = spread(msg[...])
-    out[...] = with_extra(forward_tiles(tiles, rows, NQ, 0) - trans[...], 0.0)
+    transposed_tiles(cons, take_rows(y[...], take[...]), rows, NQ)
+    out[...] = with_extra(first - spread(rows[...]), 0.0)
 
 
 def primal_step(msg, rows, hot, got, x, weight):
@@ -288,8 +301,8 @@
 def second_primal_kernel(msg, got, rows, hot, x_in, primal_sq, weight_out, out):
     x = x_in[...]
     m = msg[...]
-    weight = new_weight(jnp.ones((1, 1), F32), extra_of(m), primal_sq[...])
-    weight_out[...] = weight
+    weight = new_weight(jnp.ones((1, 1), F32), extra_of(m), primal_sq[0:1, 0:1])
+    weight_out[...] = jnp.broadcast_to(weight, (8, LANES))
     new, moved = primal_step(m, rows[...], hot[...], got, x, weight)
     ids = got[pl.ds(4, NB, stride=5), :].astype(I32)
     out[pl.ds(0, NB, stride=2), :] = with_extra(gather_tiles(ids, [2.0 * new - x], [-1] * NQ + [0] * NK), moved)
@@ -303,9 +316,8 @@
     out[...] = with_extra(forward_tiles(tiles, rows, NK, NQ), extra_of(m))
 
 
-def last_constraint_kernel(msg, tiles, out, final, rows):
+def last_constraint_kernel(msg, tiles, out, rows):
     m = msg[pl.ds(0, NB, stride=2), :]
-    final[...] = spread(msg[pl.ds(1, NB, stride=2), :])
     rows[...] = spread(m)
     out[...] = with_extra(forward_tiles(tiles, rows, NK, NQ), extra_of(m))
 
@@ -325,37 +337,40 @@
     parts = [p[...] for p in (p0, p1, p2, p3)]
     new, moved = dual_step(parts, put[...], y[...], rhs[...], kind[...], STEP_SCALE)
     y_out[...] = new
-    primal_sq[...] = primal_total(parts)
+    primal_sq[...] = jnp.broadcast_to(primal_total(parts), (8, LANES))
     rows[...] = jnp.zeros((NB, LANES), F32)
     transposed_tiles(tiles, take_rows(new, take[...]), rows, NQ)
     out[...] = with_extra(hess[...] - spread(rows[...]), moved)
 
 
-def last_dual_kernel(p0, p1, p2, p3, put, y, rhs, kind, weight, dual_out, primal_sq, out):
+def last_dual_kernel(p0, p1, p2, p3, put, y, rhs, kind, weight, y_out, primal_sq, out):
     parts = [p[...] for p in (p0, p1, p2, p3)]
-    new, moved = dual_step(parts, put[...], y[...], rhs[...], kind[...], STEP_SCALE * weight[...])
-    primal_sq[...] = primal_total(parts)
-    dual_out[...] = spread(new[:, :LANES])[:32]
+    new, moved = dual_step(parts, put[...], y[...], rhs[...], kind[...], STEP_SCALE * weight[0:1, 0:1])
+    primal_sq[...] = jnp.broadcast_to(primal_total(parts), (8, LANES))
+    y_out[...] = new[:, :LANES]
     out[...] = jnp.broadcast_to(moved, (NB, LANES))
 
 
-def last_kernel(msg, weight, primal_sq, out):
+def last_kernel(msg, y, want, weight, primal_sq, out, dual_out, final):
     dual_sq = jnp.sum(msg[:, 0:1], axis=0, keepdims=True)
-    out[...] = new_weight(weight[...], dual_sq, primal_sq[...])
-
-
-def call(kernel, outs, *args, smem=0, scratch=(), cost=0):
+    out[...] = new_weight(weight[0:1, 0:1], dual_sq, primal_sq[0:1, 0:1])
+    dual_out[...] = spread(y[...])[:32]
+    final[...] = spread(want[pl.ds(1, NB, stride=2), :])
+
+
+def call(kernel, outs, *args, smem=0, scratch=(), cost=COST, where=pltpu.VMEM, limit=VMEM_LIMIT):
     v = pl.BlockSpec(memory_space=pltpu.VMEM)
+    w = pl.BlockSpec(memory_space=where)
     s = pl.BlockSpec(memory_space=pltpu.SMEM)
     shapes = [jax.ShapeDtypeStruct(*o) for o in outs]
     res = pl.pallas_call(
         kernel,
         out_shape=shapes,
-        in_specs=[s] * smem + [v] * (len(args) - smem),
+        in_specs=[s] * smem + [w] * (len(args) - smem),
         out_specs=[v] * len(shapes),
         scratch_shapes=list(scratch),
-        compiler_params=pltpu.CompilerParams(vmem_limit_bytes=VMEM_LIMIT),
-        cost_estimate=pl.CostEstimate(flops=cost, bytes_accessed=cost, transcendentals=0) if cost else None,
+        compiler_params=pltpu.CompilerParams(vmem_limit_bytes=limit),
+        cost_estimate=pl.CostEstimate(flops=cost, bytes_accessed=10000000, transcendentals=0),
     )(*args)
     return res[0] if len(outs) == 1 else res
 
@@ -375,42 +390,42 @@
 
 
 def shards(primal, dual, objective, lower, upper, bound_kind, rhs, row_kind, q_tiles, q_index, k_tiles, k_rows, k_cols):
-    hess = q_tiles.reshape(NQ * TILE, TILE)
-    cons = k_tiles.reshape(NK * TILE, TILE)
+    hess, cons = q_tiles, k_tiles
     me = lax.axis_index(GRP).astype(I32).reshape(1)
 
     def wide(v):
         return v.reshape(-1, LANES)
 
-    first = call(start_kernel, [((5 * NB, LANES), F32)], q_index[0], k_cols, wide(primal), wide(objective), wide(lower),
-                 wide(upper), wide(bound_kind), smem=2)
-    block = call(dual_start_kernel, [((2 * NB + 8, LANES), F32)], k_rows, wide(dual), wide(rhs), wide(row_kind), smem=1)
+    inputs = (q_index[0], k_cols, k_rows, wide(primal), wide(objective), wide(lower), wide(upper), wide(bound_kind), wide(dual),
+              wide(rhs), wide(row_kind))
+    room = [(pltpu.SMEM if i < 3 else pltpu.VMEM)(v.shape, v.dtype) for i, v in enumerate(inputs)]
+    first, block = call(start_kernel, [((5 * NB, LANES), F32), ((2 * NB + 8, LANES), F32)], me, *inputs, smem=1, where=pltpu.HBM,
+                        scratch=room + [pltpu.SemaphoreType.DMA((len(inputs),))], limit=66800000)
     parts = over_group(block)
     got = exchange(first)
-    msg = call(first_gather_kernel, [ROWS], got)
-    want = exchange(msg)
-    rows, hot = call(tables_kernel, [((NB, LANES), I32), ((NB, NT * NB), BF16)], got, cost=10000000)
+    want = exchange(call(first_gather_kernel, [ROWS], got, *parts[1:]))
     wide_block = ((NB, 2 * LANES), F32)
-    y, b, kind, put, take = call(
-        dual_tables_kernel,
-        [wide_block, wide_block, wide_block, ((4 * LANES, 2 * LANES), BF16), ((2 * LANES, LANES), BF16)],
-        me, *parts, smem=1, cost=10000000)
-    trans = call(transposed_kernel, [ROWS], y, take, cons, scratch=ROWS_SCRATCH, cost=10000000)
-    grads = exchange(call(first_products_kernel, [ROWS], want, trans, hess, scratch=ROWS_SCRATCH))
+    scalar = ((8, LANES), F32)
+    y, b, kind, put, take, rows, hot, msg = call(
+        first_products_kernel,
+        [wide_block, wide_block, wide_block, ((4 * LANES, 2 * LANES), BF16), ((2 * LANES, LANES), BF16), ((NB, LANES), I32),
+         ((NB, NT * NB), BF16), ROWS],
+        want, got, *parts, hess, cons, scratch=ROWS_SCRATCH)
+    grads = exchange(msg)
     x, msg = call(first_primal_kernel, [ROWS, ROWS], grads, got, rows, hot)
     want = exchange(msg)
     prods, vec = call(constraint_kernel, [ROWS, ROWS], want, cons, scratch=ROWS_SCRATCH)
     parts = over_group(prods)
     hess_prod = call(hessian_kernel, [ROWS], vec, hess, cost=10000000)
-    y, primal_sq, msg = call(dual_kernel, [wide_block, ((1, 1), F32), ROWS], *parts, put, take, y, b, kind, hess_prod, cons,
+    y, primal_sq, msg = call(dual_kernel, [wide_block, scalar, ROWS], *parts, put, take, y, b, kind, hess_prod, cons,
                              scratch=ROWS_SCRATCH)
     grads = exchange(msg)
-    weight, both = call(second_primal_kernel, [((1, 1), F32), ((2 * NB, LANES), F32)], grads, got, rows, hot, x, primal_sq)
+    weight, both = call(second_primal_kernel, [scalar, ((2 * NB, LANES), F32)], grads, got, rows, hot, x, primal_sq)
     want = exchange(both)
-    prods, final = call(last_constraint_kernel, [ROWS, ROWS], want, cons, scratch=ROWS_SCRATCH)
+    prods = call(last_constraint_kernel, [ROWS], want, cons, scratch=ROWS_SCRATCH)
     parts = over_group(prods)
-    dual_out, primal_sq, msg = call(last_dual_kernel, [((32, LANES), F32), ((1, 1), F32), ROWS], *parts, put, y, b, kind, weight)
-    weight = call(last_kernel, [((1, 1), F32)], exchange(msg), weight, primal_sq)
+    y, primal_sq, msg = call(last_dual_kernel, [ROWS, scalar, ROWS], *parts, put, y, b, kind, weight)
+    weight, dual_out, final = call(last_kernel, [((1, 1), F32), ((32, LANES), F32), ROWS], exchange(msg), y, want, weight, primal_sq)
     return final.reshape(-1), dual_out.reshape(-1), weight.reshape(())
 
 

time: 154 us -> 139 us (0.903)
  blocking collectives: 52.8 us -> 85 us
  local copies, waits for them, and re-layouts: 17.9 us -> 0.01 us
  starting transfers between devices: 44.6 us -> 28.9 us
  waiting for transfers between devices: 20.3 us -> 11.9 us
  Pallas kernels: 16.9 us -> 11.6 us
    all_to_all x4 -> x6, blocking collectives: 52.8 us -> 85 us  [exchange(): out = lax.all_to_all(rows.reshape(NB, 1, k * LANES), BLK, 0, 0, tiled=True)]
    unnamed x34 -> x6, local copies, waits for them, and re-layouts: 17.9 us -> 0.01 us
    all_to_all x3 -> x1, waiting for transfers between devices: 16.2 us -> 0.01 us  [exchange(): out = lax.all_to_all(rows.reshape(NB, 1, k * LANES), BLK, 0, 0, tiled=True)]
    all_to_all x3 -> x1, starting transfers between devices: 28 us -> 13.5 us  [exchange(): out = lax.all_to_all(rows.reshape(NB, 1, k * LANES), BLK, 0, 0, tiled=True)]
    ppermute x9, waiting for transfers between devices: 4.1 us -> 11.9 us  [over_group(): lax.ppermute(rows, GRP, [(i, i ^ k) for i in range(4)])]
    pallas_call x15 -> x11, Pallas kernels: 16.9 us -> 11.6 us  [call(): pl.pallas_call(kernel, out_shape=shapes, in_specs=[s] * smem + [w] * (len...]
  transfers between devices with their start and end apart: 12 -> 10, of which waited for: 6 -> 5; matrix products, arithmetic and copies ran while one was open for 0% -> 0% of each run, Pallas kernels for 3% -> 0%
where the time goes in v1:
time: 139 us; the launch traced here: 138 us
  blocking collectives  85 us (61%)
  starting transfers between devices  28.9 us (21%)
  waiting for transfers between devices  11.9 us (9%)
  Pallas kernels  11.6 us (8%)
    all_to_all x6, blocking collectives, exchange(): out = lax.all_to_all(rows.reshape(NB, 1, k * LANES), BLK, 0, 0, tiled=True)  85 us
    ppermute x9, starting transfers between devices, over_group(): lax.ppermute(rows, GRP, [(i, i ^ k) for i in range(4)])  15.4 us
    all_to_all x1, starting transfers between devices, exchange(): out = lax.all_to_all(rows.reshape(NB, 1, k * LANES), BLK, 0, 0, tiled=True)  13.5 us
    ppermute x9, waiting for transfers between devices, over_group(): lax.ppermute(rows, GRP, [(i, i ^ k) for i in range(4)])  11.9 us
    pallas_call x11, Pallas kernels, call(): pl.pallas_call(kernel, out_shape=shapes, in_specs=[s] * smem + [w] * (len...  11.6 us
  transfers between devices with their start and end apart: 10, of which 5 were waited for; matrix products, arithmetic and copies ran while one was open for 0% of the time, Pallas kernels for 0%

profile of v1, /device:TPU:1, one launch (start us, length us, event | category | flops | bytes accessed | tf_op | source)
XLA Modules:
  0.0 138.2 jit_solution(9916079353132146779)
XLA Ops:
  0.6 1.8 %shard_map.148 = (f32[320,128]{1,0:T(8,128)}, f32[136,128]{1,0:T(8,128)}) custom-call(s32[1]{0:T(128)} %bitcast.me, s32[2,4]{1,0:T(2,128)} %bitcast.63, s32[1,6]{1,0:T(1,128)} %k_cols.1, s32[1,6]{1,0:T(1,128)} %k_rows.1, f32[64,128]{1,0:T(8,128)} %bitcast.55, f32[64,128]{1,0:T(8,128)} %bitcast.56, f32[64,128]{1,0:T(8,128)} %bitcast.57, f32[64,128]{1,0:T(8,128)} %bitcast.58, ...), custom_call_target="tpu_custom_call" | custom-call | flops 10000000000 | bytes 10000000 | tf_op jit(solution)/shard_map/pallas_call | solution.py:366
  2.5 13.5 %all-to-all-start = ((f32[64,1,640]{2,1,0:T(1,128)}), f32[64,1,640]{2,1,0:T(1,128)S(1)}, u32[]{:S(2)}, u32[]{:S(2)}) async-start(f32[64,1,640]{2,1,0:T(1,128)} %bitcast.54), calls=%async_computation | async-start | bytes 327680 | tf_op jit(solution)/shard_map/all_to_all | solution.py:384
  16.0 3.5 %collective-permute-start.2 = (f32[136,128]{1,0:T(8,128)}, f32[136,128]{1,0:T(8,128)S(1)}, u32[]{:S(2)}, u32[]{:S(2)}) collective-permute-start(f32[136,128]{1,0:T(8,128)} %get-tuple-element.29.p0), channel_id=1, source_target_pairs={{0,192},{64,128},{128,64},{192,0},{1,193},{65,129},{129,65},{193,1... | collective-permute-start | bytes 208904 | tf_op jit(solution)/shard_map/ppermute | solution.py:389
  19.5 0.3 collective-permute-start.1
  19.9 0.1 collective-permute-start
  20.0 3.0 %collective-permute-done.2.p3 = f32[136,128]{1,0:T(8,128)S(1)} collective-permute-done((f32[136,128]{1,0:T(8,128)}, f32[136,128]{1,0:T(8,128)S(1)}, u32[]{:S(2)}, u32[]{:S(2)}) %collective-permute-start.2) | collective-permute-done | bytes 69664 | tf_op jit(solution)/shard_map/ppermute | solution.py:389
  23.0 3.1 %collective-permute-done.1.p2 = f32[136,128]{1,0:T(8,128)S(1)} collective-permute-done((f32[136,128]{1,0:T(8,128)}, f32[136,128]{1,0:T(8,128)S(1)}, u32[]{:S(2)}, u32[]{:S(2)}) %collective-permute-start.1) | collective-permute-done | bytes 69664 | tf_op jit(solution)/shard_map/ppermute | solution.py:389
  26.1 0.0 all-to-all-done
  26.1 0.0 copy-start.1
  26.1 0.3 shard_map.149
  26.4 18.6 %all_to_all.35 = f32[64,1,128]{2,1,0:T(1,128)S(1)} all-to-all(f32[64,1,128]{2,1,0:T(1,128)S(1)} %bitcast.53), channel_id=1, replica_groups=mesh['grp_0'=2,'grp_1'=2,'blk_0'=8,'blk_1'=4,'blk_2'=2] {'blk_0','blk_1'..., dimensions={0} | all-to-all | bytes 65536 | tf_op jit(solution)/shard_map/all_to_all | solution.py:384
  45.0 2.2 %shard_map.150 = (f32[64,256]{1,0:T(8,128)S(1)}, f32[64,256]{1,0:T(8,128)S(1)}, f32[64,256]{1,0:T(8,128)S(1)}, bf16[512,256]{1,0:T(8,128)(2,1)S(1)}, bf16[256,12...) custom-call(f32[64,128]{1,0:T(8,128)S(1)} %bitcast.44, ...), custom_call_target="tpu_custom_call" | custom-call | flops 10000000000 | bytes 10000000 | tf_op jit(solution)/shard_map/pallas_call | solution.py:366
  47.2 13.1 %all_to_all.36 = f32[64,1,128]{2,1,0:T(1,128)S(1)} all-to-all(f32[64,1,128]{2,1,0:T(1,128)S(1)} %bitcast.45), channel_id=1, replica_groups=mesh['grp_0'=2,'grp_1'=2,'blk_0'=8,'blk_1'=4,'blk_2'=2] {'blk_0','blk_1'..., dimensions={0} | all-to-all | bytes 65536 | tf_op jit(solution)/shard_map/all_to_all | solution.py:384
  60.4 0.9 shard_map.151
  61.3 13.1 %all_to_all.37 = f32[64,1,128]{2,1,0:T(1,128)S(1)} all-to-all(f32[64,1,128]{2,1,0:T(1,128)S(1)} %bitcast.51), channel_id=1, replica_groups=mesh['grp_0'=2,'grp_1'=2,'blk_0'=8,'blk_1'=4,'blk_2'=2] {'blk_0','blk_1'..., dimensions={0} | all-to-all | bytes 65536 | tf_op jit(solution)/shard_map/all_to_all | solution.py:384
  74.4 1.1 shard_map.152
  75.5 6.0 %collective-permute-start.5 = (f32[64,128]{1,0:T(8,128)S(1)}, f32[64,128]{1,0:T(8,128)S(1)}, u32[]{:S(2)}, u32[]{:S(2)}) collective-permute-start(f32[64,128]{1,0:T(8,128)S(1)} %get-tuple-element.34.p0), channel_id=1, source_target_pairs={{0,192},{64,128},{128,64},{192,0},{1,193},{65,129},{129,65},{193,1... | collective-permute-start | bytes 98312 | tf_op jit(solution)/shard_map/ppermute | solution.py:389
  81.5 1.0 collective-permute-start.4
  82.5 0.6 shard_map.153.hess
  83.1 2.6 %collective-permute-done.4.p2 = f32[64,128]{1,0:T(8,128)S(1)} collective-permute-done((f32[64,128]{1,0:T(8,128)S(1)}, f32[64,128]{1,0:T(8,128)S(1)}, u32[]{:S(2)}, u32[]{:S(2)}) %collective-permute-start.4) | collective-permute-done | bytes 32800 | tf_op jit(solution)/shard_map/ppermute | solution.py:389
  85.7 1.6 %shard_map.154 = (f32[64,256]{1,0:T(8,128)S(1)}, f32[8,128]{1,0:T(8,128)S(1)}, f32[64,128]{1,0:T(8,128)S(1)}) custom-call(f32[64,128]{1,0:T(8,128)S(1)} %get-tuple-element.34.p0, f32[64,128]{1,0:T(8,128)S(1)} %collective-permute-done.3.p1, f32[64,128]{1,0:T(8,128)S(1)} %collective-permute-done.4.p2, f32[64,128]{1,0:T(8,128)S(1)} %collective-permute-done.5.p3, ...), custom_call_target="tpu_custom_call" | custom-call | flops 10000000000 | bytes 10000000 | tf_op jit(solution)/shard_map/pallas_call | solution.py:366
  87.3 13.3 %all_to_all.38 = f32[64,1,128]{2,1,0:T(1,128)S(1)} all-to-all(f32[64,1,128]{2,1,0:T(1,128)S(1)} %bitcast.47), channel_id=1, replica_groups=mesh['grp_0'=2,'grp_1'=2,'blk_0'=8,'blk_1'=4,'blk_2'=2] {'blk_0','blk_1'..., dimensions={0} | all-to-all | bytes 65536 | tf_op jit(solution)/shard_map/all_to_all | solution.py:384
  100.7 0.9 shard_map.155
  101.6 13.5 %all_to_all.39 = f32[64,1,256]{2,1,0:T(1,128)S(1)} all-to-all(f32[64,1,256]{2,1,0:T(1,128)S(1)} %bitcast.43), channel_id=1, replica_groups=mesh['grp_0'=2,'grp_1'=2,'blk_0'=8,'blk_1'=4,'blk_2'=2] {'blk_0','blk_1'..., dimensions={0} | all-to-all | bytes 131072 | tf_op jit(solution)/shard_map/all_to_all | solution.py:384
  115.0 1.1 shard_map.156.p0
  116.1 3.4 %collective-permute-start.8 = (f32[64,128]{1,0:T(8,128)S(1)}, f32[64,128]{1,0:T(8,128)S(1)}, u32[]{:S(2)}, u32[]{:S(2)}) collective-permute-start(f32[64,128]{1,0:T(8,128)S(1)} %shard_map.156.p0), channel_id=1, source_target_pairs={{0,192},{64,128},{128,64},{192,0},{1,193},{65,129},{129,65},{193,1... | collective-permute-start | bytes 98312 | tf_op jit(solution)/shard_map/ppermute | solution.py:389
  119.5 1.0 collective-permute-start.7
  120.5 0.6 collective-permute-done.8.p3
  121.1 2.7 %collective-permute-done.7.p2 = f32[64,128]{1,0:T(8,128)S(1)} collective-permute-done((f32[64,128]{1,0:T(8,128)S(1)}, f32[64,128]{1,0:T(8,128)S(1)}, u32[]{:S(2)}, u32[]{:S(2)}) %collective-permute-start.7) | collective-permute-done | bytes 32800 | tf_op jit(solution)/shard_map/ppermute | solution.py:389
  123.8 0.3 shard_map.157
  124.1 13.4 %all_to_all.40 = f32[64,1,128]{2,1,0:T(1,128)S(1)} all-to-all(f32[64,1,128]{2,1,0:T(1,128)S(1)} %bitcast.46), channel_id=1, replica_groups=mesh['grp_0'=2,'grp_1'=2,'blk_0'=8,'blk_1'=4,'blk_2'=2] {'blk_0','blk_1'..., dimensions={0} | all-to-all | bytes 65536 | tf_op jit(solution)/shard_map/all_to_all | solution.py:384
  137.5 0.8 shard_map.158
  (11 shorter events, 0.0 us)
Async XLA Ops:
  2.5 23.6 %all-to-all-start = ((f32[64,1,640]{2,1,0:T(1,128)}), f32[64,1,640]{2,1,0:T(1,128)S(1)}, u32[]{:S(2)}, u32[]{:S(2)}) async-start(f32[64,1,640]{2,1,0:T(1,128)} %bitcast.54), calls=%async_computation | async-start | bytes 327680 | tf_op jit(solution)/shard_map/all_to_all | solution.py:384
  16.0 7.0 %collective-permute-start.2 = (f32[136,128]{1,0:T(8,128)}, f32[136,128]{1,0:T(8,128)S(1)}, u32[]{:S(2)}, u32[]{:S(2)}) collective-permute-start(f32[136,128]{1,0:T(8,128)} %get-tuple-element.29.p0), channel_id=1, source_target_pairs={{0,192},{64,128},{128,64},{192,0},{1,193},{65,129},{129,65},{193,1... | collective-permute-start | bytes 208904 | tf_op jit(solution)/shard_map/ppermute | solution.py:389
  19.5 6.5 %collective-permute-start.1 = (f32[136,128]{1,0:T(8,128)}, f32[136,128]{1,0:T(8,128)S(1)}, u32[]{:S(2)}, u32[]{:S(2)}) collective-permute-start(f32[136,128]{1,0:T(8,128)} %get-tuple-element.29.p0), channel_id=1, source_target_pairs={{0,128},{64,192},{128,0},{192,64},{1,129},{65,193},{129,1},{193,65... | collective-permute-start | bytes 208904 | tf_op jit(solution)/shard_map/ppermute | solution.py:389
  19.9 6.2 %collective-permute-start = (f32[136,128]{1,0:T(8,128)}, f32[136,128]{1,0:T(8,128)S(1)}, u32[]{:S(2)}, u32[]{:S(2)}) collective-permute-start(f32[136,128]{1,0:T(8,128)} %get-tuple-element.29.p0), channel_id=1, source_target_pairs={{0,64},{64,0},{128,192},{192,128},{1,65},{65,1},{129,193},{193,129... | collective-permute-start | bytes 208904 | tf_op jit(solution)/shard_map/ppermute | solution.py:389
  26.1 18.9 %copy-start = (f32[1,4,512,512]{3,2,1,0:T(8,128)S(1)}, f32[1,4,512,512]{3,2,1,0:T(8,128)}, u32[]{:S(2)}) copy-start(f32[1,4,512,512]{3,2,1,0:T(8,128)} %tiles.5) | copy-start | bytes 12582916
  26.1 18.9 %copy-start.1 = (f32[1,6,512,512]{3,2,1,0:T(8,128)S(1)}, f32[1,6,512,512]{3,2,1,0:T(8,128)}, u32[]{:S(2)}) copy-start(f32[1,6,512,512]{3,2,1,0:T(8,128)} %tiles.7) | copy-start | bytes 18874372
  26.1 18.9 %copy-start.2 = (f32[136,128]{1,0:T(8,128)S(1)}, f32[136,128]{1,0:T(8,128)}, u32[]{:S(2)}) copy-start(f32[136,128]{1,0:T(8,128)} %get-tuple-element.29.p0) | copy-start | bytes 208900
  75.5 7.6 %collective-permute-start.5 = (f32[64,128]{1,0:T(8,128)S(1)}, f32[64,128]{1,0:T(8,128)S(1)}, u32[]{:S(2)}, u32[]{:S(2)}) collective-permute-start(f32[64,128]{1,0:T(8,128)S(1)} %get-tuple-element.34.p0), channel_id=1, source_target_pairs={{0,192},{64,128},{128,64},{192,0},{1,193},{65,129},{129,65},{193,1... | collective-permute-start | bytes 98312 | tf_op jit(solution)/shard_map/ppermute | solution.py:389
  81.5 4.3 %collective-permute-start.4 = (f32[64,128]{1,0:T(8,128)S(1)}, f32[64,128]{1,0:T(8,128)S(1)}, u32[]{:S(2)}, u32[]{:S(2)}) collective-permute-start(f32[64,128]{1,0:T(8,128)S(1)} %get-tuple-element.34.p0), channel_id=1, source_target_pairs={{0,128},{64,192},{128,0},{192,64},{1,129},{65,193},{129,1},{193,65... | collective-permute-start | bytes 98312 | tf_op jit(solution)/shard_map/ppermute | solution.py:389
  82.5 3.2 %collective-permute-start.3 = (f32[64,128]{1,0:T(8,128)S(1)}, f32[64,128]{1,0:T(8,128)S(1)}, u32[]{:S(2)}, u32[]{:S(2)}) collective-permute-start(f32[64,128]{1,0:T(8,128)S(1)} %get-tuple-element.34.p0), channel_id=1, source_target_pairs={{0,64},{64,0},{128,192},{192,128},{1,65},{65,1},{129,193},{193,129... | collective-permute-start | bytes 98312 | tf_op jit(solution)/shard_map/ppermute | solution.py:389
  116.1 5.0 %collective-permute-start.8 = (f32[64,128]{1,0:T(8,128)S(1)}, f32[64,128]{1,0:T(8,128)S(1)}, u32[]{:S(2)}, u32[]{:S(2)}) collective-permute-start(f32[64,128]{1,0:T(8,128)S(1)} %shard_map.156.p0), channel_id=1, source_target_pairs={{0,192},{64,128},{128,64},{192,0},{1,193},{65,129},{129,65},{193,1... | collective-permute-start | bytes 98312 | tf_op jit(solution)/shard_map/ppermute | solution.py:389
  119.5 4.3 %collective-permute-start.7 = (f32[64,128]{1,0:T(8,128)S(1)}, f32[64,128]{1,0:T(8,128)S(1)}, u32[]{:S(2)}, u32[]{:S(2)}) collective-permute-start(f32[64,128]{1,0:T(8,128)S(1)} %shard_map.156.p0), channel_id=1, source_target_pairs={{0,128},{64,192},{128,0},{192,64},{1,129},{65,193},{129,1},{193,65... | collective-permute-start | bytes 98312 | tf_op jit(solution)/shard_map/ppermute | solution.py:389
  120.5 3.3 %collective-permute-start.6 = (f32[64,128]{1,0:T(8,128)S(1)}, f32[64,128]{1,0:T(8,128)S(1)}, u32[]{:S(2)}, u32[]{:S(2)}) collective-permute-start(f32[64,128]{1,0:T(8,128)S(1)} %shard_map.156.p0), channel_id=1, source_target_pairs={{0,64},{64,0},{128,192},{192,128},{1,65},{65,1},{129,193},{193,129... | collective-permute-start | bytes 98312 | tf_op jit(solution)/shard_map/ppermute | solution.py:389

commit v2 on v1

--- a/solution.py
+++ b/solution.py
@@ -1,5 +1,3 @@
-import functools
-
 import jax
 import jax.numpy as jnp
 from jax import lax
@@ -16,7 +14,6 @@
 F32, BF16, I32 = jnp.float32, jnp.bfloat16, jnp.int32
 
 NB = 64
-TILE = 512
 LANES = 128
 NQ, NK = 4, 6
 NT = NQ + NK
@@ -218,7 +215,7 @@
     block[2 * NB :] = jnp.where(ln == 0, me[0].astype(F32), ids)
 
 
-def first_gather_kernel(got, p1, p2, p3, msg):
+def first_gather_kernel(got, msg):
     ids = got[pl.ds(4, NB, stride=5), :].astype(I32)
     x = got[pl.ds(0, NB, stride=5), :]
     msg[...] = gather_tiles(ids, [x], [0] * NQ + [-1] * NK)
@@ -386,10 +383,13 @@
 
 
 def over_group(rows):
-    return [rows] + [lax.ppermute(rows, GRP, [(i, i ^ k) for i in range(4)]) for k in (1, 2, 3)]
-
-
-def shards(primal, dual, objective, lower, upper, bound_kind, rhs, row_kind, q_tiles, q_index, k_tiles, k_rows, k_cols):
+    parts = [rows]
+    for k in (1, 2, 3):
+        parts.append(lax.ppermute(rows, GRP, [(i, i ^ k) for i in range(4)]))
+    return parts
+
+
+def steps(primal, dual, objective, lower, upper, bound_kind, rhs, row_kind, q_tiles, q_index, k_tiles, k_rows, k_cols):
     hess, cons = q_tiles, k_tiles
     me = lax.axis_index(GRP).astype(I32).reshape(1)
 
@@ -403,7 +403,8 @@
                         scratch=room + [pltpu.SemaphoreType.DMA((len(inputs),))], limit=66800000)
     parts = over_group(block)
     got = exchange(first)
-    want = exchange(call(first_gather_kernel, [ROWS], got, *parts[1:]))
+    msg = call(first_gather_kernel, [ROWS], got)
+    want = exchange(msg)
     wide_block = ((NB, 2 * LANES), F32)
     scalar = ((8, LANES), F32)
     y, b, kind, put, take, rows, hot, msg = call(
@@ -438,4 +439,4 @@
         P(GRP, BLK),
         P(GRP, BLK),
     )
-    return jax.shard_map(shards, mesh=finer, in_specs=placed, out_specs=(P(BLK_GRP), P(BLK_GRP), P()), check_vma=False)
+    return jax.shard_map(steps, mesh=finer, in_specs=placed, out_specs=(P(BLK_GRP), P(BLK_GRP), P()), check_vma=False)

time: 139 us -> 142 us (1.022)
  blocking collectives: 85 us -> 66.1 us
  waiting for transfers between devices: 11.9 us -> 22 us
  starting transfers between devices: 28.9 us -> 35.2 us
  local copies, waits for them, and re-layouts: 0.01 us -> 4.99 us
    all_to_all x6 -> x5, blocking collectives: 85 us -> 66.1 us  [exchange(): out = lax.all_to_all(rows.reshape(NB, 1, k * LANES), BLK, 0, 0, tiled=True)]
    all_to_all x1 -> x2, waiting for transfers between devices: 0.01 us -> 15.2 us  [exchange(): out = lax.all_to_all(rows.reshape(NB, 1, k * LANES), BLK, 0, 0, tiled=True)]
    ppermute x9, waiting for transfers between devices: 11.9 us -> 6.79 us  [over_group(): parts.append(lax.ppermute(rows, GRP, [(i, i ^ k) for i in range(4)]))]
    all_to_all x1 -> x2, starting transfers between devices: 13.5 us -> 18.6 us  [exchange(): out = lax.all_to_all(rows.reshape(NB, 1, k * LANES), BLK, 0, 0, tiled=True)]
    unnamed x6 -> x12, local copies, waits for them, and re-layouts: 0.01 us -> 4.99 us
  transfers between devices with their start and end apart: 10 -> 11, of which waited for: 5 -> 6; matrix products, arithmetic and copies ran while one was open for 0% -> 0% of each run, Pallas kernels for 0% -> 1%
where the time goes in v2:
time: 142 us; the launch traced here: 141 us
  blocking collectives  66.1 us (47%)
  starting transfers between devices  35.2 us (25%)
  waiting for transfers between devices  22 us (15%)
  Pallas kernels  12.2 us (9%)
  local copies, waits for them, and re-layouts  4.99 us (4%)
    all_to_all x5, blocking collectives, exchange(): out = lax.all_to_all(rows.reshape(NB, 1, k * LANES), BLK, 0, 0, tiled=True)  66.1 us
    all_to_all x2, starting transfers between devices, exchange(): out = lax.all_to_all(rows.reshape(NB, 1, k * LANES), BLK, 0, 0, tiled=True)  18.6 us
    ppermute x9, starting transfers between devices, over_group(): parts.append(lax.ppermute(rows, GRP, [(i, i ^ k) for i in range(4)]))  16.7 us
    all_to_all x2, waiting for transfers between devices, exchange(): out = lax.all_to_all(rows.reshape(NB, 1, k * LANES), BLK, 0, 0, tiled=True)  15.2 us
    pallas_call x11, Pallas kernels, call(): pl.pallas_call(kernel, out_shape=shapes, in_specs=[s] * smem + [w] * (len...  12.2 us
    ppermute x9, waiting for transfers between devices, over_group(): parts.append(lax.ppermute(rows, GRP, [(i, i ^ k) for i in range(4)]))  6.79 us
    unnamed x12, local copies, waits for them, and re-layouts  4.99 us
  transfers between devices with their start and end apart: 11, of which 6 were waited for; matrix products, arithmetic and copies ran while one was open for 0% of the time, Pallas kernels for 1%

profile of v2, /device:TPU:1, one launch (start us, length us, event | category | flops | bytes accessed | tf_op | source)
XLA Modules:
  0.0 141.3 jit_solution(18204683853507136778)
XLA Ops:
  0.6 1.8 %shard_map.148 = (f32[320,128]{1,0:T(8,128)}, f32[136,128]{1,0:T(8,128)}) custom-call(s32[1]{0:T(128)} %bitcast.me, s32[2,4]{1,0:T(2,128)} %bitcast.64, s32[1,6]{1,0:T(1,128)} %k_cols.1, s32[1,6]{1,0:T(1,128)} %k_rows.1, f32[64,128]{1,0:T(8,128)} %bitcast.56, f32[64,128]{1,0:T(8,128)} %bitcast.57, f32[64,128]{1,0:T(8,128)} %bitcast.58, f32[64,128]{1,0:T(8,128)} %bitcast.59, ...), custom_call_target="tpu_custom_call" | custom-call | flops 10000000000 | bytes 10000000 | tf_op jit(solution)/shard_map/pallas_call | solution.py:363
  2.5 13.5 %all-to-all-start = ((f32[64,1,640]{2,1,0:T(1,128)}), f32[64,1,640]{2,1,0:T(1,128)S(1)}, u32[]{:S(2)}, u32[]{:S(2)}) async-start(f32[64,1,640]{2,1,0:T(1,128)} %bitcast.55), calls=%async_computation | async-start | bytes 327680 | tf_op jit(solution)/shard_map/all_to_all | solution.py:381
  16.0 3.5 %collective-permute-start.2 = (f32[136,128]{1,0:T(8,128)}, f32[136,128]{1,0:T(8,128)S(1)}, u32[]{:S(2)}, u32[]{:S(2)}) collective-permute-start(f32[136,128]{1,0:T(8,128)} %get-tuple-element.29.p0), channel_id=1, source_target_pairs={{0,192},{64,128},{128,64},{192,0},{1,193},{65,129},{129,65},{193,1... | collective-permute-start | bytes 208904 | tf_op jit(solution)/shard_map/ppermute | solution.py:388
  19.5 0.3 collective-permute-start.1
  20.0 6.0 %all-to-all-done = f32[64,1,640]{2,1,0:T(1,128)S(1)} async-done(((f32[64,1,640]{2,1,0:T(1,128)}), f32[64,1,640]{2,1,0:T(1,128)S(1)}, u32[]{:S(2)}, u32[]{:S(2)}) %all-to-all-start) | async-done | bytes 163872 | tf_op jit(solution)/shard_map/all_to_all | solution.py:381
  26.0 1.0 shard_map.149
  27.0 5.1 %all-to-all-start.1 = ((f32[64,1,128]{2,1,0:T(1,128)}), f32[64,1,128]{2,1,0:T(1,128)S(1)}, u32[]{:S(2)}, u32[]{:S(2)}) async-start(f32[64,1,128]{2,1,0:T(1,128)} %bitcast.13), calls=%async_computation.1 | async-start | bytes 65536 | tf_op jit(solution)/shard_map/all_to_all | solution.py:381
  32.1 9.2 %all-to-all-done.1 = f32[64,1,128]{2,1,0:T(1,128)S(1)} async-done(((f32[64,1,128]{2,1,0:T(1,128)}), f32[64,1,128]{2,1,0:T(1,128)S(1)}, u32[]{:S(2)}, u32[]{:S(2)}) %all-to-all-start.1) | async-done | bytes 32800 | tf_op jit(solution)/shard_map/all_to_all | solution.py:381
  41.3 2.2 %copy-done = f32[1,4,512,512]{3,2,1,0:T(8,128)S(1)} copy-done((f32[1,4,512,512]{3,2,1,0:T(8,128)S(1)}, f32[1,4,512,512]{3,2,1,0:T(8,128)}, u32[]{:S(2)}) %copy-start) | copy-done | bytes 4194328
  43.5 2.8 %copy-done.2 = f32[1,6,512,512]{3,2,1,0:T(8,128)S(1)} copy-done((f32[1,6,512,512]{3,2,1,0:T(8,128)S(1)}, f32[1,6,512,512]{3,2,1,0:T(8,128)}, u32[]{:S(2)}) %copy-start.2) | copy-done | bytes 6291480
  46.3 2.2 %shard_map.150 = (f32[64,256]{1,0:T(8,128)S(1)}, f32[64,256]{1,0:T(8,128)S(1)}, f32[64,256]{1,0:T(8,128)S(1)}, bf16[512,256]{1,0:T(8,128)(2,1)S(1)}, bf16[256,12...) custom-call(f32[64,128]{1,0:T(8,128)S(1)} %bitcast.44, ...), custom_call_target="tpu_custom_call" | custom-call | flops 10000000000 | bytes 10000000 | tf_op jit(solution)/shard_map/pallas_call | solution.py:363
  48.5 13.1 %all_to_all.35 = f32[64,1,128]{2,1,0:T(1,128)S(1)} all-to-all(f32[64,1,128]{2,1,0:T(1,128)S(1)} %bitcast.45), channel_id=1, replica_groups=mesh['grp_0'=2,'grp_1'=2,'blk_0'=8,'blk_1'=4,'blk_2'=2] {'blk_0','blk_1'..., dimensions={0} | all-to-all | bytes 65536 | tf_op jit(solution)/shard_map/all_to_all | solution.py:381
  61.6 0.9 shard_map.151
  62.5 13.3 %all_to_all.36 = f32[64,1,128]{2,1,0:T(1,128)S(1)} all-to-all(f32[64,1,128]{2,1,0:T(1,128)S(1)} %bitcast.51), channel_id=1, replica_groups=mesh['grp_0'=2,'grp_1'=2,'blk_0'=8,'blk_1'=4,'blk_2'=2] {'blk_0','blk_1'..., dimensions={0} | all-to-all | bytes 65536 | tf_op jit(solution)/shard_map/all_to_all | solution.py:381
  75.8 1.1 shard_map.152
  76.9 7.9 %collective-permute-start.5 = (f32[64,128]{1,0:T(8,128)S(1)}, f32[64,128]{1,0:T(8,128)S(1)}, u32[]{:S(2)}, u32[]{:S(2)}) collective-permute-start(f32[64,128]{1,0:T(8,128)S(1)} %get-tuple-element.34.p0), channel_id=1, source_target_pairs={{0,192},{64,128},{128,64},{192,0},{1,193},{65,129},{129,65},{193,1... | collective-permute-start | bytes 98312 | tf_op jit(solution)/shard_map/ppermute | solution.py:388
  84.8 0.4 collective-permute-start.4
  85.3 0.6 shard_map.153.hess
  85.9 1.1 collective-permute-done.5.p3
  86.9 2.1 %collective-permute-done.4.p2 = f32[64,128]{1,0:T(8,128)S(1)} collective-permute-done((f32[64,128]{1,0:T(8,128)S(1)}, f32[64,128]{1,0:T(8,128)S(1)}, u32[]{:S(2)}, u32[]{:S(2)}) %collective-permute-start.4) | collective-permute-done | bytes 32800 | tf_op jit(solution)/shard_map/ppermute | solution.py:388
  89.0 1.6 %shard_map.154 = (f32[64,256]{1,0:T(8,128)S(1)}, f32[8,128]{1,0:T(8,128)S(1)}, f32[64,128]{1,0:T(8,128)S(1)}) custom-call(f32[64,128]{1,0:T(8,128)S(1)} %get-tuple-element.34.p0, f32[64,128]{1,0:T(8,128)S(1)} %collective-permute-done.3.p1, f32[64,128]{1,0:T(8,128)S(1)} %collective-permute-done.4.p2, f32[64,128]{1,0:T(8,128)S(1)} %collective-permute-done.5.p3, ...), custom_call_target="tpu_custom_call" | custom-call | flops 10000000000 | bytes 10000000 | tf_op jit(solution)/shard_map/pallas_call | solution.py:363
  90.6 13.1 %all_to_all.37 = f32[64,1,128]{2,1,0:T(1,128)S(1)} all-to-all(f32[64,1,128]{2,1,0:T(1,128)S(1)} %bitcast.47), channel_id=1, replica_groups=mesh['grp_0'=2,'grp_1'=2,'blk_0'=8,'blk_1'=4,'blk_2'=2] {'blk_0','blk_1'..., dimensions={0} | all-to-all | bytes 65536 | tf_op jit(solution)/shard_map/all_to_all | solution.py:381
  103.8 0.9 shard_map.155
  104.7 13.4 %all_to_all.38 = f32[64,1,256]{2,1,0:T(1,128)S(1)} all-to-all(f32[64,1,256]{2,1,0:T(1,128)S(1)} %bitcast.43), channel_id=1, replica_groups=mesh['grp_0'=2,'grp_1'=2,'blk_0'=8,'blk_1'=4,'blk_2'=2] {'blk_0','blk_1'..., dimensions={0} | all-to-all | bytes 131072 | tf_op jit(solution)/shard_map/all_to_all | solution.py:381
  118.1 1.1 shard_map.156.p0
  119.2 3.6 %collective-permute-start.8 = (f32[64,128]{1,0:T(8,128)S(1)}, f32[64,128]{1,0:T(8,128)S(1)}, u32[]{:S(2)}, u32[]{:S(2)}) collective-permute-start(f32[64,128]{1,0:T(8,128)S(1)} %shard_map.156.p0), channel_id=1, source_target_pairs={{0,192},{64,128},{128,64},{192,0},{1,193},{65,129},{129,65},{193,1... | collective-permute-start | bytes 98312 | tf_op jit(solution)/shard_map/ppermute | solution.py:388
  122.8 0.7 collective-permute-start.7
  123.5 0.9 collective-permute-done.8.p3
  124.4 2.7 %collective-permute-done.7.p2 = f32[64,128]{1,0:T(8,128)S(1)} collective-permute-done((f32[64,128]{1,0:T(8,128)S(1)}, f32[64,128]{1,0:T(8,128)S(1)}, u32[]{:S(2)}, u32[]{:S(2)}) %collective-permute-start.7) | collective-permute-done | bytes 32800 | tf_op jit(solution)/shard_map/ppermute | solution.py:388
  127.1 0.3 shard_map.157
  127.4 13.1 %all_to_all.39 = f32[64,1,128]{2,1,0:T(1,128)S(1)} all-to-all(f32[64,1,128]{2,1,0:T(1,128)S(1)} %bitcast.46), channel_id=1, replica_groups=mesh['grp_0'=2,'grp_1'=2,'blk_0'=8,'blk_1'=4,'blk_2'=2] {'blk_0','blk_1'..., dimensions={0} | all-to-all | bytes 65536 | tf_op jit(solution)/shard_map/all_to_all | solution.py:381
  140.5 0.8 shard_map.158
  (19 shorter events, 0.3 us)
Async XLA Ops:
  2.5 23.5 %all-to-all-start = ((f32[64,1,640]{2,1,0:T(1,128)}), f32[64,1,640]{2,1,0:T(1,128)S(1)}, u32[]{:S(2)}, u32[]{:S(2)}) async-start(f32[64,1,640]{2,1,0:T(1,128)} %bitcast.55), calls=%async_computation | async-start | bytes 327680 | tf_op jit(solution)/shard_map/all_to_all | solution.py:381
  16.0 16.1 %collective-permute-start.2 = (f32[136,128]{1,0:T(8,128)}, f32[136,128]{1,0:T(8,128)S(1)}, u32[]{:S(2)}, u32[]{:S(2)}) collective-permute-start(f32[136,128]{1,0:T(8,128)} %get-tuple-element.29.p0), channel_id=1, source_target_pairs={{0,192},{64,128},{128,64},{192,0},{1,193},{65,129},{129,65},{193,1... | collective-permute-start | bytes 208904 | tf_op jit(solution)/shard_map/ppermute | solution.py:388
  19.5 12.5 %collective-permute-start.1 = (f32[136,128]{1,0:T(8,128)}, f32[136,128]{1,0:T(8,128)S(1)}, u32[]{:S(2)}, u32[]{:S(2)}) collective-permute-start(f32[136,128]{1,0:T(8,128)} %get-tuple-element.29.p0), channel_id=1, source_target_pairs={{0,128},{64,192},{128,0},{192,64},{1,129},{65,193},{129,1},{193,65... | collective-permute-start | bytes 208904 | tf_op jit(solution)/shard_map/ppermute | solution.py:388
  19.9 12.2 %collective-permute-start = (f32[136,128]{1,0:T(8,128)}, f32[136,128]{1,0:T(8,128)S(1)}, u32[]{:S(2)}, u32[]{:S(2)}) collective-permute-start(f32[136,128]{1,0:T(8,128)} %get-tuple-element.29.p0), channel_id=1, source_target_pairs={{0,64},{64,0},{128,192},{192,128},{1,65},{65,1},{129,193},{193,129... | collective-permute-start | bytes 208904 | tf_op jit(solution)/shard_map/ppermute | solution.py:388
  26.0 15.3 %copy-start.3 = (f32[136,128]{1,0:T(8,128)S(1)}, f32[136,128]{1,0:T(8,128)}, u32[]{:S(2)}) copy-start(f32[136,128]{1,0:T(8,128)} %get-tuple-element.29.p0) | copy-start | bytes 208900
  27.0 14.3 %all-to-all-start.1 = ((f32[64,1,128]{2,1,0:T(1,128)}), f32[64,1,128]{2,1,0:T(1,128)S(1)}, u32[]{:S(2)}, u32[]{:S(2)}) async-start(f32[64,1,128]{2,1,0:T(1,128)} %bitcast.13), calls=%async_computation.1 | async-start | bytes 65536 | tf_op jit(solution)/shard_map/all_to_all | solution.py:381
  41.3 2.2 %copy-start = (f32[1,4,512,512]{3,2,1,0:T(8,128)S(1)}, f32[1,4,512,512]{3,2,1,0:T(8,128)}, u32[]{:S(2)}) copy-start(f32[1,4,512,512]{3,2,1,0:T(8,128)} %tiles.5) | copy-start | bytes 12582916
  43.5 2.8 %copy-start.2 = (f32[1,6,512,512]{3,2,1,0:T(8,128)S(1)}, f32[1,6,512,512]{3,2,1,0:T(8,128)}, u32[]{:S(2)}) copy-start(f32[1,6,512,512]{3,2,1,0:T(8,128)} %tiles.7) | copy-start | bytes 18874372
  46.3 29.5 %slice-start = ((s8[6291456]{0:T(1024)(128)(4,1)}), s8[2097152]{0:T(1024)(128)(4,1)S(1)}, s32[]{:S(2)}) async-start(s8[6291456]{0:T(1024)(128)(4,1)} %bitcast.53), calls=%async_computation.7 | async-start | bytes 4194304
  61.6 14.2 %slice-start.1 = ((s8[6291456]{0:T(1024)(128)(4,1)}), s8[4194304]{0:T(1024)(128)(4,1)S(1)}, s32[]{:S(2)}) async-start(s8[6291456]{0:T(1024)(128)(4,1)} %bitcast.53), calls=%async_computation.8 | async-start | bytes 8388608
  75.8 9.5 %copy-start.1 = (f32[1,4,512,512]{3,2,1,0:T(8,128)S(1)}, f32[1,4,512,512]{3,2,1,0:T(8,128)}, u32[]{:S(2)}) copy-start(f32[1,4,512,512]{3,2,1,0:T(8,128)} %tiles.5) | copy-start | bytes 12582916
  76.9 10.0 %collective-permute-start.5 = (f32[64,128]{1,0:T(8,128)S(1)}, f32[64,128]{1,0:T(8,128)S(1)}, u32[]{:S(2)}, u32[]{:S(2)}) collective-permute-start(f32[64,128]{1,0:T(8,128)S(1)} %get-tuple-element.34.p0), channel_id=1, source_target_pairs={{0,192},{64,128},{128,64},{192,0},{1,193},{65,129},{129,65},{193,1... | collective-permute-start | bytes 98312 | tf_op jit(solution)/shard_map/ppermute | solution.py:388
  84.8 4.3 %collective-permute-start.4 = (f32[64,128]{1,0:T(8,128)S(1)}, f32[64,128]{1,0:T(8,128)S(1)}, u32[]{:S(2)}, u32[]{:S(2)}) collective-permute-start(f32[64,128]{1,0:T(8,128)S(1)} %get-tuple-element.34.p0), channel_id=1, source_target_pairs={{0,128},{64,192},{128,0},{192,64},{1,129},{65,193},{129,1},{193,65... | collective-permute-start | bytes 98312 | tf_op jit(solution)/shard_map/ppermute | solution.py:388
  85.1 3.9 %collective-permute-start.3 = (f32[64,128]{1,0:T(8,128)S(1)}, f32[64,128]{1,0:T(8,128)S(1)}, u32[]{:S(2)}, u32[]{:S(2)}) collective-permute-start(f32[64,128]{1,0:T(8,128)S(1)} %get-tuple-element.34.p0), channel_id=1, source_target_pairs={{0,64},{64,0},{128,192},{192,128},{1,65},{65,1},{129,193},{193,129... | collective-permute-start | bytes 98312 | tf_op jit(solution)/shard_map/ppermute | solution.py:388
  119.2 5.2 %collective-permute-start.8 = (f32[64,128]{1,0:T(8,128)S(1)}, f32[64,128]{1,0:T(8,128)S(1)}, u32[]{:S(2)}, u32[]{:S(2)}) collective-permute-start(f32[64,128]{1,0:T(8,128)S(1)} %shard_map.156.p0), channel_id=1, source_target_pairs={{0,192},{64,128},{128,64},{192,0},{1,193},{65,129},{129,65},{193,1... | collective-permute-start | bytes 98312 | tf_op jit(solution)/shard_map/ppermute | solution.py:388
  122.8 4.3 %collective-permute-start.7 = (f32[64,128]{1,0:T(8,128)S(1)}, f32[64,128]{1,0:T(8,128)S(1)}, u32[]{:S(2)}, u32[]{:S(2)}) collective-permute-start(f32[64,128]{1,0:T(8,128)S(1)} %shard_map.156.p0), channel_id=1, source_target_pairs={{0,128},{64,192},{128,0},{192,64},{1,129},{65,193},{129,1},{193,65... | collective-permute-start | bytes 98312 | tf_op jit(solution)/shard_map/ppermute | solution.py:388
  123.5 3.6 %collective-permute-start.6 = (f32[64,128]{1,0:T(8,128)S(1)}, f32[64,128]{1,0:T(8,128)S(1)}, u32[]{:S(2)}, u32[]{:S(2)}) collective-permute-start(f32[64,128]{1,0:T(8,128)S(1)} %shard_map.156.p0), channel_id=1, source_target_pairs={{0,64},{64,0},{128,192},{192,128},{1,65},{65,1},{129,193},{193,129... | collective-permute-start | bytes 98312 | tf_op jit(solution)/shard_map/ppermute | solution.py:388

commit v3 on v2

--- a/solution.py
+++ b/solution.py
@@ -109,38 +109,33 @@
 
 def forward_tiles(tiles_ref, rows_ref, count, first):
     ln = lane()
-
-    def one(t, out):
+    out = jnp.zeros((NB, LANES), F32)
+    for t in range(count):
         j = first + t
-        vec = [rows_ref[pl.ds(4 * j + q, 1), :] for q in range(4)]
+        vec = [rows_ref[4 * j + q : 4 * j + q + 1, :] for q in range(4)]
         for qo in range(4):
             for h in range(2):
-                at = pl.ds(qo * 128 + h * 64, 64)
+                at = slice(qo * 128 + h * 64, qo * 128 + h * 64 + 64)
                 p = tiles_ref[0, t, at, 0:128] * vec[0]
                 for q in range(1, 4):
                     p = p + tiles_ref[0, t, at, q * 128 : (q + 1) * 128] * vec[q]
-                s = jnp.sum(p, axis=1, keepdims=True)
-                out = jnp.where(ln == h * 64 + 4 * j + qo, s, out)
-        return out
-
-    return lax.fori_loop(0, count, one, jnp.zeros((NB, LANES), F32))
+                out = jnp.where(ln == h * 64 + 4 * j + qo, jnp.sum(p, axis=1, keepdims=True), out)
+    return out
 
 
 def transposed_tiles(tiles_ref, cols, rows_ref, first):
-    def one(t, cols):
+    for t in range(NK):
+        j = first + t
         acc = [jnp.zeros((8, LANES), F32) for _ in range(4)]
         for qo in range(4):
             for h in range(2):
-                at = pl.ds(qo * 128 + h * 64, 64)
-                v = column(cols, h * 64 + qo)
+                at = slice(qo * 128 + h * 64, qo * 128 + h * 64 + 64)
+                v = along(cols, jnp.full((NB, LANES), h * 64 + 4 * j + qo, I32))
                 for q in range(4):
                     p = tiles_ref[0, t, at, q * 128 : (q + 1) * 128] * v
                     acc[q] = acc[q] + jnp.sum(p.reshape(8, 8, LANES), axis=0)
         for q in range(4):
-            rows_ref[pl.ds(4 * (first + t) + q, 1), :] = jnp.sum(acc[q], axis=0, keepdims=True)
-        return pltpu.roll(cols, LANES - 4, 1)
-
-    lax.fori_loop(0, NK, one, pltpu.roll(cols, LANES - 4 * first, 1))
+            rows_ref[4 * j + q : 4 * j + q + 1, :] = jnp.sum(acc[q], axis=0, keepdims=True)
 
 
 def join(parts, part):
@@ -155,10 +150,20 @@
     return jnp.concatenate(blocks, axis=1)
 
 
+def pack(prods, extra):
+    ln = lane(32)
+    both = jnp.where((ln & 63) < 40, prods[:32], pltpu.roll(prods[32:], 24, 1))
+    return jnp.where(ln == 0, extra, both)
+
+
+def unpack(packed):
+    return jnp.concatenate([packed, pltpu.roll(packed, LANES - 24, 1)], axis=0)
+
+
 def dual_step(parts, hot, y, rhs, kind, step):
     high, low = [], []
     for p in parts:
-        a, b = split(p, 2)
+        a, b = split(unpack(p), 2)
         high.append(a)
         low.append(b)
     extrap = dot(jnp.concatenate(high, axis=1), hot) + dot(jnp.concatenate(low, axis=1), hot)
@@ -235,7 +240,7 @@
         hot_out[:, c * LANES : (c + 1) * LANES] = jnp.where(sub == row, 1.0, 0.0).astype(BF16)
 
 
-def dual_tables(parts, y, rhs, kind, put, take):
+def dual_tables(parts, y, rhs, kind, tiles, take):
     y[...] = join([p[0:NB] for p in parts], 0)
     rhs[...] = join([p[0:NB] for p in parts], 1)
     kind[...] = join([p[NB : 2 * NB] for p in parts], 0)
@@ -244,16 +249,9 @@
     for p in parts:
         r = p[2 * NB :].astype(I32)
         rel.append((((r >> 3) ^ mine) << 3) | (r & 7))
+    tiles[...] = jnp.concatenate(rel, axis=0)
     ln = lane(LANES)
     sub = iota((LANES, LANES), 0)
-    sub_ok = (slot_of(sub) >= NQ) & (slot_of(sub) < NT)
-    for p in range(4):
-        r = jnp.transpose(jnp.broadcast_to(rel[p][:1].astype(F32), (LANES, LANES))).astype(I32)
-        same = ((ln & 64) == (sub & 64)) & ((ln & 3) == (sub & 3)) & sub_ok
-        for kk in range(2):
-            tile = (2 * kk + ((ln >> 5) & 1)) * 8 + ((ln >> 2) & 7)
-            hit = same & (tile == r)
-            put[p * LANES : (p + 1) * LANES, kk * LANES : (kk + 1) * LANES] = jnp.where(hit, 1.0, 0.0).astype(BF16)
     r = jnp.broadcast_to(rel[0][:1], (LANES, LANES))
     lane_ok = (slot_of(ln) >= NQ) & (slot_of(ln) < NT)
     for kk in range(2):
@@ -262,14 +260,25 @@
         take[kk * LANES : (kk + 1) * LANES, :] = jnp.where(hit, 1.0, 0.0).astype(BF16)
 
 
+def put_table(tiles, put):
+    ln = lane(LANES)
+    sub = iota((LANES, LANES), 0)
+    same = ((ln & 64) == (sub & 64)) & ((ln & 3) == (sub & 3)) & (slot_of(sub) >= NQ) & (slot_of(sub) < NT)
+    for p in range(4):
+        r = jnp.transpose(jnp.broadcast_to(tiles[8 * p : 8 * p + 1].astype(F32), (LANES, LANES))).astype(I32)
+        for kk in range(2):
+            tile = (2 * kk + ((ln >> 5) & 1)) * 8 + ((ln >> 2) & 7)
+            put[p * LANES : (p + 1) * LANES, kk * LANES : (kk + 1) * LANES] = jnp.where(same & (tile == r), 1.0, 0.0).astype(BF16)
+
+
 def take_rows(y, take):
     a, b = split(y, 2)
     return dot(a, take) + dot(b, take)
 
 
-def first_products_kernel(msg, got, p0, p1, p2, p3, hess, cons, y, rhs, kind, put, take, rows_out, hot_out, out, rows):
+def first_products_kernel(msg, got, p0, p1, p2, p3, hess, cons, y, rhs, kind, tiles, take, rows_out, hot_out, out, rows):
     primal_tables(got, rows_out, hot_out)
-    dual_tables([p0, p1, p2, p3], y, rhs, kind, put, take)
+    dual_tables([p0, p1, p2, p3], y, rhs, kind, tiles, take)
     rows[...] = spread(msg[...])
     first = forward_tiles(hess, rows, NQ, 0)
     rows[...] = jnp.zeros((NB, LANES), F32)
@@ -310,23 +319,24 @@
     m = msg[...]
     rows[...] = spread(m)
     vec[...] = rows[...]
-    out[...] = with_extra(forward_tiles(tiles, rows, NK, NQ), extra_of(m))
+    out[...] = pack(forward_tiles(tiles, rows, NK, NQ), extra_of(m))
 
 
 def last_constraint_kernel(msg, tiles, out, rows):
     m = msg[pl.ds(0, NB, stride=2), :]
     rows[...] = spread(m)
-    out[...] = with_extra(forward_tiles(tiles, rows, NK, NQ), extra_of(m))
-
-
-def hessian_kernel(vec, tiles, out):
+    out[...] = pack(forward_tiles(tiles, rows, NK, NQ), extra_of(m))
+
+
+def hessian_kernel(vec, rel, tiles, out, put):
     out[...] = forward_tiles(tiles, vec, NQ, 0)
+    put_table(rel, put)
 
 
 def primal_total(parts):
-    s = parts[0][0:1, EXTRA : EXTRA + 1]
+    s = parts[0][0:1, 0:1]
     for p in parts[1:]:
-        s = s + p[0:1, EXTRA : EXTRA + 1]
+        s = s + p[0:1, 0:1]
     return s
 
 
@@ -373,6 +383,7 @@
 
 
 ROWS = ((NB, LANES), F32)
+PACKED = ((NB // 2, LANES), F32)
 ROWS_SCRATCH = (pltpu.VMEM((NB, LANES), F32),)
 
 
@@ -407,23 +418,23 @@
     want = exchange(msg)
     wide_block = ((NB, 2 * LANES), F32)
     scalar = ((8, LANES), F32)
-    y, b, kind, put, take, rows, hot, msg = call(
+    y, b, kind, rel, take, rows, hot, msg = call(
         first_products_kernel,
-        [wide_block, wide_block, wide_block, ((4 * LANES, 2 * LANES), BF16), ((2 * LANES, LANES), BF16), ((NB, LANES), I32),
+        [wide_block, wide_block, wide_block, ((32, LANES), I32), ((2 * LANES, LANES), BF16), ((NB, LANES), I32),
          ((NB, NT * NB), BF16), ROWS],
         want, got, *parts, hess, cons, scratch=ROWS_SCRATCH)
     grads = exchange(msg)
     x, msg = call(first_primal_kernel, [ROWS, ROWS], grads, got, rows, hot)
     want = exchange(msg)
-    prods, vec = call(constraint_kernel, [ROWS, ROWS], want, cons, scratch=ROWS_SCRATCH)
+    prods, vec = call(constraint_kernel, [PACKED, ROWS], want, cons, scratch=ROWS_SCRATCH)
     parts = over_group(prods)
-    hess_prod = call(hessian_kernel, [ROWS], vec, hess, cost=10000000)
+    hess_prod, put = call(hessian_kernel, [ROWS, ((4 * LANES, 2 * LANES), BF16)], vec, rel, hess)
     y, primal_sq, msg = call(dual_kernel, [wide_block, scalar, ROWS], *parts, put, take, y, b, kind, hess_prod, cons,
                              scratch=ROWS_SCRATCH)
     grads = exchange(msg)
     weight, both = call(second_primal_kernel, [scalar, ((2 * NB, LANES), F32)], grads, got, rows, hot, x, primal_sq)
     want = exchange(both)
-    prods = call(last_constraint_kernel, [ROWS], want, cons, scratch=ROWS_SCRATCH)
+    prods = call(last_constraint_kernel, [PACKED], want, cons, scratch=ROWS_SCRATCH)
     parts = over_group(prods)
     y, primal_sq, msg = call(last_dual_kernel, [ROWS, scalar, ROWS], *parts, put, y, b, kind, weight)
     weight, dual_out, final = call(last_kernel, [((1, 1), F32), ((32, LANES), F32), ROWS], exchange(msg), y, want, weight, primal_sq)

time: 142 us -> 140 us (0.986)
  Pallas kernels: 12.2 us -> 10.2 us
    pallas_call x11, Pallas kernels: 12.2 us -> 10.2 us  [call(): pl.pallas_call(kernel, out_shape=shapes, in_specs=[s] * smem + [w] * (len...]
where the time goes in v3:
time: 140 us; the launch traced here: 139 us
  blocking collectives  66.1 us (47%)
  starting transfers between devices  35.3 us (25%)
  waiting for transfers between devices  21.8 us (16%)
  Pallas kernels  10.2 us (7%)
  local copies, waits for them, and re-layouts  4.99 us (4%)
    all_to_all x5, blocking collectives, exchange(): out = lax.all_to_all(rows.reshape(NB, 1, k * LANES), BLK, 0, 0, tiled=True)  66.1 us
    all_to_all x2, starting transfers between devices, exchange(): out = lax.all_to_all(rows.reshape(NB, 1, k * LANES), BLK, 0, 0, tiled=True)  18.6 us
    ppermute x9, starting transfers between devices, over_group(): parts.append(lax.ppermute(rows, GRP, [(i, i ^ k) for i in range(4)]))  16.7 us
    all_to_all x2, waiting for transfers between devices, exchange(): out = lax.all_to_all(rows.reshape(NB, 1, k * LANES), BLK, 0, 0, tiled=True)  15.2 us
    pallas_call x11, Pallas kernels, call(): pl.pallas_call(kernel, out_shape=shapes, in_specs=[s] * smem + [w] * (len...  10.2 us
    ppermute x9, waiting for transfers between devices, over_group(): parts.append(lax.ppermute(rows, GRP, [(i, i ^ k) for i in range(4)]))  6.58 us
    unnamed x12, local copies, waits for them, and re-layouts  4.99 us
  transfers between devices with their start and end apart: 11, of which 6 were waited for; matrix products, arithmetic and copies ran while one was open for 0% of the time, Pallas kernels for 1%

profile of v3, /device:TPU:1, one launch (start us, length us, event | category | flops | bytes accessed | tf_op | source)
XLA Modules:
  0.0 139.1 jit_solution(15301700022166212387)
XLA Ops:
  0.6 1.8 %shard_map.148 = (f32[320,128]{1,0:T(8,128)}, f32[136,128]{1,0:T(8,128)}) custom-call(s32[1]{0:T(128)} %bitcast.me, s32[2,4]{1,0:T(2,128)} %bitcast.64, s32[1,6]{1,0:T(1,128)} %k_cols.1, s32[1,6]{1,0:T(1,128)} %k_rows.1, f32[64,128]{1,0:T(8,128)} %bitcast.56, f32[64,128]{1,0:T(8,128)} %bitcast.57, f32[64,128]{1,0:T(8,128)} %bitcast.58, f32[64,128]{1,0:T(8,128)} %bitcast.59, ...), custom_call_target="tpu_custom_call" | custom-call | flops 10000000000 | bytes 10000000 | tf_op jit(solution)/shard_map/pallas_call | solution.py:373
  2.5 13.5 %all-to-all-start = ((f32[64,1,640]{2,1,0:T(1,128)}), f32[64,1,640]{2,1,0:T(1,128)S(1)}, u32[]{:S(2)}, u32[]{:S(2)}) async-start(f32[64,1,640]{2,1,0:T(1,128)} %bitcast.55), calls=%async_computation | async-start | bytes 327680 | tf_op jit(solution)/shard_map/all_to_all | solution.py:392
  16.0 3.5 %collective-permute-start.2 = (f32[136,128]{1,0:T(8,128)}, f32[136,128]{1,0:T(8,128)S(1)}, u32[]{:S(2)}, u32[]{:S(2)}) collective-permute-start(f32[136,128]{1,0:T(8,128)} %get-tuple-element.31.p0), channel_id=1, source_target_pairs={{0,192},{64,128},{128,64},{192,0},{1,193},{65,129},{129,65},{193,1... | collective-permute-start | bytes 208904 | tf_op jit(solution)/shard_map/ppermute | solution.py:399
  19.5 0.3 collective-permute-start.1
  20.0 6.0 %all-to-all-done = f32[64,1,640]{2,1,0:T(1,128)S(1)} async-done(((f32[64,1,640]{2,1,0:T(1,128)}), f32[64,1,640]{2,1,0:T(1,128)S(1)}, u32[]{:S(2)}, u32[]{:S(2)}) %all-to-all-start) | async-done | bytes 163872 | tf_op jit(solution)/shard_map/all_to_all | solution.py:392
  26.0 1.0 shard_map.149
  26.9 5.1 %all-to-all-start.1 = ((f32[64,1,128]{2,1,0:T(1,128)}), f32[64,1,128]{2,1,0:T(1,128)S(1)}, u32[]{:S(2)}, u32[]{:S(2)}) async-start(f32[64,1,128]{2,1,0:T(1,128)} %bitcast.13), calls=%async_computation.1 | async-start | bytes 65536 | tf_op jit(solution)/shard_map/all_to_all | solution.py:392
  32.1 9.2 %all-to-all-done.1 = f32[64,1,128]{2,1,0:T(1,128)S(1)} async-done(((f32[64,1,128]{2,1,0:T(1,128)}), f32[64,1,128]{2,1,0:T(1,128)S(1)}, u32[]{:S(2)}, u32[]{:S(2)}) %all-to-all-start.1) | async-done | bytes 32800 | tf_op jit(solution)/shard_map/all_to_all | solution.py:392
  41.3 2.8 %copy-done = f32[1,6,512,512]{3,2,1,0:T(8,128)S(1)} copy-done((f32[1,6,512,512]{3,2,1,0:T(8,128)S(1)}, f32[1,6,512,512]{3,2,1,0:T(8,128)}, u32[]{:S(2)}) %copy-start) | copy-done | bytes 6291480
  44.1 2.2 %copy-done.1 = f32[1,4,512,512]{3,2,1,0:T(8,128)S(1)} copy-done((f32[1,4,512,512]{3,2,1,0:T(8,128)S(1)}, f32[1,4,512,512]{3,2,1,0:T(8,128)}, u32[]{:S(2)}) %copy-start.1) | copy-done | bytes 4194328
  46.3 1.4 shard_map.150
  47.6 13.1 %all_to_all.35 = f32[64,1,128]{2,1,0:T(1,128)S(1)} all-to-all(f32[64,1,128]{2,1,0:T(1,128)S(1)} %bitcast.45), channel_id=1, replica_groups=mesh['grp_0'=2,'grp_1'=2,'blk_0'=8,'blk_1'=4,'blk_2'=2] {'blk_0','blk_1'..., dimensions={0} | all-to-all | bytes 65536 | tf_op jit(solution)/shard_map/all_to_all | solution.py:392
  60.8 0.9 shard_map.151
  61.7 13.3 %all_to_all.36 = f32[64,1,128]{2,1,0:T(1,128)S(1)} all-to-all(f32[64,1,128]{2,1,0:T(1,128)S(1)} %bitcast.51), channel_id=1, replica_groups=mesh['grp_0'=2,'grp_1'=2,'blk_0'=8,'blk_1'=4,'blk_2'=2] {'blk_0','blk_1'..., dimensions={0} | all-to-all | bytes 65536 | tf_op jit(solution)/shard_map/all_to_all | solution.py:392
  75.0 0.7 shard_map.152
  75.6 7.9 %collective-permute-start.5 = (f32[32,128]{1,0:T(8,128)S(1)}, f32[32,128]{1,0:T(8,128)S(1)}, u32[]{:S(2)}, u32[]{:S(2)}) collective-permute-start(f32[32,128]{1,0:T(8,128)S(1)} %get-tuple-element.36.p0), channel_id=1, source_target_pairs={{0,192},{64,128},{128,64},{192,0},{1,193},{65,129},{129,65},{193,1... | collective-permute-start | bytes 49160 | tf_op jit(solution)/shard_map/ppermute | solution.py:399
  83.5 0.4 collective-permute-start.4
  84.0 0.5 shard_map.153
  84.5 0.9 collective-permute-done.5.p3
  85.4 2.3 %collective-permute-done.4.p2 = f32[32,128]{1,0:T(8,128)S(1)} collective-permute-done((f32[32,128]{1,0:T(8,128)S(1)}, f32[32,128]{1,0:T(8,128)S(1)}, u32[]{:S(2)}, u32[]{:S(2)}) %collective-permute-start.4) | collective-permute-done | bytes 16416 | tf_op jit(solution)/shard_map/ppermute | solution.py:399
  87.6 1.4 shard_map.154
  89.0 13.3 %all_to_all.37 = f32[64,1,128]{2,1,0:T(1,128)S(1)} all-to-all(f32[64,1,128]{2,1,0:T(1,128)S(1)} %bitcast.47), channel_id=1, replica_groups=mesh['grp_0'=2,'grp_1'=2,'blk_0'=8,'blk_1'=4,'blk_2'=2] {'blk_0','blk_1'..., dimensions={0} | all-to-all | bytes 65536 | tf_op jit(solution)/shard_map/all_to_all | solution.py:392
  102.3 0.9 shard_map.155
  103.2 13.3 %all_to_all.38 = f32[64,1,256]{2,1,0:T(1,128)S(1)} all-to-all(f32[64,1,256]{2,1,0:T(1,128)S(1)} %bitcast.43), channel_id=1, replica_groups=mesh['grp_0'=2,'grp_1'=2,'blk_0'=8,'blk_1'=4,'blk_2'=2] {'blk_0','blk_1'..., dimensions={0} | all-to-all | bytes 131072 | tf_op jit(solution)/shard_map/all_to_all | solution.py:392
  116.5 0.7 shard_map.156.p0
  117.1 3.7 %collective-permute-start.8 = (f32[32,128]{1,0:T(8,128)S(1)}, f32[32,128]{1,0:T(8,128)S(1)}, u32[]{:S(2)}, u32[]{:S(2)}) collective-permute-start(f32[32,128]{1,0:T(8,128)S(1)} %shard_map.156.p0), channel_id=1, source_target_pairs={{0,192},{64,128},{128,64},{192,0},{1,193},{65,129},{129,65},{193,1... | collective-permute-start | bytes 49160 | tf_op jit(solution)/shard_map/ppermute | solution.py:399
  120.8 0.6 collective-permute-start.7
  121.4 0.8 collective-permute-done.8.p3
  122.2 2.7 %collective-permute-done.7.p2 = f32[32,128]{1,0:T(8,128)S(1)} collective-permute-done((f32[32,128]{1,0:T(8,128)S(1)}, f32[32,128]{1,0:T(8,128)S(1)}, u32[]{:S(2)}, u32[]{:S(2)}) %collective-permute-start.7) | collective-permute-done | bytes 16416 | tf_op jit(solution)/shard_map/ppermute | solution.py:399
  124.9 0.3 shard_map.157
  125.2 13.1 %all_to_all.39 = f32[64,1,128]{2,1,0:T(1,128)S(1)} all-to-all(f32[64,1,128]{2,1,0:T(1,128)S(1)} %bitcast.46), channel_id=1, replica_groups=mesh['grp_0'=2,'grp_1'=2,'blk_0'=8,'blk_1'=4,'blk_2'=2] {'blk_0','blk_1'..., dimensions={0} | all-to-all | bytes 65536 | tf_op jit(solution)/shard_map/all_to_all | solution.py:392
  138.4 0.8 shard_map.158
  (19 shorter events, 0.3 us)
Async XLA Ops:
  2.5 23.5 %all-to-all-start = ((f32[64,1,640]{2,1,0:T(1,128)}), f32[64,1,640]{2,1,0:T(1,128)S(1)}, u32[]{:S(2)}, u32[]{:S(2)}) async-start(f32[64,1,640]{2,1,0:T(1,128)} %bitcast.55), calls=%async_computation | async-start | bytes 327680 | tf_op jit(solution)/shard_map/all_to_all | solution.py:392
  16.0 16.1 %collective-permute-start.2 = (f32[136,128]{1,0:T(8,128)}, f32[136,128]{1,0:T(8,128)S(1)}, u32[]{:S(2)}, u32[]{:S(2)}) collective-permute-start(f32[136,128]{1,0:T(8,128)} %get-tuple-element.31.p0), channel_id=1, source_target_pairs={{0,192},{64,128},{128,64},{192,0},{1,193},{65,129},{129,65},{193,1... | collective-permute-start | bytes 208904 | tf_op jit(solution)/shard_map/ppermute | solution.py:399
  19.5 12.5 %collective-permute-start.1 = (f32[136,128]{1,0:T(8,128)}, f32[136,128]{1,0:T(8,128)S(1)}, u32[]{:S(2)}, u32[]{:S(2)}) collective-permute-start(f32[136,128]{1,0:T(8,128)} %get-tuple-element.31.p0), channel_id=1, source_target_pairs={{0,128},{64,192},{128,0},{192,64},{1,129},{65,193},{129,1},{193,65... | collective-permute-start | bytes 208904 | tf_op jit(solution)/shard_map/ppermute | solution.py:399
  19.9 12.2 %collective-permute-start = (f32[136,128]{1,0:T(8,128)}, f32[136,128]{1,0:T(8,128)S(1)}, u32[]{:S(2)}, u32[]{:S(2)}) collective-permute-start(f32[136,128]{1,0:T(8,128)} %get-tuple-element.31.p0), channel_id=1, source_target_pairs={{0,64},{64,0},{128,192},{192,128},{1,65},{65,1},{129,193},{193,129... | collective-permute-start | bytes 208904 | tf_op jit(solution)/shard_map/ppermute | solution.py:399
  26.0 15.3 %copy-start.3 = (f32[136,128]{1,0:T(8,128)S(1)}, f32[136,128]{1,0:T(8,128)}, u32[]{:S(2)}) copy-start(f32[136,128]{1,0:T(8,128)} %get-tuple-element.31.p0) | copy-start | bytes 208900
  26.9 14.4 %all-to-all-start.1 = ((f32[64,1,128]{2,1,0:T(1,128)}), f32[64,1,128]{2,1,0:T(1,128)S(1)}, u32[]{:S(2)}, u32[]{:S(2)}) async-start(f32[64,1,128]{2,1,0:T(1,128)} %bitcast.13), calls=%async_computation.1 | async-start | bytes 65536 | tf_op jit(solution)/shard_map/all_to_all | solution.py:392
  41.3 2.8 %copy-start = (f32[1,6,512,512]{3,2,1,0:T(8,128)S(1)}, f32[1,6,512,512]{3,2,1,0:T(8,128)}, u32[]{:S(2)}) copy-start(f32[1,6,512,512]{3,2,1,0:T(8,128)} %tiles.7) | copy-start | bytes 18874372
  44.1 2.2 %copy-start.1 = (f32[1,4,512,512]{3,2,1,0:T(8,128)S(1)}, f32[1,4,512,512]{3,2,1,0:T(8,128)}, u32[]{:S(2)}) copy-start(f32[1,4,512,512]{3,2,1,0:T(8,128)} %tiles.5) | copy-start | bytes 12582916
  46.3 28.7 %slice-start = ((s8[6291456]{0:T(1024)(128)(4,1)}), s8[2097152]{0:T(1024)(128)(4,1)S(1)}, s32[]{:S(2)}) async-start(s8[6291456]{0:T(1024)(128)(4,1)} %bitcast.53), calls=%async_computation.7 | async-start | bytes 4194304
  60.8 14.2 %slice-start.1 = ((s8[6291456]{0:T(1024)(128)(4,1)}), s8[4194304]{0:T(1024)(128)(4,1)S(1)}, s32[]{:S(2)}) async-start(s8[6291456]{0:T(1024)(128)(4,1)} %bitcast.53), calls=%async_computation.8 | async-start | bytes 8388608
  75.0 9.1 %copy-start.2 = (f32[1,4,512,512]{3,2,1,0:T(8,128)S(1)}, f32[1,4,512,512]{3,2,1,0:T(8,128)}, u32[]{:S(2)}) copy-start(f32[1,4,512,512]{3,2,1,0:T(8,128)} %tiles.5) | copy-start | bytes 12582916
  75.6 9.7 %collective-permute-start.5 = (f32[32,128]{1,0:T(8,128)S(1)}, f32[32,128]{1,0:T(8,128)S(1)}, u32[]{:S(2)}, u32[]{:S(2)}) collective-permute-start(f32[32,128]{1,0:T(8,128)S(1)} %get-tuple-element.36.p0), channel_id=1, source_target_pairs={{0,192},{64,128},{128,64},{192,0},{1,193},{65,129},{129,65},{193,1... | collective-permute-start | bytes 49160 | tf_op jit(solution)/shard_map/ppermute | solution.py:399
  83.5 4.1 %collective-permute-start.4 = (f32[32,128]{1,0:T(8,128)S(1)}, f32[32,128]{1,0:T(8,128)S(1)}, u32[]{:S(2)}, u32[]{:S(2)}) collective-permute-start(f32[32,128]{1,0:T(8,128)S(1)} %get-tuple-element.36.p0), channel_id=1, source_target_pairs={{0,128},{64,192},{128,0},{192,64},{1,129},{65,193},{129,1},{193,65... | collective-permute-start | bytes 49160 | tf_op jit(solution)/shard_map/ppermute | solution.py:399
  83.9 3.7 %collective-permute-start.3 = (f32[32,128]{1,0:T(8,128)S(1)}, f32[32,128]{1,0:T(8,128)S(1)}, u32[]{:S(2)}, u32[]{:S(2)}) collective-permute-start(f32[32,128]{1,0:T(8,128)S(1)} %get-tuple-element.36.p0), channel_id=1, source_target_pairs={{0,64},{64,0},{128,192},{192,128},{1,65},{65,1},{129,193},{193,129... | collective-permute-start | bytes 49160 | tf_op jit(solution)/shard_map/ppermute | solution.py:399
  117.1 5.1 %collective-permute-start.8 = (f32[32,128]{1,0:T(8,128)S(1)}, f32[32,128]{1,0:T(8,128)S(1)}, u32[]{:S(2)}, u32[]{:S(2)}) collective-permute-start(f32[32,128]{1,0:T(8,128)S(1)} %shard_map.156.p0), channel_id=1, source_target_pairs={{0,192},{64,128},{128,64},{192,0},{1,193},{65,129},{129,65},{193,1... | collective-permute-start | bytes 49160 | tf_op jit(solution)/shard_map/ppermute | solution.py:399
  120.8 4.1 %collective-permute-start.7 = (f32[32,128]{1,0:T(8,128)S(1)}, f32[32,128]{1,0:T(8,128)S(1)}, u32[]{:S(2)}, u32[]{:S(2)}) collective-permute-start(f32[32,128]{1,0:T(8,128)S(1)} %shard_map.156.p0), channel_id=1, source_target_pairs={{0,128},{64,192},{128,0},{192,64},{1,129},{65,193},{129,1},{193,65... | collective-permute-start | bytes 49160 | tf_op jit(solution)/shard_map/ppermute | solution.py:399
  121.4 3.5 %collective-permute-start.6 = (f32[32,128]{1,0:T(8,128)S(1)}, f32[32,128]{1,0:T(8,128)S(1)}, u32[]{:S(2)}, u32[]{:S(2)}) collective-permute-start(f32[32,128]{1,0:T(8,128)S(1)} %shard_map.156.p0), channel_id=1, source_target_pairs={{0,64},{64,0},{128,192},{192,128},{1,65},{65,1},{129,193},{193,129... | collective-permute-start | bytes 49160 | tf_op jit(solution)/shard_map/ppermute | solution.py:399

commit v4 on v3

v4 whole, which is shorter than its diff:
```python
import jax
import jax.numpy as jnp
from jax import lax
from jax.experimental import pallas as pl
from jax.experimental.pallas import tpu as pltpu
from jax.sharding import Mesh
from jax.sharding import PartitionSpec as P

BLK = ("zh", "zl", "xh", "xl", "yl")
CUBE = ("zl", "xl", "yl")
GRP = ("grp_0", "grp_1")
BLK_GRP = (*BLK, *GRP)
EPSILON = 1e-06
STEP_SCALE = 0.5
F32, BF16, I32 = jnp.float32, jnp.bfloat16, jnp.int32

NB = 64
LANES = 128
NQ, NK = 4, 6
NT = NQ + NK
VMEM_LIMIT = 8 * 1024 * 1024
COST = 10000000000


def iota(shape, dim):
    return lax.broadcasted_iota(I32, shape, dim)


def lane(rows=NB):
    return iota((rows, LANES), 1)


def slot_of(lanes):
    return (lanes >> 2) & 15


def split(v, n):
    parts = []
    for _ in range(n - 1):
        p = v.astype(BF16)
        parts.append(p)
        v = v - p.astype(F32)
    parts.append(v.astype(BF16))
    return parts


def dot(a, b):
    return jnp.dot(a, b, preferred_element_type=F32)


def spread(v):
    return jnp.transpose(jnp.concatenate([v, pltpu.roll(v, 64, 1)], axis=0))[:NB]


def total(v):
    return jnp.sum(jnp.sum(v, axis=0, keepdims=True), axis=1, keepdims=True)


def along(v, idx):
    return jnp.take_along_axis(v, idx, axis=1)


def column(v, c):
    return jnp.broadcast_to(v[:, c : c + 1], v.shape)


def gather_tiles(ids, tables, out, k):
    ln = lane()
    t_of = along(ids & 15, slot_of(ln))
    idx = (ln & 64) + t_of * 4 + (ln & 3)
    owner = ids >> 4
    ones = []
    for j in range(NT):
        o = jnp.where((ln & 63) == column(owner, j), 1.0, 0.0).astype(BF16)
        ones.append(jnp.concatenate([o, o], axis=1))
    ones = jnp.concatenate(ones, axis=0)
    for n, table in enumerate(tables):
        a, b, c = split(table, 3)
        got = dot(ones, jnp.concatenate([a, b, c, jnp.zeros_like(a)], axis=0))
        msg = jnp.zeros((NB, LANES), F32)
        for j in range(NT):
            msg = jnp.where(slot_of(ln) == j, along(got[j * NB : (j + 1) * NB], idx), msg)
        out[pl.ds(n, NB, stride=k), :] = msg


def cube_of(b):
    return ((b >> 3) & 1) * 4 + ((b >> 1) & 1) * 2 + (b & 1)


def send_rows(rows_ref, out, k):
    low = lane(5) < 64
    for q in range(4):
        a = rows_ref[pl.ds(q, 5, stride=8), :]
        b = rows_ref[pl.ds(q + 4, 5, stride=8), :]
        halves = (jnp.where(low, a, pltpu.roll(b, 64, 1)), jnp.where(low, pltpu.roll(a, 64, 1), b))
        for peer in range(NB):
            if cube_of(peer) >> 1 == q:
                out[peer * k : peer * k + 5, :] = halves[cube_of(peer) & 1]


def match_table(got, hot):
    base = lax.axis_index("zh") * 16 + lax.axis_index("xh") * 4
    ids = got[pl.ds(5, NB, stride=6), :]
    flat = jnp.transpose(jnp.concatenate([ids, ids], axis=0))
    l8 = lane(8)
    sub = iota((8, LANES), 0)
    member = base + ((sub >> 2) & 1) * 8 + ((sub >> 1) & 1) * 2 + (sub & 1)
    want = jnp.zeros((8, LANES), F32)
    for p in range(8):
        b = base + (p >> 2) * 8 + ((p >> 1) & 1) * 2 + (p & 1)
        want = jnp.where(sub == p, jnp.broadcast_to(got[pl.ds(b * 6 + 5, 1), :], (8, LANES)), want)
    want = jnp.where(l8 < NT, want, (member * 16 + l8 - NT).astype(F32))
    l1 = lane(1)

    def slot_row(j):
        r = NT + j if j < NQ else j
        return flat[r : r + 1]

    for parity in range(2):
        for c in range(NT // 2):
            pair = []
            for u in (2 * c, 2 * c + 1):
                part, k = u // 5, u % 5
                pair.append(slot_row(2 * k + (part ^ parity)))
            row = jnp.where(l1 < 64, pair[0], pair[1])
            hits = []
            for kk in range(13):
                w = jnp.broadcast_to(want[:, 2 * kk + parity : 2 * kk + parity + 1], (8, LANES))
                hits.append(jnp.where(w == row, 1.0, 0.0))
            hot[parity * 104 : parity * 104 + 104, c * LANES : (c + 1) * LANES] = jnp.concatenate(hits, axis=0).astype(BF16)


def sum_rows(msg, hot, out, k):
    blocks = [msg[pl.ds(n, NB, stride=k), :] for n in range(5)]
    blocks += [pltpu.roll(v, 64, 1) for v in blocks]
    high, low = [], []
    for v in blocks:
        a, b = split(v, 2)
        high.append(a)
        low.append(b)
    got = dot(hot[...], jnp.concatenate(high, axis=0)) + dot(hot[...], jnp.concatenate(low, axis=0))
    left = lane(8) < 64
    for kk in range(13):
        out[pl.ds(kk, 8, stride=13), :] = jnp.where(left, got[8 * kk : 8 * kk + 8], got[104 + 8 * kk : 112 + 8 * kk])


def receive_rows(msg, rows):
    low = lane(13) < 64
    for q in range(4):
        a = msg[26 * q : 26 * q + 13, :]
        b = msg[26 * q + 13 : 26 * q + 26, :]
        rows[pl.ds(q, 13, stride=8), :] = jnp.where(low, a, pltpu.roll(b, 64, 1))
        rows[pl.ds(q + 4, 13, stride=8), :] = jnp.where(low, pltpu.roll(a, 64, 1), b)


def project(v, low, high, kind):
    v = jnp.where((kind == 1.0) | (kind == 2.0), jnp.maximum(v, low), v)
    return jnp.where((kind == 2.0) | (kind == 3.0), jnp.minimum(v, high), v)


def forward_tiles(tiles_ref, rows_ref, count, first):
    ln = lane()
    out = jnp.zeros((NB, LANES), F32)
    for t in range(count):
        j = first + t
        vec = [rows_ref[4 * j + q : 4 * j + q + 1, :] for q in range(4)]
        for qo in range(4):
            for h in range(2):
                at = slice(qo * 128 + h * 64, qo * 128 + h * 64 + 64)
                p = tiles_ref[0, t, at, 0:128] * vec[0]
                for q in range(1, 4):
                    p = p + tiles_ref[0, t, at, q * 128 : (q + 1) * 128] * vec[q]
                out = jnp.where(ln == h * 64 + 4 * j + qo, jnp.sum(p, axis=1, keepdims=True), out)
    return out


def transposed_tiles(tiles_ref, cols, rows_ref, first):
    for t in range(NK):
        j = first + t
        acc = [jnp.zeros((8, LANES), F32) for _ in range(4)]
        for qo in range(4):
            for h in range(2):
                at = slice(qo * 128 + h * 64, qo * 128 + h * 64 + 64)
                v = along(cols, jnp.full((NB, LANES), h * 64 + 4 * j + qo, I32))
                for q in range(4):
                    p = tiles_ref[0, t, at, q * 128 : (q + 1) * 128] * v
                    acc[q] = acc[q] + jnp.sum(p.reshape(8, 8, LANES), axis=0)
        for q in range(4):
            rows_ref[4 * j + q : 4 * j + q + 1, :] = jnp.sum(acc[q], axis=0, keepdims=True)


def join(parts, part):
    low = (lane() & 32) == 0
    blocks = []
    for k in (0, 2):
        a, b = parts[k], parts[k + 1]
        if part == 0:
            blocks.append(jnp.where(low, a, pltpu.roll(b, 32, 1)))
        else:
            blocks.append(jnp.where(low, pltpu.roll(a, LANES - 32, 1), b))
    return jnp.concatenate(blocks, axis=1)


def pack(prods, extra):
    ln = lane(32)
    both = jnp.where((ln & 63) < 40, prods[:32], pltpu.roll(prods[32:], 24, 1))
    return jnp.where(ln == 0, extra, both)


def unpack(packed):
    return jnp.concatenate([packed, pltpu.roll(packed, LANES - 24, 1)], axis=0)


def dual_step(parts, hot, y, rhs, kind, step):
    high, low = [], []
    for p in parts:
        a, b = split(unpack(p), 2)
        high.append(a)
        low.append(b)
    extrap = dot(jnp.concatenate(high, axis=1), hot) + dot(jnp.concatenate(low, axis=1), hot)
    new = y + step * (rhs - extrap)
    new = jnp.where(kind == 1.0, jnp.maximum(new, 0.0), new)
    moved = new - y
    return new, total(moved * moved)


def new_weight(weight, dual_sq, primal_sq):
    return jnp.sqrt(weight * jnp.sqrt((dual_sq + EPSILON) / (primal_sq + EPSILON)))


def spread_two(v, w):
    t = jnp.transpose(jnp.concatenate([v, w], axis=0))
    low = lane() < 64
    top, bottom = t[:NB], t[NB:]
    return jnp.where(low, top, pltpu.roll(bottom, 64, 1)), jnp.where(low, pltpu.roll(top, 64, 1), bottom)


def start_kernel(me, q_index, k_cols, k_rows, primal, objective, lower, upper, bound_kind, dual, rhs, row_kind, out, block, own, *scratch):
    refs = (q_index, k_cols, k_rows, primal, objective, lower, upper, bound_kind, dual, rhs, row_kind)
    sems = scratch[-1]
    copies = [pltpu.make_async_copy(r, s, sems.at[i]) for i, (r, s) in enumerate(zip(refs, scratch))]
    for c in copies:
        c.start()
    qi, kc, kr, p, ob, lo, up, bk, du, rh, rk = scratch[:-1]
    for c in copies:
        c.wait()
    kind = bk[...].astype(F32)
    a, b = spread_two(p[...], ob[...])
    c, d = spread_two(lo[...], up[...])
    for k, v in enumerate((a, b, c, d, spread(kind))):
        out[pl.ds(k, NB, stride=6), :] = v
    for k, v in enumerate((p[...], ob[...], lo[...], up[...], kind)):
        own[k * NB : (k + 1) * NB] = v
    ln = lane(8)
    ids = jnp.zeros((8, LANES), F32)
    for j in range(NQ):
        ids = jnp.where(ln == j, qi[1, j].astype(F32), ids)
        ids = jnp.where(ln == NT + j, qi[0, j].astype(F32), ids)
    for j in range(NK):
        ids = jnp.where(ln == NQ + j, kc[0, j].astype(F32), ids)
    out[pl.ds(5, NB, stride=6), :] = jnp.broadcast_to(ids[:1], (NB, LANES))
    a, b = spread_two(
        jnp.concatenate([du[...], rh[...]], axis=0),
        jnp.concatenate([rk[...].astype(F32), jnp.zeros((32, LANES), F32)], axis=0),
    )
    block[0:NB] = a
    block[NB : 2 * NB] = b
    ids = jnp.zeros((8, LANES), F32)
    for j in range(NK):
        ids = jnp.where(slot_of(ln) == NQ + j, kr[0, j].astype(F32), ids)
    block[2 * NB :] = jnp.where(ln == 0, me[0].astype(F32), ids)


def first_gather_kernel(got, msg):
    ids = got[pl.ds(5, NB, stride=6), :].astype(I32)
    gather_tiles(ids, [got[pl.ds(n, NB, stride=6), :] for n in range(5)], msg, 5)


def dual_tables(parts, y, rhs, kind, tiles, take):
    y[...] = join([p[0:NB] for p in parts], 0)
    rhs[...] = join([p[0:NB] for p in parts], 1)
    kind[...] = join([p[NB : 2 * NB] for p in parts], 0)
    mine = jnp.broadcast_to(parts[0][2 * NB :, 0:1], (8, LANES)).astype(I32)
    rel = []
    for p in parts:
        r = p[2 * NB :].astype(I32)
        rel.append((((r >> 3) ^ mine) << 3) | (r & 7))
    tiles[...] = jnp.concatenate(rel, axis=0)
    ln = lane(LANES)
    sub = iota((LANES, LANES), 0)
    r = jnp.broadcast_to(rel[0][:1], (LANES, LANES))
    lane_ok = (slot_of(ln) >= NQ) & (slot_of(ln) < NT)
    for kk in range(2):
        tile = (2 * kk + ((sub >> 5) & 1)) * 8 + ((sub >> 2) & 7)
        hit = ((ln & 64) == (sub & 64)) & ((ln & 3) == (sub & 3)) & lane_ok & (tile == r)
        take[kk * LANES : (kk + 1) * LANES, :] = jnp.where(hit, 1.0, 0.0).astype(BF16)


def put_table(tiles, put):
    ln = lane(LANES)
    sub = iota((LANES, LANES), 0)
    same = ((ln & 64) == (sub & 64)) & ((ln & 3) == (sub & 3)) & (slot_of(sub) >= NQ) & (slot_of(sub) < NT)
    for p in range(4):
        r = jnp.transpose(jnp.broadcast_to(tiles[8 * p : 8 * p + 1].astype(F32), (LANES, LANES))).astype(I32)
        for kk in range(2):
            tile = (2 * kk + ((ln >> 5) & 1)) * 8 + ((ln >> 2) & 7)
            put[p * LANES : (p + 1) * LANES, kk * LANES : (kk + 1) * LANES] = jnp.where(same & (tile == r), 1.0, 0.0).astype(BF16)


def take_rows(y, take):
    a, b = split(y, 2)
    return dot(a, take) + dot(b, take)


def first_products_kernel(msg, got, p0, p1, p2, p3, hess, cons, y, rhs, kind, tiles, take, hot, read, out, rows):
    match_table(got, hot)
    dual_tables([p0, p1, p2, p3], y, rhs, kind, tiles, take)
    m = [msg[pl.ds(n, NB, stride=5), :] for n in range(5)]
    v = (*spread_two(m[0], m[1]), *spread_two(m[2], m[3]), spread(m[4]))
    for n in range(5):
        read[n * NB : (n + 1) * NB] = v[n]
    first = spread(forward_tiles(hess, read, NQ, 0))
    transposed_tiles(cons, take_rows(y[...], take[...]), rows, NQ)
    rows[0 : 4 * NQ] = first[0 : 4 * NQ]
    rows[4 * NQ : 4 * NT] = -rows[4 * NQ : 4 * NT]
    send_rows(rows, out, 5)


def first_sum_kernel(msg, hot, out):
    sum_rows(msg, hot, out, 5)


def second_sum_kernel(msg, hot, weight, out):
    sum_rows(msg, hot, out, 6)
    tail = jnp.sum(msg[pl.ds(5, NB, stride=6), :], axis=0, keepdims=True)
    weight[...] = jnp.broadcast_to(new_weight(jnp.ones((1, 1), F32), tail[:, 1:2], tail[:, 0:1]), (8, LANES))


def primal_step(grads, own, read, weight, own_out, read_out, rows):
    receive_rows(grads, rows)
    tau = STEP_SCALE / weight

    def step(v, first, n):
        x, c, low, high, kind = (v[k * NB : k * NB + n] for k in range(5))
        return x, project(x - tau * (rows[first : first + n] + c), low, high, kind)

    x, new = step(own, 4 * NT, NB)
    own_out[...] = new
    moved = new - x
    old, fresh = step(read, 0, 4 * NT)
    read_out[0 : 4 * NT] = fresh
    rows[0 : 4 * NT] = 2.0 * fresh - old
    return total(moved * moved)


def first_primal_kernel(grads, own, read, tiles, own_out, read_out, out, rows):
    moved = primal_step(grads, own, read, jnp.ones((1, 1), F32), own_out, read_out, rows)
    out[...] = pack(forward_tiles(tiles, rows, NK, NQ), moved)


def second_primal_kernel(grads, own, own_x, read, read_x, weight, tiles, own_out, out, rows):
    receive_rows(grads, rows)
    tau = STEP_SCALE / weight[0:1, 0:1]

    def step(x, v, first, n):
        c, low, high, kind = (v[k * NB : k * NB + n] for k in range(1, 5))
        return project(x - tau * (rows[first : first + n] + c), low, high, kind)

    x = own_x[...]
    new = step(x, own, 4 * NT, NB)
    own_out[...] = new
    moved = new - x
    old = read_x[0 : 4 * NT]
    rows[0 : 4 * NT] = 2.0 * step(old, read, 0, 4 * NT) - old
    out[...] = pack(forward_tiles(tiles, rows, NK, NQ), total(moved * moved))


def hessian_kernel(vec, rel, tiles, out, put):
    out[...] = spread(forward_tiles(tiles, vec, NQ, 0))
    put_table(rel, put)


def primal_total(parts):
    s = parts[0][0:1, 0:1]
    for p in parts[1:]:
        s = s + p[0:1, 0:1]
    return s


def dual_kernel(p0, p1, p2, p3, put, take, y, rhs, kind, hess, tiles, y_out, out, rows):
    parts = [p[...] for p in (p0, p1, p2, p3)]
    new, moved = dual_step(parts, put[...], y[...], rhs[...], kind[...], STEP_SCALE)
    y_out[...] = new
    transposed_tiles(tiles, take_rows(new, take[...]), rows, NQ)
    rows[0 : 4 * NQ] = hess[0 : 4 * NQ]
    rows[4 * NQ : 4 * NT] = -rows[4 * NQ : 4 * NT]
    send_rows(rows, out, 6)
    out[pl.ds(5, NB, stride=6), :] = jnp.where(lane() == 0, primal_total(parts), moved)


def last_dual_kernel(p0, p1, p2, p3, put, y, rhs, kind, weight, y_out, out):
    parts = [p[...] for p in (p0, p1, p2, p3)]
    new, moved = dual_step(parts, put[...], y[...], rhs[...], kind[...], STEP_SCALE * weight[0:1, 0:1])
    y_out[...] = new[:, :LANES]
    out[...] = jnp.where(lane() == 0, primal_total(parts), moved)


def last_kernel(msg, y, x, weight, out, dual_out, final):
    tail = jnp.sum(msg[...], axis=0, keepdims=True)
    out[...] = new_weight(weight[0:1, 0:1], tail[:, 1:2], tail[:, 0:1])
    dual_out[...] = spread(y[...])[:32]
    final[...] = x[...]


def call(kernel, outs, *args, smem=0, scratch=(), cost=COST, where=pltpu.VMEM, limit=VMEM_LIMIT):
    v = pl.BlockSpec(memory_space=pltpu.VMEM)
    w = pl.BlockSpec(memory_space=where)
    s = pl.BlockSpec(memory_space=pltpu.SMEM)
    shapes = [jax.ShapeDtypeStruct(*o) for o in outs]
    res = pl.pallas_call(
        kernel,
        out_shape=shapes,
        in_specs=[s] * smem + [w] * (len(args) - smem),
        out_specs=[v] * len(shapes),
        scratch_shapes=list(scratch),
        compiler_params=pltpu.CompilerParams(vmem_limit_bytes=limit),
        cost_estimate=pl.CostEstimate(flops=cost, bytes_accessed=10000000, transcendentals=0),
    )(*args)
    return res[0] if len(outs) == 1 else res


ROWS = ((NB, LANES), F32)
PACKED = ((NB // 2, LANES), F32)
ROWS_SCRATCH = (pltpu.VMEM((NB, LANES), F32),)


def exchange(rows):
    k = rows.shape[0] // NB
    out = lax.all_to_all(rows.reshape(NB, 1, k * LANES), BLK, 0, 0, tiled=True)
    return out.reshape(NB * k, LANES)


def exchange_in_cube(rows):
    k = rows.shape[0] // 8
    return lax.all_to_all(rows.reshape(8, 1, k * LANES), CUBE, 0, 0, tiled=True).reshape(8 * k, LANES)


def over_group(rows):
    parts = [rows]
    for k in (1, 2, 3):
        parts.append(lax.ppermute(rows, GRP, [(i, i ^ k) for i in range(4)]))
    return parts


def steps(primal, dual, objective, lower, upper, bound_kind, rhs, row_kind, q_tiles, q_index, k_tiles, k_rows, k_cols):
    hess, cons = q_tiles, k_tiles
    me = lax.axis_index(GRP).astype(I32).reshape(1)

    def wide(v):
        return v.reshape(-1, LANES)

    inputs = (q_index[0], k_cols, k_rows, wide(primal), wide(objective), wide(lower), wide(upper), wide(bound_kind), wide(dual),
              wide(rhs), wide(row_kind))
    room = [(pltpu.SMEM if i < 3 else pltpu.VMEM)(v.shape, v.dtype) for i, v in enumerate(inputs)]
    five = ((5 * NB, LANES), F32)
    first, block, own = call(start_kernel, [((6 * NB, LANES), F32), ((2 * NB + 8, LANES), F32), five], me, *inputs, smem=1,
                             where=pltpu.HBM, scratch=room + [pltpu.SemaphoreType.DMA((len(inputs),))], limit=66800000)
    parts = over_group(block)
    got = exchange(first)
    msg = call(first_gather_kernel, [five], got)
    want = exchange(msg)
    wide_block = ((NB, 2 * LANES), F32)
    scalar = ((8, LANES), F32)
    cube = ((8 * 13, LANES), F32)
    grads = (pltpu.VMEM((104, LANES), F32),)
    y, b, kind, rel, take, hot, read, msg = call(
        first_products_kernel,
        [wide_block, wide_block, wide_block, ((32, LANES), I32), ((2 * LANES, LANES), BF16), ((208, NT * NB), BF16), five, five],
        want, got, *parts, hess, cons, scratch=ROWS_SCRATCH)
    msg = call(first_sum_kernel, [cube], exchange(msg), hot)
    own_x, read_x, prods = call(first_primal_kernel, [ROWS, ROWS, PACKED], exchange_in_cube(msg), own, read, cons, scratch=grads)
    parts = over_group(prods)
    hess_prod, put = call(hessian_kernel, [ROWS, ((4 * LANES, 2 * LANES), BF16)], read_x, rel, hess)
    y, msg = call(dual_kernel, [wide_block, ((6 * NB, LANES), F32)], *parts, put, take, y, b, kind, hess_prod, cons,
                  scratch=ROWS_SCRATCH)
    weight, msg = call(second_sum_kernel, [scalar, cube], exchange(msg), hot)
    final, prods = call(second_primal_kernel, [ROWS, PACKED], exchange_in_cube(msg), own, own_x, read, read_x, weight, cons,
                        scratch=grads)
    parts = over_group(prods)
    y, msg = call(last_dual_kernel, [ROWS, ROWS], *parts, put, y, b, kind, weight)
    weight, dual_out, final = call(last_kernel, [((1, 1), F32), ((32, LANES), F32), ROWS], exchange(msg), y, final, weight)
    return final.reshape(-1), dual_out.reshape(-1), weight.reshape(())


def solution(mesh):
    finer = Mesh(mesh.devices.reshape(2, 2, 4, 2, 2, 2, 2), (*GRP, *BLK))
    placed = (P(BLK_GRP),) * 8 + (
        P(GRP, BLK, None, None),
        P(GRP, None, BLK),
        P(GRP, BLK, None, None),
        P(GRP, BLK),
        P(GRP, BLK),
    )
    return jax.shard_map(steps, mesh=finer, in_specs=placed, out_specs=(P(BLK_GRP), P(BLK_GRP), P()), check_vma=False)
```

time: 140 us -> 138 us (0.986)
  blocking collectives: 66.1 us -> 88 us
  starting transfers between devices: 35.3 us -> 22.1 us
  waiting for transfers between devices: 21.8 us -> 10.8 us
    all_to_all x2 -> x1, waiting for transfers between devices: 15.2 us -> 0.13 us  [exchange(): out = lax.all_to_all(rows.reshape(NB, 1, k * LANES), BLK, 0, 0, tiled=True)]
    all_to_all x0 -> x2, blocking collectives: none -> 14.6 us  [exchange_in_cube(): lax.all_to_all(rows.reshape(8, 1, k * LANES), CUBE, 0, 0, tiled=True)]
    all_to_all x2 -> x1, starting transfers between devices: 18.6 us -> 5.74 us  [exchange(): out = lax.all_to_all(rows.reshape(NB, 1, k * LANES), BLK, 0, 0, tiled=True)]
    all_to_all x5 -> x4, blocking collectives: 66.1 us -> 73.4 us  [exchange(): out = lax.all_to_all(rows.reshape(NB, 1, k * LANES), BLK, 0, 0, tiled=True)]
    ppermute x9, waiting for transfers between devices: 6.58 us -> 10.7 us  [over_group(): parts.append(lax.ppermute(rows, GRP, [(i, i ^ k) for i in range(4)]))]
    unnamed x12 -> x14, local copies, waits for them, and re-layouts: 4.99 us -> 5 us
  transfers between devices with their start and end apart: 11 -> 10, of which waited for: 6 -> 6; matrix products, arithmetic and copies ran while one was open for 0% -> 0% of each run, Pallas kernels for 1% -> 0%
where the time goes in v4:
time: 138 us; the launch traced here: 137 us
  blocking collectives  88 us (64%)
  starting transfers between devices  22.1 us (16%)
  waiting for transfers between devices  10.8 us (8%)
  Pallas kernels  10.7 us (8%)
  local copies, waits for them, and re-layouts  5 us (4%)
    all_to_all x4, blocking collectives, exchange(): out = lax.all_to_all(rows.reshape(NB, 1, k * LANES), BLK, 0, 0, tiled=True)  73.4 us
    ppermute x9, starting transfers between devices, over_group(): parts.append(lax.ppermute(rows, GRP, [(i, i ^ k) for i in range(4)]))  16.4 us
    all_to_all x2, blocking collectives, exchange_in_cube(): lax.all_to_all(rows.reshape(8, 1, k * LANES), CUBE, 0, 0, tiled=True)  14.6 us
    pallas_call x11, Pallas kernels, call(): pl.pallas_call(kernel, out_shape=shapes, in_specs=[s] * smem + [w] * (len...  10.7 us
    ppermute x9, waiting for transfers between devices, over_group(): parts.append(lax.ppermute(rows, GRP, [(i, i ^ k) for i in range(4)]))  10.7 us
    all_to_all x1, starting transfers between devices, exchange(): out = lax.all_to_all(rows.reshape(NB, 1, k * LANES), BLK, 0, 0, tiled=True)  5.74 us
    unnamed x14, local copies, waits for them, and re-layouts  5 us
  transfers between devices with their start and end apart: 10, of which 6 were waited for; matrix products, arithmetic and copies ran while one was open for 0% of the time, Pallas kernels for 0%

profile of v4, /device:TPU:1, one launch (start us, length us, event | category | flops | bytes accessed | tf_op | source)
XLA Modules:
  0.0 137.3 jit_solution(9321538168276936151)
XLA Ops:
  0.6 2.1 %shard_map.148 = (f32[384,128]{1,0:T(8,128)}, f32[136,128]{1,0:T(8,128)}, f32[320,128]{1,0:T(8,128)}) custom-call(s32[1]{0:T(128)} %bitcast.me, s32[2,4]{1,0:T(2,128)} %bitcast.53, s32[1,6]{1,0:T(1,128)} %k_cols.1, s32[1,6]{1,0:T(1,128)} %k_rows.1, f32[64,128]{1,0:T(8,128)} %bitcast.45, f32[64,128]{1,0:T(8,128)} %bitcast.46, f32[64,128]{1,0:T(8,128)} %bitcast.47, ...), custom_call_target="tpu_custom_call" | custom-call | flops 10000000000 | bytes 10000000 | tf_op jit(solution)/shard_map/pallas_call | solution.py:420
  2.7 23.7 %all_to_all.35 = f32[64,1,768]{2,1,0:T(1,128)S(1)} all-to-all(f32[64,1,768]{2,1,0:T(1,128)} %bitcast.44), channel_id=1, replica_groups=mesh['grp_0'=2,'grp_1'=2,'zh'=4,'zl'=2,'xh'=2,'xl'=2,'yl'=2] {'zh','zl',..., dimensions={0} | all-to-all | bytes 393216 | tf_op jit(solution)/shard_map/all_to_all | solution.py:439
  26.4 2.0 %shard_map.149 = f32[320,128]{1,0:T(8,128)} custom-call(f32[384,128]{1,0:T(8,128)S(1)} %bitcast.29), custom_call_target="tpu_custom_call" | custom-call | flops 10000000000 | bytes 10000000 | tf_op jit(solution)/shard_map/pallas_call | solution.py:420
  28.4 5.7 %all-to-all-start.1 = ((f32[64,1,640]{2,1,0:T(1,128)}), f32[64,1,640]{2,1,0:T(1,128)S(1)}, u32[]{:S(2)}, u32[]{:S(2)}) async-start(f32[64,1,640]{2,1,0:T(1,128)} %bitcast.12), calls=%async_computation.1 | async-start | bytes 327680 | tf_op jit(solution)/shard_map/all_to_all | solution.py:439
  34.2 4.2 %collective-permute-start.2 = (f32[136,128]{1,0:T(8,128)S(1)}, f32[136,128]{1,0:T(8,128)S(1)}, u32[]{:S(2)}, u32[]{:S(2)}) collective-permute-start(f32[136,128]{1,0:T(8,128)S(1)} %copy-done.3), channel_id=1, source_target_pairs={{0,192},{64,128},{128,64},{192,0},{1,193},{65,129},{129,65},{193,1... | collective-permute-start | bytes 208904 | tf_op jit(solution)/shard_map/ppermute | solution.py:451
  38.4 0.3 collective-permute-start.1
  38.7 0.1 collective-permute-start
  38.8 2.7 %collective-permute-done.2.p3 = f32[136,128]{1,0:T(8,128)S(1)} collective-permute-done((f32[136,128]{1,0:T(8,128)S(1)}, f32[136,128]{1,0:T(8,128)S(1)}, u32[]{:S(2)}, u32[]{:S(2)}) %collective-permute-start.2) | collective-permute-done | bytes 69664 | tf_op jit(solution)/shard_map/ppermute | solution.py:451
  41.6 2.4 %collective-permute-done.1.p2 = f32[136,128]{1,0:T(8,128)S(1)} collective-permute-done((f32[136,128]{1,0:T(8,128)S(1)}, f32[136,128]{1,0:T(8,128)S(1)}, u32[]{:S(2)}, u32[]{:S(2)}) %collective-permute-start.1) | collective-permute-done | bytes 69664 | tf_op jit(solution)/shard_map/ppermute | solution.py:451
  44.1 2.8 %copy-done = f32[1,6,512,512]{3,2,1,0:T(8,128)S(1)} copy-done((f32[1,6,512,512]{3,2,1,0:T(8,128)S(1)}, f32[1,6,512,512]{3,2,1,0:T(8,128)}, u32[]{:S(2)}) %copy-start) | copy-done | bytes 6291480
  46.9 2.2 %copy-done.1 = f32[1,4,512,512]{3,2,1,0:T(8,128)S(1)} copy-done((f32[1,4,512,512]{3,2,1,0:T(8,128)S(1)}, f32[1,4,512,512]{3,2,1,0:T(8,128)}, u32[]{:S(2)}) %copy-start.1) | copy-done | bytes 4194328
  49.1 1.4 %shard_map.150 = (f32[64,256]{1,0:T(8,128)S(1)}, f32[64,256]{1,0:T(8,128)S(1)}, f32[64,256]{1,0:T(8,128)S(1)}, s32[32,128]{1,0:T(8,128)S(1)}, bf16[256,128]{1,0:...) custom-call(f32[320,128]{1,0:T(8,128)S(1)} %bitcast.33, ...), custom_call_target="tpu_custom_call" | custom-call | flops 10000000000 | bytes 10000000 | tf_op jit(solution)/shard_map/pallas_call | solution.py:420
  50.6 19.5 %all_to_all.36 = f32[64,1,640]{2,1,0:T(1,128)S(1)} all-to-all(f32[64,1,640]{2,1,0:T(1,128)S(1)} %bitcast.34), channel_id=1, replica_groups=mesh['grp_0'=2,'grp_1'=2,'zh'=4,'zl'=2,'xh'=2,'xl'=2,'yl'=2] {'zh','zl',..., dimensions={0} | all-to-all | bytes 327680 | tf_op jit(solution)/shard_map/all_to_all | solution.py:439
  70.1 0.4 shard_map.151
  70.5 7.0 %all_to_all.37 = f32[8,1,1664]{2,1,0:T(1,128)S(1)} all-to-all(f32[8,1,1664]{2,1,0:T(1,128)S(1)} %bitcast.39), channel_id=1, replica_groups=mesh['grp_0'=2,'grp_1'=2,'zh'=4,'zl'=2,'xh'=2,'xl'=2,'yl'=2] {'zl','xl',..., dimensions={0} | all-to-all | bytes 106496 | tf_op jit(solution)/shard_map/all_to_all | solution.py:445
  77.5 0.6 shard_map.152
  78.2 5.5 %collective-permute-start.5 = (f32[32,128]{1,0:T(8,128)S(1)}, f32[32,128]{1,0:T(8,128)S(1)}, u32[]{:S(2)}, u32[]{:S(2)}) collective-permute-start(f32[32,128]{1,0:T(8,128)S(1)} %get-tuple-element.36.p0), channel_id=1, source_target_pairs={{0,192},{64,128},{128,64},{192,0},{1,193},{65,129},{129,65},{193,1... | collective-permute-start | bytes 49160 | tf_op jit(solution)/shard_map/ppermute | solution.py:451
  83.6 1.0 collective-permute-start.4
  84.7 0.6 shard_map.153
  85.3 2.5 %collective-permute-done.4.p2 = f32[32,128]{1,0:T(8,128)S(1)} collective-permute-done((f32[32,128]{1,0:T(8,128)S(1)}, f32[32,128]{1,0:T(8,128)S(1)}, u32[]{:S(2)}, u32[]{:S(2)}) %collective-permute-start.4) | collective-permute-done | bytes 16416 | tf_op jit(solution)/shard_map/ppermute | solution.py:451
  87.7 1.5 %shard_map.154 = (f32[64,256]{1,0:T(8,128)S(1)}, f32[384,128]{1,0:T(8,128)S(1)}) custom-call(f32[32,128]{1,0:T(8,128)S(1)} %get-tuple-element.36.p0, f32[32,128]{1,0:T(8,128)S(1)} %collective-permute-done.3.p1, f32[32,128]{1,0:T(8,128)S(1)} %collective-permute-done.4.p2, f32[32,128]{1,0:T(8,128)S(1)} %collective-permute-done.5.p3, ...), custom_call_target="tpu_custom_call" | custom-call | flops 10000000000 | bytes 10000000 | tf_op jit(solution)/shard_map/pallas_call | solution.py:420
  89.3 15.9 %all_to_all.38 = f32[64,1,768]{2,1,0:T(1,128)S(1)} all-to-all(f32[64,1,768]{2,1,0:T(1,128)S(1)} %bitcast.31), channel_id=1, replica_groups=mesh['grp_0'=2,'grp_1'=2,'zh'=4,'zl'=2,'xh'=2,'xl'=2,'yl'=2] {'zh','zl',..., dimensions={0} | all-to-all | bytes 393216 | tf_op jit(solution)/shard_map/all_to_all | solution.py:439
  105.1 0.4 shard_map.155
  105.5 7.5 %all_to_all.39 = f32[8,1,1664]{2,1,0:T(1,128)S(1)} all-to-all(f32[8,1,1664]{2,1,0:T(1,128)S(1)} %bitcast.38), channel_id=1, replica_groups=mesh['grp_0'=2,'grp_1'=2,'zh'=4,'zl'=2,'xh'=2,'xl'=2,'yl'=2] {'zl','xl',..., dimensions={0} | all-to-all | bytes 106496 | tf_op jit(solution)/shard_map/all_to_all | solution.py:445
  113.1 0.6 shard_map.156
  113.7 4.1 %collective-permute-start.8 = (f32[32,128]{1,0:T(8,128)S(1)}, f32[32,128]{1,0:T(8,128)S(1)}, u32[]{:S(2)}, u32[]{:S(2)}) collective-permute-start(f32[32,128]{1,0:T(8,128)S(1)} %get-tuple-element.49.p0), channel_id=1, source_target_pairs={{0,192},{64,128},{128,64},{192,0},{1,193},{65,129},{129,65},{193,1... | collective-permute-start | bytes 49160 | tf_op jit(solution)/shard_map/ppermute | solution.py:451
  117.8 1.1 collective-permute-start.7
  118.9 0.3 collective-permute-done.8.p3
  119.2 2.7 %collective-permute-done.7.p2 = f32[32,128]{1,0:T(8,128)S(1)} collective-permute-done((f32[32,128]{1,0:T(8,128)S(1)}, f32[32,128]{1,0:T(8,128)S(1)}, u32[]{:S(2)}, u32[]{:S(2)}) %collective-permute-start.7) | collective-permute-done | bytes 16416 | tf_op jit(solution)/shard_map/ppermute | solution.py:451
  121.9 0.3 shard_map.157
  122.2 14.3 %all_to_all.40 = f32[64,1,128]{2,1,0:T(1,128)S(1)} all-to-all(f32[64,1,128]{2,1,0:T(1,128)S(1)} %bitcast.40), channel_id=1, replica_groups=mesh['grp_0'=2,'grp_1'=2,'zh'=4,'zl'=2,'xh'=2,'xl'=2,'yl'=2] {'zh','zl',..., dimensions={0} | all-to-all | bytes 65536 | tf_op jit(solution)/shard_map/all_to_all | solution.py:439
  136.6 0.8 shard_map.158
  (20 shorter events, 0.2 us)
Async XLA Ops:
  26.4 7.8 %copy-start.3 = (f32[136,128]{1,0:T(8,128)S(1)}, f32[136,128]{1,0:T(8,128)}, u32[]{:S(2)}) copy-start(f32[136,128]{1,0:T(8,128)} %get-tuple-element.31.p0) | copy-start | bytes 208900
  28.4 15.7 %all-to-all-start.1 = ((f32[64,1,640]{2,1,0:T(1,128)}), f32[64,1,640]{2,1,0:T(1,128)S(1)}, u32[]{:S(2)}, u32[]{:S(2)}) async-start(f32[64,1,640]{2,1,0:T(1,128)} %bitcast.12), calls=%async_computation.1 | async-start | bytes 327680 | tf_op jit(solution)/shard_map/all_to_all | solution.py:439
  34.2 7.4 %collective-permute-start.2 = (f32[136,128]{1,0:T(8,128)S(1)}, f32[136,128]{1,0:T(8,128)S(1)}, u32[]{:S(2)}, u32[]{:S(2)}) collective-permute-start(f32[136,128]{1,0:T(8,128)S(1)} %copy-done.3), channel_id=1, source_target_pairs={{0,192},{64,128},{128,64},{192,0},{1,193},{65,129},{129,65},{193,1... | collective-permute-start | bytes 208904 | tf_op jit(solution)/shard_map/ppermute | solution.py:451
  38.4 5.7 %collective-permute-start.1 = (f32[136,128]{1,0:T(8,128)S(1)}, f32[136,128]{1,0:T(8,128)S(1)}, u32[]{:S(2)}, u32[]{:S(2)}) collective-permute-start(f32[136,128]{1,0:T(8,128)S(1)} %copy-done.3), channel_id=1, source_target_pairs={{0,128},{64,192},{128,0},{192,64},{1,129},{65,193},{129,1},{193,65... | collective-permute-start | bytes 208904 | tf_op jit(solution)/shard_map/ppermute | solution.py:451
  38.7 5.3 %collective-permute-start = (f32[136,128]{1,0:T(8,128)S(1)}, f32[136,128]{1,0:T(8,128)S(1)}, u32[]{:S(2)}, u32[]{:S(2)}) collective-permute-start(f32[136,128]{1,0:T(8,128)S(1)} %copy-done.3), channel_id=1, source_target_pairs={{0,64},{64,0},{128,192},{192,128},{1,65},{65,1},{129,193},{193,129... | collective-permute-start | bytes 208904 | tf_op jit(solution)/shard_map/ppermute | solution.py:451
  44.1 2.8 %copy-start = (f32[1,6,512,512]{3,2,1,0:T(8,128)S(1)}, f32[1,6,512,512]{3,2,1,0:T(8,128)}, u32[]{:S(2)}) copy-start(f32[1,6,512,512]{3,2,1,0:T(8,128)} %tiles.7) | copy-start | bytes 18874372
  46.9 2.2 %copy-start.1 = (f32[1,4,512,512]{3,2,1,0:T(8,128)S(1)}, f32[1,4,512,512]{3,2,1,0:T(8,128)}, u32[]{:S(2)}) copy-start(f32[1,4,512,512]{3,2,1,0:T(8,128)} %tiles.5) | copy-start | bytes 12582916
  49.1 28.4 %slice-start = ((s8[6291456]{0:T(1024)(128)(4,1)}), s8[2097152]{0:T(1024)(128)(4,1)S(1)}, s32[]{:S(2)}) async-start(s8[6291456]{0:T(1024)(128)(4,1)} %bitcast.42), calls=%async_computation.7 | async-start | bytes 4194304
  50.5 27.0 %slice-start.1 = ((s8[6291456]{0:T(1024)(128)(4,1)}), s8[4194304]{0:T(1024)(128)(4,1)S(1)}, s32[]{:S(2)}) async-start(s8[6291456]{0:T(1024)(128)(4,1)} %bitcast.42), calls=%async_computation.8 | async-start | bytes 8388608
  70.1 7.4 %copy-start.4 = (f32[320,128]{1,0:T(8,128)S(1)}, f32[320,128]{1,0:T(8,128)}, u32[]{:S(2)}) copy-start(f32[320,128]{1,0:T(8,128)} %get-tuple-element.34.own) | copy-start | bytes 491524
  77.5 7.2 %copy-start.2 = (f32[1,4,512,512]{3,2,1,0:T(8,128)S(1)}, f32[1,4,512,512]{3,2,1,0:T(8,128)}, u32[]{:S(2)}) copy-start(f32[1,4,512,512]{3,2,1,0:T(8,128)} %tiles.5) | copy-start | bytes 12582916
  78.2 7.1 %collective-permute-start.5 = (f32[32,128]{1,0:T(8,128)S(1)}, f32[32,128]{1,0:T(8,128)S(1)}, u32[]{:S(2)}, u32[]{:S(2)}) collective-permute-start(f32[32,128]{1,0:T(8,128)S(1)} %get-tuple-element.36.p0), channel_id=1, source_target_pairs={{0,192},{64,128},{128,64},{192,0},{1,193},{65,129},{129,65},{193,1... | collective-permute-start | bytes 49160 | tf_op jit(solution)/shard_map/ppermute | solution.py:451
  83.6 4.1 %collective-permute-start.4 = (f32[32,128]{1,0:T(8,128)S(1)}, f32[32,128]{1,0:T(8,128)S(1)}, u32[]{:S(2)}, u32[]{:S(2)}) collective-permute-start(f32[32,128]{1,0:T(8,128)S(1)} %get-tuple-element.36.p0), channel_id=1, source_target_pairs={{0,128},{64,192},{128,0},{192,64},{1,129},{65,193},{129,1},{193,65... | collective-permute-start | bytes 49160 | tf_op jit(solution)/shard_map/ppermute | solution.py:451
  84.7 3.1 %collective-permute-start.3 = (f32[32,128]{1,0:T(8,128)S(1)}, f32[32,128]{1,0:T(8,128)S(1)}, u32[]{:S(2)}, u32[]{:S(2)}) collective-permute-start(f32[32,128]{1,0:T(8,128)S(1)} %get-tuple-element.36.p0), channel_id=1, source_target_pairs={{0,64},{64,0},{128,192},{192,128},{1,65},{65,1},{129,193},{193,129... | collective-permute-start | bytes 49160 | tf_op jit(solution)/shard_map/ppermute | solution.py:451
  113.7 5.5 %collective-permute-start.8 = (f32[32,128]{1,0:T(8,128)S(1)}, f32[32,128]{1,0:T(8,128)S(1)}, u32[]{:S(2)}, u32[]{:S(2)}) collective-permute-start(f32[32,128]{1,0:T(8,128)S(1)} %get-tuple-element.49.p0), channel_id=1, source_target_pairs={{0,192},{64,128},{128,64},{192,0},{1,193},{65,129},{129,65},{193,1... | collective-permute-start | bytes 49160 | tf_op jit(solution)/shard_map/ppermute | solution.py:451
  117.8 4.1 %collective-permute-start.7 = (f32[32,128]{1,0:T(8,128)S(1)}, f32[32,128]{1,0:T(8,128)S(1)}, u32[]{:S(2)}, u32[]{:S(2)}) collective-permute-start(f32[32,128]{1,0:T(8,128)S(1)} %get-tuple-element.49.p0), channel_id=1, source_target_pairs={{0,128},{64,192},{128,0},{192,64},{1,129},{65,193},{129,1},{193,65... | collective-permute-start | bytes 49160 | tf_op jit(solution)/shard_map/ppermute | solution.py:451
  118.9 3.0 %collective-permute-start.6 = (f32[32,128]{1,0:T(8,128)S(1)}, f32[32,128]{1,0:T(8,128)S(1)}, u32[]{:S(2)}, u32[]{:S(2)}) collective-permute-start(f32[32,128]{1,0:T(8,128)S(1)} %get-tuple-element.49.p0), channel_id=1, source_target_pairs={{0,64},{64,0},{128,192},{192,128},{1,65},{65,1},{129,193},{193,129... | collective-permute-start | bytes 49160 | tf_op jit(solution)/shard_map/ppermute | solution.py:451

commit v5 on v4

--- a/solution.py
+++ b/solution.py
@@ -20,6 +20,8 @@
 NT = NQ + NK
 VMEM_LIMIT = 8 * 1024 * 1024
 COST = 10000000000
+FIRST, IDS = 5, 4
+FREE = 1e38
 
 
 def iota(shape, dim):
@@ -64,7 +66,7 @@
     return jnp.broadcast_to(v[:, c : c + 1], v.shape)
 
 
-def gather_tiles(ids, tables, out, k):
+def gather_tiles(ids, tables, out, first, k):
     ln = lane()
     t_of = along(ids & 15, slot_of(ln))
     idx = (ln & 64) + t_of * 4 + (ln & 3)
@@ -80,82 +82,93 @@
         msg = jnp.zeros((NB, LANES), F32)
         for j in range(NT):
             msg = jnp.where(slot_of(ln) == j, along(got[j * NB : (j + 1) * NB], idx), msg)
-        out[pl.ds(n, NB, stride=k), :] = msg
+        out[pl.ds(first + n, NB, stride=k), :] = msg
 
 
 def cube_of(b):
     return ((b >> 3) & 1) * 4 + ((b >> 1) & 1) * 2 + (b & 1)
 
 
-def send_rows(rows_ref, out, k):
-    low = lane(5) < 64
+def send_rows(rows_ref, out, n, k):
+    low = lane(n) < 64
     for q in range(4):
-        a = rows_ref[pl.ds(q, 5, stride=8), :]
-        b = rows_ref[pl.ds(q + 4, 5, stride=8), :]
+        a = rows_ref[pl.ds(q, n, stride=8), :]
+        b = rows_ref[pl.ds(q + 4, n, stride=8), :]
         halves = (jnp.where(low, a, pltpu.roll(b, 64, 1)), jnp.where(low, pltpu.roll(a, 64, 1), b))
         for peer in range(NB):
             if cube_of(peer) >> 1 == q:
-                out[peer * k : peer * k + 5, :] = halves[cube_of(peer) & 1]
-
-
-def match_table(got, hot):
+                out[peer * k : peer * k + n, :] = halves[cube_of(peer) & 1]
+
+
+def wanted(got):
     base = lax.axis_index("zh") * 16 + lax.axis_index("xh") * 4
-    ids = got[pl.ds(5, NB, stride=6), :]
-    flat = jnp.transpose(jnp.concatenate([ids, ids], axis=0))
-    l8 = lane(8)
+    ln = lane(8)
     sub = iota((8, LANES), 0)
-    member = base + ((sub >> 2) & 1) * 8 + ((sub >> 1) & 1) * 2 + (sub & 1)
     want = jnp.zeros((8, LANES), F32)
     for p in range(8):
         b = base + (p >> 2) * 8 + ((p >> 1) & 1) * 2 + (p & 1)
-        want = jnp.where(sub == p, jnp.broadcast_to(got[pl.ds(b * 6 + 5, 1), :], (8, LANES)), want)
-    want = jnp.where(l8 < NT, want, (member * 16 + l8 - NT).astype(F32))
-    l1 = lane(1)
-
-    def slot_row(j):
+        want = jnp.where(sub == p, jnp.broadcast_to(got[pl.ds(b * FIRST + IDS, 1), :], (8, LANES)), want)
+    member = base + ((sub >> 2) & 1) * 8 + ((sub >> 1) & 1) * 2 + (sub & 1)
+    return jnp.where(ln < NT, want, (member * 16 + ln - NT).astype(F32))
+
+
+def matches(want, row_of, n, m):
+    low = lane(1) < 64
+    sides = []
+    for parity in range(2):
+        chunks = []
+        for c in range(n):
+            a, b = (row_of(u % n, (u // n) ^ parity) for u in (2 * c, 2 * c + 1))
+            row = jnp.where(low, a, b)
+            hits = []
+            for kk in range(m):
+                w = jnp.broadcast_to(want[:, 2 * kk + parity : 2 * kk + parity + 1], (8, LANES))
+                hits.append(jnp.where(w == row, 1.0, 0.0))
+            chunks.append(jnp.concatenate(hits, axis=0))
+        sides.append(jnp.concatenate(chunks, axis=1))
+    return jnp.concatenate(sides, axis=0).astype(BF16)
+
+
+def match_table(got):
+    ids = got[pl.ds(IDS, NB, stride=FIRST), :]
+    flat = jnp.transpose(jnp.concatenate([ids, ids], axis=0))
+
+    def row_of(pair, odd):
+        j = 2 * pair + odd
         r = NT + j if j < NQ else j
         return flat[r : r + 1]
 
-    for parity in range(2):
-        for c in range(NT // 2):
-            pair = []
-            for u in (2 * c, 2 * c + 1):
-                part, k = u // 5, u % 5
-                pair.append(slot_row(2 * k + (part ^ parity)))
-            row = jnp.where(l1 < 64, pair[0], pair[1])
-            hits = []
-            for kk in range(13):
-                w = jnp.broadcast_to(want[:, 2 * kk + parity : 2 * kk + parity + 1], (8, LANES))
-                hits.append(jnp.where(w == row, 1.0, 0.0))
-            hot[parity * 104 : parity * 104 + 104, c * LANES : (c + 1) * LANES] = jnp.concatenate(hits, axis=0).astype(BF16)
-
-
-def sum_rows(msg, hot, out, k):
-    blocks = [msg[pl.ds(n, NB, stride=k), :] for n in range(5)]
+    return matches(wanted(got), row_of, NT // 2, 13)
+
+
+def sum_rows(msg, hot, out, n, m, k):
+    blocks = [msg[pl.ds(i, NB, stride=k), :] for i in range(n)]
     blocks += [pltpu.roll(v, 64, 1) for v in blocks]
     high, low = [], []
     for v in blocks:
         a, b = split(v, 2)
         high.append(a)
         low.append(b)
-    got = dot(hot[...], jnp.concatenate(high, axis=0)) + dot(hot[...], jnp.concatenate(low, axis=0))
+    got = dot(hot, jnp.concatenate(high, axis=0)) + dot(hot, jnp.concatenate(low, axis=0))
     left = lane(8) < 64
-    for kk in range(13):
-        out[pl.ds(kk, 8, stride=13), :] = jnp.where(left, got[8 * kk : 8 * kk + 8], got[104 + 8 * kk : 112 + 8 * kk])
-
-
-def receive_rows(msg, rows):
-    low = lane(13) < 64
+    for kk in range(m):
+        out[pl.ds(kk, 8, stride=m), :] = jnp.where(left, got[8 * kk : 8 * kk + 8], got[8 * (m + kk) : 8 * (m + kk) + 8])
+
+
+def receive_rows(msg, rows, m):
+    low = lane(m) < 64
     for q in range(4):
-        a = msg[26 * q : 26 * q + 13, :]
-        b = msg[26 * q + 13 : 26 * q + 26, :]
-        rows[pl.ds(q, 13, stride=8), :] = jnp.where(low, a, pltpu.roll(b, 64, 1))
-        rows[pl.ds(q + 4, 13, stride=8), :] = jnp.where(low, pltpu.roll(a, 64, 1), b)
-
-
-def project(v, low, high, kind):
-    v = jnp.where((kind == 1.0) | (kind == 2.0), jnp.maximum(v, low), v)
-    return jnp.where((kind == 2.0) | (kind == 3.0), jnp.minimum(v, high), v)
+        a = msg[2 * m * q : 2 * m * q + m, :]
+        b = msg[2 * m * q + m : 2 * m * q + 2 * m, :]
+        rows[pl.ds(q, m, stride=8), :] = jnp.where(low, a, pltpu.roll(b, 64, 1))
+        rows[pl.ds(q + 4, m, stride=8), :] = jnp.where(low, pltpu.roll(a, 64, 1), b)
+
+
+def bounds(lower, upper, kind, free):
+    return (
+        jnp.where((kind == 1) | (kind == 2), lower, -free),
+        jnp.where((kind == 2) | (kind == 3), upper, free),
+    )
 
 
 def forward_tiles(tiles_ref, rows_ref, count, first):
@@ -235,7 +248,7 @@
     return jnp.where(low, top, pltpu.roll(bottom, 64, 1)), jnp.where(low, pltpu.roll(top, 64, 1), bottom)
 
 
-def start_kernel(me, q_index, k_cols, k_rows, primal, objective, lower, upper, bound_kind, dual, rhs, row_kind, out, block, own, *scratch):
+def start_kernel(me, q_index, k_cols, k_rows, primal, objective, lower, upper, bound_kind, dual, rhs, row_kind, out, block, *scratch):
     refs = (q_index, k_cols, k_rows, primal, objective, lower, upper, bound_kind, dual, rhs, row_kind)
     sems = scratch[-1]
     copies = [pltpu.make_async_copy(r, s, sems.at[i]) for i, (r, s) in enumerate(zip(refs, scratch))]
@@ -244,13 +257,9 @@
     qi, kc, kr, p, ob, lo, up, bk, du, rh, rk = scratch[:-1]
     for c in copies:
         c.wait()
-    kind = bk[...].astype(F32)
-    a, b = spread_two(p[...], ob[...])
-    c, d = spread_two(lo[...], up[...])
-    for k, v in enumerate((a, b, c, d, spread(kind))):
-        out[pl.ds(k, NB, stride=6), :] = v
-    for k, v in enumerate((p[...], ob[...], lo[...], up[...], kind)):
-        own[k * NB : (k + 1) * NB] = v
+    low, high = bounds(lo[...], up[...], bk[...], FREE)
+    for k, v in enumerate((*spread_two(p[...], ob[...]), *spread_two(low, high))):
+        out[pl.ds(k, NB, stride=FIRST), :] = v
     ln = lane(8)
     ids = jnp.zeros((8, LANES), F32)
     for j in range(NQ):
@@ -258,7 +267,7 @@
         ids = jnp.where(ln == NT + j, qi[0, j].astype(F32), ids)
     for j in range(NK):
         ids = jnp.where(ln == NQ + j, kc[0, j].astype(F32), ids)
-    out[pl.ds(5, NB, stride=6), :] = jnp.broadcast_to(ids[:1], (NB, LANES))
+    out[pl.ds(IDS, NB, stride=FIRST), :] = jnp.broadcast_to(ids[:1], (NB, LANES))
     a, b = spread_two(
         jnp.concatenate([du[...], rh[...]], axis=0),
         jnp.concatenate([rk[...].astype(F32), jnp.zeros((32, LANES), F32)], axis=0),
@@ -272,8 +281,8 @@
 
 
 def first_gather_kernel(got, msg):
-    ids = got[pl.ds(5, NB, stride=6), :].astype(I32)
-    gather_tiles(ids, [got[pl.ds(n, NB, stride=6), :] for n in range(5)], msg, 5)
+    ids = got[pl.ds(IDS, NB, stride=FIRST), :].astype(I32)
+    gather_tiles(ids, [got[pl.ds(n, NB, stride=FIRST), :] for n in range(4)], msg, 0, 4)
 
 
 def dual_tables(parts, y, rhs, kind, tiles, take):
@@ -313,66 +322,53 @@
 
 
 def first_products_kernel(msg, got, p0, p1, p2, p3, hess, cons, y, rhs, kind, tiles, take, hot, read, out, rows):
-    match_table(got, hot)
+    hot[...] = match_table(got)
     dual_tables([p0, p1, p2, p3], y, rhs, kind, tiles, take)
-    m = [msg[pl.ds(n, NB, stride=5), :] for n in range(5)]
-    v = (*spread_two(m[0], m[1]), *spread_two(m[2], m[3]), spread(m[4]))
-    for n in range(5):
-        read[n * NB : (n + 1) * NB] = v[n]
+    m = [msg[pl.ds(n, NB, stride=4), :] for n in range(4)]
+    for n, v in enumerate((*spread_two(m[0], m[1]), *spread_two(m[2], m[3]))):
+        read[n * NB : (n + 1) * NB] = v
     first = spread(forward_tiles(hess, read, NQ, 0))
     transposed_tiles(cons, take_rows(y[...], take[...]), rows, NQ)
     rows[0 : 4 * NQ] = first[0 : 4 * NQ]
     rows[4 * NQ : 4 * NT] = -rows[4 * NQ : 4 * NT]
-    send_rows(rows, out, 5)
+    send_rows(rows, out, 5, 5)
 
 
 def first_sum_kernel(msg, hot, out):
-    sum_rows(msg, hot, out, 5)
+    sum_rows(msg, hot[...], out, 5, 13, 5)
 
 
 def second_sum_kernel(msg, hot, weight, out):
-    sum_rows(msg, hot, out, 6)
+    sum_rows(msg, hot[...], out, 5, 13, 6)
     tail = jnp.sum(msg[pl.ds(5, NB, stride=6), :], axis=0, keepdims=True)
     weight[...] = jnp.broadcast_to(new_weight(jnp.ones((1, 1), F32), tail[:, 1:2], tail[:, 0:1]), (8, LANES))
 
 
-def primal_step(grads, own, read, weight, own_out, read_out, rows):
-    receive_rows(grads, rows)
-    tau = STEP_SCALE / weight
-
-    def step(v, first, n):
-        x, c, low, high, kind = (v[k * NB : k * NB + n] for k in range(5))
-        return x, project(x - tau * (rows[first : first + n] + c), low, high, kind)
-
-    x, new = step(own, 4 * NT, NB)
+def primal_step(grads, own, read, own_x, read_x, tau, own_out, rows):
+    receive_rows(grads, rows, 13)
+    c, low, high, kind = own
+    x = own_x[...]
+    low, high = bounds(low[...], high[...], kind[...], jnp.inf)
+    new = jnp.minimum(jnp.maximum(x - tau * (rows[4 * NT :] + c[...]), low), high)
     own_out[...] = new
     moved = new - x
-    old, fresh = step(read, 0, 4 * NT)
-    read_out[0 : 4 * NT] = fresh
-    rows[0 : 4 * NT] = 2.0 * fresh - old
-    return total(moved * moved)
-
-
-def first_primal_kernel(grads, own, read, tiles, own_out, read_out, out, rows):
-    moved = primal_step(grads, own, read, jnp.ones((1, 1), F32), own_out, read_out, rows)
+    c, low, high = (read[k * NB : k * NB + 4 * NT] for k in range(1, 4))
+    x = read_x[0 : 4 * NT]
+    new = jnp.minimum(jnp.maximum(x - tau * (rows[0 : 4 * NT] + c), low), high)
+    rows[0 : 4 * NT] = 2.0 * new - x
+    return new, total(moved * moved)
+
+
+def first_primal_kernel(grads, c, low, high, kind, read, own_x, tiles, own_out, read_out, out, rows):
+    new, moved = primal_step(grads, (c, low, high, kind), read, own_x, read, jnp.full((1, 1), STEP_SCALE, F32), own_out, rows)
+    read_out[0 : 4 * NT] = new
     out[...] = pack(forward_tiles(tiles, rows, NK, NQ), moved)
 
 
-def second_primal_kernel(grads, own, own_x, read, read_x, weight, tiles, own_out, out, rows):
-    receive_rows(grads, rows)
+def second_primal_kernel(grads, c, low, high, kind, read, own_x, read_x, weight, tiles, own_out, out, rows):
     tau = STEP_SCALE / weight[0:1, 0:1]
-
-    def step(x, v, first, n):
-        c, low, high, kind = (v[k * NB : k * NB + n] for k in range(1, 5))
-        return project(x - tau * (rows[first : first + n] + c), low, high, kind)
-
-    x = own_x[...]
-    new = step(x, own, 4 * NT, NB)
-    own_out[...] = new
-    moved = new - x
-    old = read_x[0 : 4 * NT]
-    rows[0 : 4 * NT] = 2.0 * step(old, read, 0, 4 * NT) - old
-    out[...] = pack(forward_tiles(tiles, rows, NK, NQ), total(moved * moved))
+    _, moved = primal_step(grads, (c, low, high, kind), read, own_x, read_x, tau, own_out, rows)
+    out[...] = pack(forward_tiles(tiles, rows, NK, NQ), moved)
 
 
 def hessian_kernel(vec, rel, tiles, out, put):
@@ -394,7 +390,7 @@
     transposed_tiles(tiles, take_rows(new, take[...]), rows, NQ)
     rows[0 : 4 * NQ] = hess[0 : 4 * NQ]
     rows[4 * NQ : 4 * NT] = -rows[4 * NQ : 4 * NT]
-    send_rows(rows, out, 6)
+    send_rows(rows, out, 5, 6)
     out[pl.ds(5, NB, stride=6), :] = jnp.where(lane() == 0, primal_total(parts), moved)
 
 
@@ -462,12 +458,12 @@
     inputs = (q_index[0], k_cols, k_rows, wide(primal), wide(objective), wide(lower), wide(upper), wide(bound_kind), wide(dual),
               wide(rhs), wide(row_kind))
     room = [(pltpu.SMEM if i < 3 else pltpu.VMEM)(v.shape, v.dtype) for i, v in enumerate(inputs)]
-    five = ((5 * NB, LANES), F32)
-    first, block, own = call(start_kernel, [((6 * NB, LANES), F32), ((2 * NB + 8, LANES), F32), five], me, *inputs, smem=1,
-                             where=pltpu.HBM, scratch=room + [pltpu.SemaphoreType.DMA((len(inputs),))], limit=66800000)
+    first, block = call(start_kernel, [((FIRST * NB, LANES), F32), ((2 * NB + 8, LANES), F32)], me, *inputs, smem=1,
+                        where=pltpu.HBM, scratch=room + [pltpu.SemaphoreType.DMA((len(inputs),))], limit=66800000)
     parts = over_group(block)
     got = exchange(first)
-    msg = call(first_gather_kernel, [five], got)
+    four = ((4 * NB, LANES), F32)
+    msg = call(first_gather_kernel, [four], got)
     want = exchange(msg)
     wide_block = ((NB, 2 * LANES), F32)
     scalar = ((8, LANES), F32)
@@ -475,16 +471,19 @@
     grads = (pltpu.VMEM((104, LANES), F32),)
     y, b, kind, rel, take, hot, read, msg = call(
         first_products_kernel,
-        [wide_block, wide_block, wide_block, ((32, LANES), I32), ((2 * LANES, LANES), BF16), ((208, NT * NB), BF16), five, five],
+        [wide_block, wide_block, wide_block, ((32, LANES), I32), ((2 * LANES, LANES), BF16), ((208, NT * NB), BF16),
+         four, ((5 * NB, LANES), F32)],
         want, got, *parts, hess, cons, scratch=ROWS_SCRATCH)
     msg = call(first_sum_kernel, [cube], exchange(msg), hot)
-    own_x, read_x, prods = call(first_primal_kernel, [ROWS, ROWS, PACKED], exchange_in_cube(msg), own, read, cons, scratch=grads)
+    own = [wide(v) for v in (objective, lower, upper, bound_kind)]
+    own_x, read_x, prods = call(first_primal_kernel, [ROWS, ((4 * NT, LANES), F32), PACKED], exchange_in_cube(msg), *own, read,
+                                wide(primal), cons, scratch=grads)
     parts = over_group(prods)
     hess_prod, put = call(hessian_kernel, [ROWS, ((4 * LANES, 2 * LANES), BF16)], read_x, rel, hess)
     y, msg = call(dual_kernel, [wide_block, ((6 * NB, LANES), F32)], *parts, put, take, y, b, kind, hess_prod, cons,
                   scratch=ROWS_SCRATCH)
     weight, msg = call(second_sum_kernel, [scalar, cube], exchange(msg), hot)
-    final, prods = call(second_primal_kernel, [ROWS, PACKED], exchange_in_cube(msg), own, own_x, read, read_x, weight, cons,
+    final, prods = call(second_primal_kernel, [ROWS, PACKED], exchange_in_cube(msg), *own, read, own_x, read_x, weight, cons,
                         scratch=grads)
     parts = over_group(prods)
     y, msg = call(last_dual_kernel, [ROWS, ROWS], *parts, put, y, b, kind, weight)

time: 138 us -> 137 us (level)
    unnamed x14 -> x22, local copies, waits for them, and re-layouts: 5 us -> 5.01 us
where the time goes in v5:
time: 137 us; the launch traced here: 136 us
  blocking collectives  88.3 us (64%)
  starting transfers between devices  21.3 us (16%)
  waiting for transfers between devices  10.5 us (8%)
  Pallas kernels  10.2 us (7%)
  local copies, waits for them, and re-layouts  5.01 us (4%)
    all_to_all x4, blocking collectives, exchange(): out = lax.all_to_all(rows.reshape(NB, 1, k * LANES), BLK, 0, 0, tiled=True)  74.2 us
    ppermute x9, starting transfers between devices, over_group(): parts.append(lax.ppermute(rows, GRP, [(i, i ^ k) for i in range(4)]))  16.2 us
    all_to_all x2, blocking collectives, exchange_in_cube(): lax.all_to_all(rows.reshape(8, 1, k * LANES), CUBE, 0, 0, tiled=True)  14.1 us
    ppermute x9, waiting for transfers between devices, over_group(): parts.append(lax.ppermute(rows, GRP, [(i, i ^ k) for i in range(4)]))  10.5 us
    pallas_call x11, Pallas kernels, call(): pl.pallas_call(kernel, out_shape=shapes, in_specs=[s] * smem + [w] * (len...  10.2 us
    all_to_all x1, starting transfers between devices, exchange(): out = lax.all_to_all(rows.reshape(NB, 1, k * LANES), BLK, 0, 0, tiled=True)  5.08 us
    unnamed x22, local copies, waits for them, and re-layouts  5.01 us
  transfers between devices with their start and end apart: 10, of which 6 were waited for; matrix products, arithmetic and copies ran while one was open for 0% of the time, Pallas kernels for 0%

profile of v5, /device:TPU:1, one launch (start us, length us, event | category | flops | bytes accessed | tf_op | source)
XLA Modules:
  0.0 136.1 jit_solution(8155598163293960585)
XLA Ops:
  0.6 1.8 %shard_map.148 = (f32[320,128]{1,0:T(8,128)}, f32[136,128]{1,0:T(8,128)}) custom-call(s32[1]{0:T(128)} %bitcast.me, s32[2,4]{1,0:T(2,128)} %bitcast.62, s32[1,6]{1,0:T(1,128)} %k_cols.1, s32[1,6]{1,0:T(1,128)} %k_rows.1, f32[64,128]{1,0:T(8,128)} %bitcast.44, f32[64,128]{1,0:T(8,128)} %bitcast.46, f32[64,128]{1,0:T(8,128)} %bitcast.49, f32[64,128]{1,0:T(8,128)} %bitcast.52, ...), custom_call_target="tpu_custom_call" | custom-call | flops 10000000000 | bytes 10000000 | tf_op jit(solution)/shard_map/pallas_call | solution.py:416
  2.5 23.5 %all_to_all.35 = f32[64,1,640]{2,1,0:T(1,128)S(1)} all-to-all(f32[64,1,640]{2,1,0:T(1,128)} %bitcast.58), channel_id=1, replica_groups=mesh['grp_0'=2,'grp_1'=2,'zh'=4,'zl'=2,'xh'=2,'xl'=2,'yl'=2] {'zh','zl',..., dimensions={0} | all-to-all | bytes 327680 | tf_op jit(solution)/shard_map/all_to_all | solution.py:435
  26.0 1.8 %shard_map.149 = f32[256,128]{1,0:T(8,128)} custom-call(f32[320,128]{1,0:T(8,128)S(1)} %bitcast.31), custom_call_target="tpu_custom_call" | custom-call | flops 10000000000 | bytes 10000000 | tf_op jit(solution)/shard_map/pallas_call | solution.py:416
  27.7 5.1 %all-to-all-start.1 = ((f32[64,1,512]{2,1,0:T(1,128)}), f32[64,1,512]{2,1,0:T(1,128)S(1)}, u32[]{:S(2)}, u32[]{:S(2)}) async-start(f32[64,1,512]{2,1,0:T(1,128)} %bitcast.12), calls=%async_computation.1 | async-start | bytes 262144 | tf_op jit(solution)/shard_map/all_to_all | solution.py:435
  32.8 4.5 %collective-permute-start.2 = (f32[136,128]{1,0:T(8,128)S(1)}, f32[136,128]{1,0:T(8,128)S(1)}, u32[]{:S(2)}, u32[]{:S(2)}) collective-permute-start(f32[136,128]{1,0:T(8,128)S(1)} %copy-done.3), channel_id=1, source_target_pairs={{0,192},{64,128},{128,64},{192,0},{1,193},{65,129},{129,65},{193,1... | collective-permute-start | bytes 208904 | tf_op jit(solution)/shard_map/ppermute | solution.py:447
  37.3 0.3 collective-permute-start.1
  37.6 0.1 collective-permute-start
  37.8 2.7 %collective-permute-done.2.p3 = f32[136,128]{1,0:T(8,128)S(1)} collective-permute-done((f32[136,128]{1,0:T(8,128)S(1)}, f32[136,128]{1,0:T(8,128)S(1)}, u32[]{:S(2)}, u32[]{:S(2)}) %collective-permute-start.2) | collective-permute-done | bytes 69664 | tf_op jit(solution)/shard_map/ppermute | solution.py:447
  40.5 2.1 %collective-permute-done.1.p2 = f32[136,128]{1,0:T(8,128)S(1)} collective-permute-done((f32[136,128]{1,0:T(8,128)S(1)}, f32[136,128]{1,0:T(8,128)S(1)}, u32[]{:S(2)}, u32[]{:S(2)}) %collective-permute-start.1) | collective-permute-done | bytes 69664 | tf_op jit(solution)/shard_map/ppermute | solution.py:447
  42.6 2.8 %copy-done = f32[1,6,512,512]{3,2,1,0:T(8,128)S(1)} copy-done((f32[1,6,512,512]{3,2,1,0:T(8,128)S(1)}, f32[1,6,512,512]{3,2,1,0:T(8,128)}, u32[]{:S(2)}) %copy-start) | copy-done | bytes 6291480
  45.4 2.2 %copy-done.1 = f32[1,4,512,512]{3,2,1,0:T(8,128)S(1)} copy-done((f32[1,4,512,512]{3,2,1,0:T(8,128)S(1)}, f32[1,4,512,512]{3,2,1,0:T(8,128)}, u32[]{:S(2)}) %copy-start.1) | copy-done | bytes 4194328
  47.6 1.4 %shard_map.150 = (f32[64,256]{1,0:T(8,128)S(1)}, f32[64,256]{1,0:T(8,128)S(1)}, f32[64,256]{1,0:T(8,128)S(1)}, s32[32,128]{1,0:T(8,128)S(1)}, bf16[256,128]{1,0:...) custom-call(f32[256,128]{1,0:T(8,128)S(1)} %bitcast.35, ...), custom_call_target="tpu_custom_call" | custom-call | flops 10000000000 | bytes 10000000 | tf_op jit(solution)/shard_map/pallas_call | solution.py:416
  49.0 19.9 %all_to_all.36 = f32[64,1,640]{2,1,0:T(1,128)S(1)} all-to-all(f32[64,1,640]{2,1,0:T(1,128)S(1)} %bitcast.33), channel_id=1, replica_groups=mesh['grp_0'=2,'grp_1'=2,'zh'=4,'zl'=2,'xh'=2,'xl'=2,'yl'=2] {'zh','zl',..., dimensions={0} | all-to-all | bytes 327680 | tf_op jit(solution)/shard_map/all_to_all | solution.py:435
  68.9 0.4 shard_map.151
  69.3 7.0 %all_to_all.37 = f32[8,1,1664]{2,1,0:T(1,128)S(1)} all-to-all(f32[8,1,1664]{2,1,0:T(1,128)S(1)} %bitcast.39), channel_id=1, replica_groups=mesh['grp_0'=2,'grp_1'=2,'zh'=4,'zl'=2,'xh'=2,'xl'=2,'yl'=2] {'zl','xl',..., dimensions={0} | all-to-all | bytes 106496 | tf_op jit(solution)/shard_map/all_to_all | solution.py:441
  76.4 0.7 shard_map.152
  77.0 5.6 %collective-permute-start.5 = (f32[32,128]{1,0:T(8,128)S(1)}, f32[32,128]{1,0:T(8,128)S(1)}, u32[]{:S(2)}, u32[]{:S(2)}) collective-permute-start(f32[32,128]{1,0:T(8,128)S(1)} %get-tuple-element.34.p0), channel_id=1, source_target_pairs={{0,192},{64,128},{128,64},{192,0},{1,193},{65,129},{129,65},{193,1... | collective-permute-start | bytes 49160 | tf_op jit(solution)/shard_map/ppermute | solution.py:447
  82.6 0.9 collective-permute-start.4
  83.5 0.6 shard_map.153
  84.1 2.6 %collective-permute-done.4.p2 = f32[32,128]{1,0:T(8,128)S(1)} collective-permute-done((f32[32,128]{1,0:T(8,128)S(1)}, f32[32,128]{1,0:T(8,128)S(1)}, u32[]{:S(2)}, u32[]{:S(2)}) %collective-permute-start.4) | collective-permute-done | bytes 16416 | tf_op jit(solution)/shard_map/ppermute | solution.py:447
  86.7 1.5 %shard_map.154 = (f32[64,256]{1,0:T(8,128)S(1)}, f32[384,128]{1,0:T(8,128)S(1)}) custom-call(f32[32,128]{1,0:T(8,128)S(1)} %get-tuple-element.34.p0, f32[32,128]{1,0:T(8,128)S(1)} %collective-permute-done.3.p1, f32[32,128]{1,0:T(8,128)S(1)} %collective-permute-done.4.p2, f32[32,128]{1,0:T(8,128)S(1)} %collective-permute-done.5.p3, ...), custom_call_target="tpu_custom_call" | custom-call | flops 10000000000 | bytes 10000000 | tf_op jit(solution)/shard_map/pallas_call | solution.py:416
  88.2 16.5 %all_to_all.38 = f32[64,1,768]{2,1,0:T(1,128)S(1)} all-to-all(f32[64,1,768]{2,1,0:T(1,128)S(1)} %bitcast.29), channel_id=1, replica_groups=mesh['grp_0'=2,'grp_1'=2,'zh'=4,'zl'=2,'xh'=2,'xl'=2,'yl'=2] {'zh','zl',..., dimensions={0} | all-to-all | bytes 393216 | tf_op jit(solution)/shard_map/all_to_all | solution.py:435
  104.7 0.4 shard_map.155
  105.1 7.1 %all_to_all.39 = f32[8,1,1664]{2,1,0:T(1,128)S(1)} all-to-all(f32[8,1,1664]{2,1,0:T(1,128)S(1)} %bitcast.38), channel_id=1, replica_groups=mesh['grp_0'=2,'grp_1'=2,'zh'=4,'zl'=2,'xh'=2,'xl'=2,'yl'=2] {'zl','xl',..., dimensions={0} | all-to-all | bytes 106496 | tf_op jit(solution)/shard_map/all_to_all | solution.py:441
  112.2 0.7 shard_map.156
  112.8 3.8 %collective-permute-start.8 = (f32[32,128]{1,0:T(8,128)S(1)}, f32[32,128]{1,0:T(8,128)S(1)}, u32[]{:S(2)}, u32[]{:S(2)}) collective-permute-start(f32[32,128]{1,0:T(8,128)S(1)} %get-tuple-element.47.p0), channel_id=1, source_target_pairs={{0,192},{64,128},{128,64},{192,0},{1,193},{65,129},{129,65},{193,1... | collective-permute-start | bytes 49160 | tf_op jit(solution)/shard_map/ppermute | solution.py:447
  116.6 1.0 collective-permute-start.7
  117.6 0.4 collective-permute-done.8.p3
  118.0 2.7 %collective-permute-done.7.p2 = f32[32,128]{1,0:T(8,128)S(1)} collective-permute-done((f32[32,128]{1,0:T(8,128)S(1)}, f32[32,128]{1,0:T(8,128)S(1)}, u32[]{:S(2)}, u32[]{:S(2)}) %collective-permute-start.7) | collective-permute-done | bytes 16416 | tf_op jit(solution)/shard_map/ppermute | solution.py:447
  120.7 0.3 shard_map.157
  121.0 14.3 %all_to_all.40 = f32[64,1,128]{2,1,0:T(1,128)S(1)} all-to-all(f32[64,1,128]{2,1,0:T(1,128)S(1)} %bitcast.40), channel_id=1, replica_groups=mesh['grp_0'=2,'grp_1'=2,'zh'=4,'zl'=2,'xh'=2,'xl'=2,'yl'=2] {'zh','zl',..., dimensions={0} | all-to-all | bytes 65536 | tf_op jit(solution)/shard_map/all_to_all | solution.py:435
  135.4 0.8 shard_map.158
  (28 shorter events, 0.1 us)
Async XLA Ops:
  26.0 6.8 %copy-start.3 = (f32[136,128]{1,0:T(8,128)S(1)}, f32[136,128]{1,0:T(8,128)}, u32[]{:S(2)}) copy-start(f32[136,128]{1,0:T(8,128)} %get-tuple-element.30.p0) | copy-start | bytes 208900
  27.7 14.9 %all-to-all-start.1 = ((f32[64,1,512]{2,1,0:T(1,128)}), f32[64,1,512]{2,1,0:T(1,128)S(1)}, u32[]{:S(2)}, u32[]{:S(2)}) async-start(f32[64,1,512]{2,1,0:T(1,128)} %bitcast.12), calls=%async_computation.1 | async-start | bytes 262144 | tf_op jit(solution)/shard_map/all_to_all | solution.py:435
  32.8 7.7 %collective-permute-start.2 = (f32[136,128]{1,0:T(8,128)S(1)}, f32[136,128]{1,0:T(8,128)S(1)}, u32[]{:S(2)}, u32[]{:S(2)}) collective-permute-start(f32[136,128]{1,0:T(8,128)S(1)} %copy-done.3), channel_id=1, source_target_pairs={{0,192},{64,128},{128,64},{192,0},{1,193},{65,129},{129,65},{193,1... | collective-permute-start | bytes 208904 | tf_op jit(solution)/shard_map/ppermute | solution.py:447
  37.3 5.3 %collective-permute-start.1 = (f32[136,128]{1,0:T(8,128)S(1)}, f32[136,128]{1,0:T(8,128)S(1)}, u32[]{:S(2)}, u32[]{:S(2)}) collective-permute-start(f32[136,128]{1,0:T(8,128)S(1)} %copy-done.3), channel_id=1, source_target_pairs={{0,128},{64,192},{128,0},{192,64},{1,129},{65,193},{129,1},{193,65... | collective-permute-start | bytes 208904 | tf_op jit(solution)/shard_map/ppermute | solution.py:447
  37.6 4.9 %collective-permute-start = (f32[136,128]{1,0:T(8,128)S(1)}, f32[136,128]{1,0:T(8,128)S(1)}, u32[]{:S(2)}, u32[]{:S(2)}) collective-permute-start(f32[136,128]{1,0:T(8,128)S(1)} %copy-done.3), channel_id=1, source_target_pairs={{0,64},{64,0},{128,192},{192,128},{1,65},{65,1},{129,193},{193,129... | collective-permute-start | bytes 208904 | tf_op jit(solution)/shard_map/ppermute | solution.py:447
  42.6 2.8 %copy-start = (f32[1,6,512,512]{3,2,1,0:T(8,128)S(1)}, f32[1,6,512,512]{3,2,1,0:T(8,128)}, u32[]{:S(2)}) copy-start(f32[1,6,512,512]{3,2,1,0:T(8,128)} %tiles.7) | copy-start | bytes 18874372
  45.4 2.2 %copy-start.1 = (f32[1,4,512,512]{3,2,1,0:T(8,128)S(1)}, f32[1,4,512,512]{3,2,1,0:T(8,128)}, u32[]{:S(2)}) copy-start(f32[1,4,512,512]{3,2,1,0:T(8,128)} %tiles.5) | copy-start | bytes 12582916
  47.6 28.7 %slice-start = ((s8[6291456]{0:T(1024)(128)(4,1)}), s8[2097152]{0:T(1024)(128)(4,1)S(1)}, s32[]{:S(2)}) async-start(s8[6291456]{0:T(1024)(128)(4,1)} %bitcast.42), calls=%async_computation.7 | async-start | bytes 4194304
  49.0 27.3 %slice-start.1 = ((s8[6291456]{0:T(1024)(128)(4,1)}), s8[4194304]{0:T(1024)(128)(4,1)S(1)}, s32[]{:S(2)}) async-start(s8[6291456]{0:T(1024)(128)(4,1)} %bitcast.42), calls=%async_computation.8 | async-start | bytes 8388608
  68.9 7.4 %copy-start.4 = (f32[8192]{0:T(1024)S(1)}, f32[8192]{0:T(1024)}, u32[]{:S(2)}) copy-start(f32[8192]{0:T(1024)} %param.13) | copy-start | bytes 98308
  68.9 7.4 %copy-start.5 = (f32[8192]{0:T(1024)S(1)}, f32[8192]{0:T(1024)}, u32[]{:S(2)}) copy-start(f32[8192]{0:T(1024)} %param.15) | copy-start | bytes 98308
  68.9 7.4 %copy-start.6 = (f32[8192]{0:T(1024)S(1)}, f32[8192]{0:T(1024)}, u32[]{:S(2)}) copy-start(f32[8192]{0:T(1024)} %param.16) | copy-start | bytes 98308
  68.9 7.4 %copy-start.7 = (f32[8192]{0:T(1024)S(1)}, f32[8192]{0:T(1024)}, u32[]{:S(2)}) copy-start(f32[8192]{0:T(1024)} %param.17) | copy-start | bytes 98308
  68.9 7.4 %copy-start.8 = (s32[8192]{0:T(1024)S(1)}, s32[8192]{0:T(1024)}, u32[]{:S(2)}) copy-start(s32[8192]{0:T(1024)} %param.18) | copy-start | bytes 98308
  76.3 7.1 %copy-start.2 = (f32[1,4,512,512]{3,2,1,0:T(8,128)S(1)}, f32[1,4,512,512]{3,2,1,0:T(8,128)}, u32[]{:S(2)}) copy-start(f32[1,4,512,512]{3,2,1,0:T(8,128)} %tiles.5) | copy-start | bytes 12582916
  77.0 7.0 %collective-permute-start.5 = (f32[32,128]{1,0:T(8,128)S(1)}, f32[32,128]{1,0:T(8,128)S(1)}, u32[]{:S(2)}, u32[]{:S(2)}) collective-permute-start(f32[32,128]{1,0:T(8,128)S(1)} %get-tuple-element.34.p0), channel_id=1, source_target_pairs={{0,192},{64,128},{128,64},{192,0},{1,193},{65,129},{129,65},{193,1... | collective-permute-start | bytes 49160 | tf_op jit(solution)/shard_map/ppermute | solution.py:447
  82.6 4.1 %collective-permute-start.4 = (f32[32,128]{1,0:T(8,128)S(1)}, f32[32,128]{1,0:T(8,128)S(1)}, u32[]{:S(2)}, u32[]{:S(2)}) collective-permute-start(f32[32,128]{1,0:T(8,128)S(1)} %get-tuple-element.34.p0), channel_id=1, source_target_pairs={{0,128},{64,192},{128,0},{192,64},{1,129},{65,193},{129,1},{193,65... | collective-permute-start | bytes 49160 | tf_op jit(solution)/shard_map/ppermute | solution.py:447
  83.5 3.2 %collective-permute-start.3 = (f32[32,128]{1,0:T(8,128)S(1)}, f32[32,128]{1,0:T(8,128)S(1)}, u32[]{:S(2)}, u32[]{:S(2)}) collective-permute-start(f32[32,128]{1,0:T(8,128)S(1)} %get-tuple-element.34.p0), channel_id=1, source_target_pairs={{0,64},{64,0},{128,192},{192,128},{1,65},{65,1},{129,193},{193,129... | collective-permute-start | bytes 49160 | tf_op jit(solution)/shard_map/ppermute | solution.py:447
  112.8 5.2 %collective-permute-start.8 = (f32[32,128]{1,0:T(8,128)S(1)}, f32[32,128]{1,0:T(8,128)S(1)}, u32[]{:S(2)}, u32[]{:S(2)}) collective-permute-start(f32[32,128]{1,0:T(8,128)S(1)} %get-tuple-element.47.p0), channel_id=1, source_target_pairs={{0,192},{64,128},{128,64},{192,0},{1,193},{65,129},{129,65},{193,1... | collective-permute-start | bytes 49160 | tf_op jit(solution)/shard_map/ppermute | solution.py:447
  116.6 4.1 %collective-permute-start.7 = (f32[32,128]{1,0:T(8,128)S(1)}, f32[32,128]{1,0:T(8,128)S(1)}, u32[]{:S(2)}, u32[]{:S(2)}) collective-permute-start(f32[32,128]{1,0:T(8,128)S(1)} %get-tuple-element.47.p0), channel_id=1, source_target_pairs={{0,128},{64,192},{128,0},{192,64},{1,129},{65,193},{129,1},{193,65... | collective-permute-start | bytes 49160 | tf_op jit(solution)/shard_map/ppermute | solution.py:447
  117.6 3.1 %collective-permute-start.6 = (f32[32,128]{1,0:T(8,128)S(1)}, f32[32,128]{1,0:T(8,128)S(1)}, u32[]{:S(2)}, u32[]{:S(2)}) collective-permute-start(f32[32,128]{1,0:T(8,128)S(1)} %get-tuple-element.47.p0), channel_id=1, source_target_pairs={{0,64},{64,0},{128,192},{192,128},{1,65},{65,1},{129,193},{193,129... | collective-permute-start | bytes 49160 | tf_op jit(solution)/shard_map/ppermute | solution.py:447

commit v6 on v5

--- a/solution.py
+++ b/solution.py
@@ -66,23 +66,33 @@
     return jnp.broadcast_to(v[:, c : c + 1], v.shape)
 
 
-def gather_tiles(ids, tables, out, first, k):
+def gather_tiles(ids, tables, out):
     ln = lane()
-    t_of = along(ids & 15, slot_of(ln))
-    idx = (ln & 64) + t_of * 4 + (ln & 3)
+    slot = slot_of(ln)
+
+    def index(tile):
+        return (ln & 64) + along(ids & 15, tile) * 4 + (ln & 3)
+
+    idx = [index(jnp.where(slot < NT, slot, slot - NT + n * (16 - NT))) for n in range(2)]
     owner = ids >> 4
     ones = []
     for j in range(NT):
         o = jnp.where((ln & 63) == column(owner, j), 1.0, 0.0).astype(BF16)
         ones.append(jnp.concatenate([o, o], axis=1))
     ones = jnp.concatenate(ones, axis=0)
-    for n, table in enumerate(tables):
-        a, b, c = split(table, 3)
-        got = dot(ones, jnp.concatenate([a, b, c, jnp.zeros_like(a)], axis=0))
+    got = []
+    for n in (0, 2):
+        pieces = [jnp.concatenate([a, b], axis=1) for a, b in zip(split(tables[n], 3), split(tables[n + 1], 3))]
+        both = dot(ones, jnp.concatenate([*pieces, jnp.zeros_like(pieces[0])], axis=0))
+        got += [both[:, :LANES], both[:, LANES:]]
+    for n in range(3):
         msg = jnp.zeros((NB, LANES), F32)
-        for j in range(NT):
-            msg = jnp.where(slot_of(ln) == j, along(got[j * NB : (j + 1) * NB], idx), msg)
-        out[pl.ds(first + n, NB, stride=k), :] = msg
+        for s in range(16):
+            j = s if s < NT else s - NT + n * (16 - NT)
+            if j < NT:
+                table = got[n if s < NT else 3]
+                msg = jnp.where(slot == s, along(table[j * NB : (j + 1) * NB], idx[n & 1]), msg)
+        out[pl.ds(n, NB, stride=3), :] = msg
 
 
 def cube_of(b):
@@ -144,12 +154,8 @@
 def sum_rows(msg, hot, out, n, m, k):
     blocks = [msg[pl.ds(i, NB, stride=k), :] for i in range(n)]
     blocks += [pltpu.roll(v, 64, 1) for v in blocks]
-    high, low = [], []
-    for v in blocks:
-        a, b = split(v, 2)
-        high.append(a)
-        low.append(b)
-    got = dot(hot, jnp.concatenate(high, axis=0)) + dot(hot, jnp.concatenate(low, axis=0))
+    got = dot(hot, jnp.concatenate([jnp.concatenate(split(v, 2), axis=1) for v in blocks], axis=0))
+    got = got[:, :LANES] + got[:, LANES:]
     left = lane(8) < 64
     for kk in range(m):
         out[pl.ds(kk, 8, stride=m), :] = jnp.where(left, got[8 * kk : 8 * kk + 8], got[8 * (m + kk) : 8 * (m + kk) + 8])
@@ -230,7 +236,8 @@
         a, b = split(unpack(p), 2)
         high.append(a)
         low.append(b)
-    extrap = dot(jnp.concatenate(high, axis=1), hot) + dot(jnp.concatenate(low, axis=1), hot)
+    extrap = dot(jnp.concatenate([jnp.concatenate(high, axis=1), jnp.concatenate(low, axis=1)], axis=0), hot)
+    extrap = extrap[:NB] + extrap[NB:]
     new = y + step * (rhs - extrap)
     new = jnp.where(kind == 1.0, jnp.maximum(new, 0.0), new)
     moved = new - y
@@ -282,7 +289,7 @@
 
 def first_gather_kernel(got, msg):
     ids = got[pl.ds(IDS, NB, stride=FIRST), :].astype(I32)
-    gather_tiles(ids, [got[pl.ds(n, NB, stride=FIRST), :] for n in range(4)], msg, 0, 4)
+    gather_tiles(ids, [got[pl.ds(n, NB, stride=FIRST), :] for n in range(4)], msg)
 
 
 def dual_tables(parts, y, rhs, kind, tiles, take):
@@ -317,16 +324,20 @@
 
 
 def take_rows(y, take):
-    a, b = split(y, 2)
-    return dot(a, take) + dot(b, take)
+    got = dot(jnp.concatenate(split(y, 2), axis=0), take)
+    return got[:NB] + got[NB:]
 
 
 def first_products_kernel(msg, got, p0, p1, p2, p3, hess, cons, y, rhs, kind, tiles, take, hot, read, out, rows):
     hot[...] = match_table(got)
     dual_tables([p0, p1, p2, p3], y, rhs, kind, tiles, take)
-    m = [msg[pl.ds(n, NB, stride=4), :] for n in range(4)]
-    for n, v in enumerate((*spread_two(m[0], m[1]), *spread_two(m[2], m[3]))):
-        read[n * NB : (n + 1) * NB] = v
+    m = [msg[pl.ds(n, NB, stride=3), :] for n in range(3)]
+    m = (*spread_two(m[0], m[1]), spread(m[2]))
+    for n in range(3):
+        read[n * NB : (n + 1) * NB] = m[n]
+    read[3 * NB : 3 * NB + 24] = m[0][40:64]
+    read[3 * NB + 24 : 3 * NB + 40] = m[1][40:56]
+    read[3 * NB + 40 : 4 * NB] = jnp.zeros((24, LANES), F32)
     first = spread(forward_tiles(hess, read, NQ, 0))
     transposed_tiles(cons, take_rows(y[...], take[...]), rows, NQ)
     rows[0 : 4 * NQ] = first[0 : 4 * NQ]
@@ -463,7 +474,7 @@
     parts = over_group(block)
     got = exchange(first)
     four = ((4 * NB, LANES), F32)
-    msg = call(first_gather_kernel, [four], got)
+    msg = call(first_gather_kernel, [((3 * NB, LANES), F32)], got)
     want = exchange(msg)
     wide_block = ((NB, 2 * LANES), F32)
     scalar = ((8, LANES), F32)

time: 137 us -> 136 us (level)
  transfers between devices with their start and end apart: 10 -> 10, of which waited for: 6 -> 7; matrix products, arithmetic and copies ran while one was open for 0% -> 0% of each run, Pallas kernels for 0% -> 0%
where the time goes in v6:
time: 136 us
  blocking collectives  88.4 us (65%)
  starting transfers between devices  20.9 us (15%)
  waiting for transfers between devices  10.7 us (8%)
  Pallas kernels  9.98 us (7%)
  local copies, waits for them, and re-layouts  5.01 us (4%)
    all_to_all x4, blocking collectives, exchange(): out = lax.all_to_all(rows.reshape(NB, 1, k * LANES), BLK, 0, 0, tiled=True)  74.3 us
    ppermute x9, starting transfers between devices, over_group(): parts.append(lax.ppermute(rows, GRP, [(i, i ^ k) for i in range(4)]))  15.8 us
    all_to_all x2, blocking collectives, exchange_in_cube(): lax.all_to_all(rows.reshape(8, 1, k * LANES), CUBE, 0, 0, tiled=True)  14.2 us
    ppermute x9, waiting for transfers between devices, over_group(): parts.append(lax.ppermute(rows, GRP, [(i, i ^ k) for i in range(4)]))  10.6 us
    pallas_call x11, Pallas kernels, call(): pl.pallas_call(kernel, out_shape=shapes, in_specs=[s] * smem + [w] * (len...  9.98 us
    all_to_all x1, starting transfers between devices, exchange(): out = lax.all_to_all(rows.reshape(NB, 1, k * LANES), BLK, 0, 0, tiled=True)  5.08 us
    unnamed x22, local copies, waits for them, and re-layouts  5.01 us
  transfers between devices with their start and end apart: 10, of which 7 were waited for; matrix products, arithmetic and copies ran while one was open for 0% of the time, Pallas kernels for 0%

profile of v6, /device:TPU:1, one launch (start us, length us, event | category | flops | bytes accessed | tf_op | source)
XLA Modules:
  0.0 135.8 jit_solution(12574079351752840959)
XLA Ops:
  0.6 1.8 %shard_map.148 = (f32[320,128]{1,0:T(8,128)}, f32[136,128]{1,0:T(8,128)}) custom-call(s32[1]{0:T(128)} %bitcast.me, s32[2,4]{1,0:T(2,128)} %bitcast.62, s32[1,6]{1,0:T(1,128)} %k_cols.1, s32[1,6]{1,0:T(1,128)} %k_rows.1, f32[64,128]{1,0:T(8,128)} %bitcast.44, f32[64,128]{1,0:T(8,128)} %bitcast.46, f32[64,128]{1,0:T(8,128)} %bitcast.49, f32[64,128]{1,0:T(8,128)} %bitcast.52, ...), custom_call_target="tpu_custom_call" | custom-call | flops 10000000000 | bytes 10000000 | tf_op jit(solution)/shard_map/pallas_call | solution.py:427
  2.5 23.5 %all_to_all.35 = f32[64,1,640]{2,1,0:T(1,128)S(1)} all-to-all(f32[64,1,640]{2,1,0:T(1,128)} %bitcast.58), channel_id=1, replica_groups=mesh['grp_0'=2,'grp_1'=2,'zh'=4,'zl'=2,'xh'=2,'xl'=2,'yl'=2] {'zh','zl',..., dimensions={0} | all-to-all | bytes 327680 | tf_op jit(solution)/shard_map/all_to_all | solution.py:446
  26.0 1.8 %shard_map.149 = f32[192,128]{1,0:T(8,128)} custom-call(f32[320,128]{1,0:T(8,128)S(1)} %bitcast.31), custom_call_target="tpu_custom_call" | custom-call | flops 10000000000 | bytes 10000000 | tf_op jit(solution)/shard_map/pallas_call | solution.py:427
  27.8 5.1 %all-to-all-start.1 = ((f32[64,1,384]{2,1,0:T(1,128)}), f32[64,1,384]{2,1,0:T(1,128)S(1)}, u32[]{:S(2)}, u32[]{:S(2)}) async-start(f32[64,1,384]{2,1,0:T(1,128)} %bitcast.12), calls=%async_computation.1 | async-start | bytes 196608 | tf_op jit(solution)/shard_map/all_to_all | solution.py:446
  32.9 4.5 %collective-permute-start.2 = (f32[136,128]{1,0:T(8,128)S(1)}, f32[136,128]{1,0:T(8,128)S(1)}, u32[]{:S(2)}, u32[]{:S(2)}) collective-permute-start(f32[136,128]{1,0:T(8,128)S(1)} %copy-done.3), channel_id=1, source_target_pairs={{0,192},{64,128},{128,64},{192,0},{1,193},{65,129},{129,65},{193,1... | collective-permute-start | bytes 208904 | tf_op jit(solution)/shard_map/ppermute | solution.py:458
  37.3 0.4 collective-permute-start.1
  37.7 0.1 collective-permute-start
  37.8 2.6 %collective-permute-done.2.p3 = f32[136,128]{1,0:T(8,128)S(1)} collective-permute-done((f32[136,128]{1,0:T(8,128)S(1)}, f32[136,128]{1,0:T(8,128)S(1)}, u32[]{:S(2)}, u32[]{:S(2)}) %collective-permute-start.2) | collective-permute-done | bytes 69664 | tf_op jit(solution)/shard_map/ppermute | solution.py:458
  40.5 2.0 %collective-permute-done.1.p2 = f32[136,128]{1,0:T(8,128)S(1)} collective-permute-done((f32[136,128]{1,0:T(8,128)S(1)}, f32[136,128]{1,0:T(8,128)S(1)}, u32[]{:S(2)}, u32[]{:S(2)}) %collective-permute-start.1) | collective-permute-done | bytes 69664 | tf_op jit(solution)/shard_map/ppermute | solution.py:458
  42.6 2.8 %copy-done = f32[1,6,512,512]{3,2,1,0:T(8,128)S(1)} copy-done((f32[1,6,512,512]{3,2,1,0:T(8,128)S(1)}, f32[1,6,512,512]{3,2,1,0:T(8,128)}, u32[]{:S(2)}) %copy-start) | copy-done | bytes 6291480
  45.4 2.2 %copy-done.1 = f32[1,4,512,512]{3,2,1,0:T(8,128)S(1)} copy-done((f32[1,4,512,512]{3,2,1,0:T(8,128)S(1)}, f32[1,4,512,512]{3,2,1,0:T(8,128)}, u32[]{:S(2)}) %copy-start.1) | copy-done | bytes 4194328
  47.6 1.4 shard_map.150
  48.9 20.1 %all_to_all.36 = f32[64,1,640]{2,1,0:T(1,128)S(1)} all-to-all(f32[64,1,640]{2,1,0:T(1,128)S(1)} %bitcast.33), channel_id=1, replica_groups=mesh['grp_0'=2,'grp_1'=2,'zh'=4,'zl'=2,'xh'=2,'xl'=2,'yl'=2] {'zh','zl',..., dimensions={0} | all-to-all | bytes 327680 | tf_op jit(solution)/shard_map/all_to_all | solution.py:446
  69.1 0.3 shard_map.151
  69.4 7.0 %all_to_all.37 = f32[8,1,1664]{2,1,0:T(1,128)S(1)} all-to-all(f32[8,1,1664]{2,1,0:T(1,128)S(1)} %bitcast.39), channel_id=1, replica_groups=mesh['grp_0'=2,'grp_1'=2,'zh'=4,'zl'=2,'xh'=2,'xl'=2,'yl'=2] {'zl','xl',..., dimensions={0} | all-to-all | bytes 106496 | tf_op jit(solution)/shard_map/all_to_all | solution.py:452
  76.5 0.7 shard_map.152
  77.1 5.4 %collective-permute-start.5 = (f32[32,128]{1,0:T(8,128)S(1)}, f32[32,128]{1,0:T(8,128)S(1)}, u32[]{:S(2)}, u32[]{:S(2)}) collective-permute-start(f32[32,128]{1,0:T(8,128)S(1)} %get-tuple-element.34.p0), channel_id=1, source_target_pairs={{0,192},{64,128},{128,64},{192,0},{1,193},{65,129},{129,65},{193,1... | collective-permute-start | bytes 49160 | tf_op jit(solution)/shard_map/ppermute | solution.py:458
  82.5 0.7 collective-permute-start.4
  83.3 0.6 shard_map.153
  83.9 2.7 %collective-permute-done.4.p2 = f32[32,128]{1,0:T(8,128)S(1)} collective-permute-done((f32[32,128]{1,0:T(8,128)S(1)}, f32[32,128]{1,0:T(8,128)S(1)}, u32[]{:S(2)}, u32[]{:S(2)}) %collective-permute-start.4) | collective-permute-done | bytes 16416 | tf_op jit(solution)/shard_map/ppermute | solution.py:458
  86.6 1.4 %shard_map.154 = (f32[64,256]{1,0:T(8,128)S(1)}, f32[384,128]{1,0:T(8,128)S(1)}) custom-call(f32[32,128]{1,0:T(8,128)S(1)} %get-tuple-element.34.p0, f32[32,128]{1,0:T(8,128)S(1)} %collective-permute-done.3.p1, f32[32,128]{1,0:T(8,128)S(1)} %collective-permute-done.4.p2, f32[32,128]{1,0:T(8,128)S(1)} %collective-permute-done.5.p3, ...), custom_call_target="tpu_custom_call" | custom-call | flops 10000000000 | bytes 10000000 | tf_op jit(solution)/shard_map/pallas_call | solution.py:427
  88.0 16.3 %all_to_all.38 = f32[64,1,768]{2,1,0:T(1,128)S(1)} all-to-all(f32[64,1,768]{2,1,0:T(1,128)S(1)} %bitcast.29), channel_id=1, replica_groups=mesh['grp_0'=2,'grp_1'=2,'zh'=4,'zl'=2,'xh'=2,'xl'=2,'yl'=2] {'zh','zl',..., dimensions={0} | all-to-all | bytes 393216 | tf_op jit(solution)/shard_map/all_to_all | solution.py:446
  104.4 0.3 shard_map.155
  104.7 7.2 %all_to_all.39 = f32[8,1,1664]{2,1,0:T(1,128)S(1)} all-to-all(f32[8,1,1664]{2,1,0:T(1,128)S(1)} %bitcast.38), channel_id=1, replica_groups=mesh['grp_0'=2,'grp_1'=2,'zh'=4,'zl'=2,'xh'=2,'xl'=2,'yl'=2] {'zl','xl',..., dimensions={0} | all-to-all | bytes 106496 | tf_op jit(solution)/shard_map/all_to_all | solution.py:452
  111.8 0.7 shard_map.156
  112.5 3.8 %collective-permute-start.8 = (f32[32,128]{1,0:T(8,128)S(1)}, f32[32,128]{1,0:T(8,128)S(1)}, u32[]{:S(2)}, u32[]{:S(2)}) collective-permute-start(f32[32,128]{1,0:T(8,128)S(1)} %get-tuple-element.47.p0), channel_id=1, source_target_pairs={{0,192},{64,128},{128,64},{192,0},{1,193},{65,129},{129,65},{193,1... | collective-permute-start | bytes 49160 | tf_op jit(solution)/shard_map/ppermute | solution.py:458
  116.3 0.9 collective-permute-start.7
  117.2 0.5 collective-permute-done.8.p3
  117.7 2.7 %collective-permute-done.7.p2 = f32[32,128]{1,0:T(8,128)S(1)} collective-permute-done((f32[32,128]{1,0:T(8,128)S(1)}, f32[32,128]{1,0:T(8,128)S(1)}, u32[]{:S(2)}, u32[]{:S(2)}) %collective-permute-start.7) | collective-permute-done | bytes 16416 | tf_op jit(solution)/shard_map/ppermute | solution.py:458
  120.4 0.3 shard_map.157
  120.7 14.3 %all_to_all.40 = f32[64,1,128]{2,1,0:T(1,128)S(1)} all-to-all(f32[64,1,128]{2,1,0:T(1,128)S(1)} %bitcast.40), channel_id=1, replica_groups=mesh['grp_0'=2,'grp_1'=2,'zh'=4,'zl'=2,'xh'=2,'xl'=2,'yl'=2] {'zh','zl',..., dimensions={0} | all-to-all | bytes 65536 | tf_op jit(solution)/shard_map/all_to_all | solution.py:446
  135.1 0.8 shard_map.158
  (28 shorter events, 0.3 us)
Async XLA Ops:
  26.0 6.9 %copy-start.3 = (f32[136,128]{1,0:T(8,128)S(1)}, f32[136,128]{1,0:T(8,128)}, u32[]{:S(2)}) copy-start(f32[136,128]{1,0:T(8,128)} %get-tuple-element.30.p0) | copy-start | bytes 208900
  27.8 14.8 %all-to-all-start.1 = ((f32[64,1,384]{2,1,0:T(1,128)}), f32[64,1,384]{2,1,0:T(1,128)S(1)}, u32[]{:S(2)}, u32[]{:S(2)}) async-start(f32[64,1,384]{2,1,0:T(1,128)} %bitcast.12), calls=%async_computation.1 | async-start | bytes 196608 | tf_op jit(solution)/shard_map/all_to_all | solution.py:446
  32.9 7.6 %collective-permute-start.2 = (f32[136,128]{1,0:T(8,128)S(1)}, f32[136,128]{1,0:T(8,128)S(1)}, u32[]{:S(2)}, u32[]{:S(2)}) collective-permute-start(f32[136,128]{1,0:T(8,128)S(1)} %copy-done.3), channel_id=1, source_target_pairs={{0,192},{64,128},{128,64},{192,0},{1,193},{65,129},{129,65},{193,1... | collective-permute-start | bytes 208904 | tf_op jit(solution)/shard_map/ppermute | solution.py:458
  37.3 5.1 %collective-permute-start.1 = (f32[136,128]{1,0:T(8,128)S(1)}, f32[136,128]{1,0:T(8,128)S(1)}, u32[]{:S(2)}, u32[]{:S(2)}) collective-permute-start(f32[136,128]{1,0:T(8,128)S(1)} %copy-done.3), channel_id=1, source_target_pairs={{0,128},{64,192},{128,0},{192,64},{1,129},{65,193},{129,1},{193,65... | collective-permute-start | bytes 208904 | tf_op jit(solution)/shard_map/ppermute | solution.py:458
  37.7 4.8 %collective-permute-start = (f32[136,128]{1,0:T(8,128)S(1)}, f32[136,128]{1,0:T(8,128)S(1)}, u32[]{:S(2)}, u32[]{:S(2)}) collective-permute-start(f32[136,128]{1,0:T(8,128)S(1)} %copy-done.3), channel_id=1, source_target_pairs={{0,64},{64,0},{128,192},{192,128},{1,65},{65,1},{129,193},{193,129... | collective-permute-start | bytes 208904 | tf_op jit(solution)/shard_map/ppermute | solution.py:458
  42.6 2.8 %copy-start = (f32[1,6,512,512]{3,2,1,0:T(8,128)S(1)}, f32[1,6,512,512]{3,2,1,0:T(8,128)}, u32[]{:S(2)}) copy-start(f32[1,6,512,512]{3,2,1,0:T(8,128)} %tiles.7) | copy-start | bytes 18874372
  45.4 2.2 %copy-start.1 = (f32[1,4,512,512]{3,2,1,0:T(8,128)S(1)}, f32[1,4,512,512]{3,2,1,0:T(8,128)}, u32[]{:S(2)}) copy-start(f32[1,4,512,512]{3,2,1,0:T(8,128)} %tiles.5) | copy-start | bytes 12582916
  47.6 28.9 %slice-start = ((s8[6291456]{0:T(1024)(128)(4,1)}), s8[2097152]{0:T(1024)(128)(4,1)S(1)}, s32[]{:S(2)}) async-start(s8[6291456]{0:T(1024)(128)(4,1)} %bitcast.42), calls=%async_computation.7 | async-start | bytes 4194304
  48.9 27.5 %slice-start.1 = ((s8[6291456]{0:T(1024)(128)(4,1)}), s8[4194304]{0:T(1024)(128)(4,1)S(1)}, s32[]{:S(2)}) async-start(s8[6291456]{0:T(1024)(128)(4,1)} %bitcast.42), calls=%async_computation.8 | async-start | bytes 8388608
  69.1 7.3 %copy-start.4 = (f32[8192]{0:T(1024)S(1)}, f32[8192]{0:T(1024)}, u32[]{:S(2)}) copy-start(f32[8192]{0:T(1024)} %param.13) | copy-start | bytes 98308
  69.1 7.4 %copy-start.5 = (f32[8192]{0:T(1024)S(1)}, f32[8192]{0:T(1024)}, u32[]{:S(2)}) copy-start(f32[8192]{0:T(1024)} %param.15) | copy-start | bytes 98308
  69.1 7.4 %copy-start.6 = (f32[8192]{0:T(1024)S(1)}, f32[8192]{0:T(1024)}, u32[]{:S(2)}) copy-start(f32[8192]{0:T(1024)} %param.16) | copy-start | bytes 98308
  69.1 7.4 %copy-start.7 = (f32[8192]{0:T(1024)S(1)}, f32[8192]{0:T(1024)}, u32[]{:S(2)}) copy-start(f32[8192]{0:T(1024)} %param.17) | copy-start | bytes 98308
  69.1 7.4 %copy-start.8 = (s32[8192]{0:T(1024)S(1)}, s32[8192]{0:T(1024)}, u32[]{:S(2)}) copy-start(s32[8192]{0:T(1024)} %param.18) | copy-start | bytes 98308
  76.5 6.8 %copy-start.2 = (f32[1,4,512,512]{3,2,1,0:T(8,128)S(1)}, f32[1,4,512,512]{3,2,1,0:T(8,128)}, u32[]{:S(2)}) copy-start(f32[1,4,512,512]{3,2,1,0:T(8,128)} %tiles.5) | copy-start | bytes 12582916
  77.1 6.8 %collective-permute-start.5 = (f32[32,128]{1,0:T(8,128)S(1)}, f32[32,128]{1,0:T(8,128)S(1)}, u32[]{:S(2)}, u32[]{:S(2)}) collective-permute-start(f32[32,128]{1,0:T(8,128)S(1)} %get-tuple-element.34.p0), channel_id=1, source_target_pairs={{0,192},{64,128},{128,64},{192,0},{1,193},{65,129},{129,65},{193,1... | collective-permute-start | bytes 49160 | tf_op jit(solution)/shard_map/ppermute | solution.py:458
  82.5 4.1 %collective-permute-start.4 = (f32[32,128]{1,0:T(8,128)S(1)}, f32[32,128]{1,0:T(8,128)S(1)}, u32[]{:S(2)}, u32[]{:S(2)}) collective-permute-start(f32[32,128]{1,0:T(8,128)S(1)} %get-tuple-element.34.p0), channel_id=1, source_target_pairs={{0,128},{64,192},{128,0},{192,64},{1,129},{65,193},{129,1},{193,65... | collective-permute-start | bytes 49160 | tf_op jit(solution)/shard_map/ppermute | solution.py:458
  83.2 3.4 %collective-permute-start.3 = (f32[32,128]{1,0:T(8,128)S(1)}, f32[32,128]{1,0:T(8,128)S(1)}, u32[]{:S(2)}, u32[]{:S(2)}) collective-permute-start(f32[32,128]{1,0:T(8,128)S(1)} %get-tuple-element.34.p0), channel_id=1, source_target_pairs={{0,64},{64,0},{128,192},{192,128},{1,65},{65,1},{129,193},{193,129... | collective-permute-start | bytes 49160 | tf_op jit(solution)/shard_map/ppermute | solution.py:458
  112.5 5.3 %collective-permute-start.8 = (f32[32,128]{1,0:T(8,128)S(1)}, f32[32,128]{1,0:T(8,128)S(1)}, u32[]{:S(2)}, u32[]{:S(2)}) collective-permute-start(f32[32,128]{1,0:T(8,128)S(1)} %get-tuple-element.47.p0), channel_id=1, source_target_pairs={{0,192},{64,128},{128,64},{192,0},{1,193},{65,129},{129,65},{193,1... | collective-permute-start | bytes 49160 | tf_op jit(solution)/shard_map/ppermute | solution.py:458
  116.3 4.1 %collective-permute-start.7 = (f32[32,128]{1,0:T(8,128)S(1)}, f32[32,128]{1,0:T(8,128)S(1)}, u32[]{:S(2)}, u32[]{:S(2)}) collective-permute-start(f32[32,128]{1,0:T(8,128)S(1)} %get-tuple-element.47.p0), channel_id=1, source_target_pairs={{0,128},{64,192},{128,0},{192,64},{1,129},{65,193},{129,1},{193,65... | collective-permute-start | bytes 49160 | tf_op jit(solution)/shard_map/ppermute | solution.py:458
  117.2 3.2 %collective-permute-start.6 = (f32[32,128]{1,0:T(8,128)S(1)}, f32[32,128]{1,0:T(8,128)S(1)}, u32[]{:S(2)}, u32[]{:S(2)}) collective-permute-start(f32[32,128]{1,0:T(8,128)S(1)} %get-tuple-element.47.p0), channel_id=1, source_target_pairs={{0,64},{64,0},{128,192},{192,128},{1,65},{65,1},{129,193},{193,129... | collective-permute-start | bytes 49160 | tf_op jit(solution)/shard_map/ppermute | solution.py:458

commit v7 on v6

--- a/solution.py
+++ b/solution.py
@@ -151,23 +151,23 @@
     return matches(wanted(got), row_of, NT // 2, 13)
 
 
-def sum_rows(msg, hot, out, n, m, k):
+def sum_rows(msg, hot, out, n, m, k, skip=0):
     blocks = [msg[pl.ds(i, NB, stride=k), :] for i in range(n)]
     blocks += [pltpu.roll(v, 64, 1) for v in blocks]
     got = dot(hot, jnp.concatenate([jnp.concatenate(split(v, 2), axis=1) for v in blocks], axis=0))
     got = got[:, :LANES] + got[:, LANES:]
     left = lane(8) < 64
-    for kk in range(m):
-        out[pl.ds(kk, 8, stride=m), :] = jnp.where(left, got[8 * kk : 8 * kk + 8], got[8 * (m + kk) : 8 * (m + kk) + 8])
-
-
-def receive_rows(msg, rows, m):
+    for kk in range(skip, m):
+        out[pl.ds(kk - skip, 8, stride=m - skip), :] = jnp.where(left, got[8 * kk : 8 * kk + 8], got[8 * (m + kk) : 8 * (m + kk) + 8])
+
+
+def receive_rows(msg, rows, m, first=0):
     low = lane(m) < 64
     for q in range(4):
         a = msg[2 * m * q : 2 * m * q + m, :]
         b = msg[2 * m * q + m : 2 * m * q + 2 * m, :]
-        rows[pl.ds(q, m, stride=8), :] = jnp.where(low, a, pltpu.roll(b, 64, 1))
-        rows[pl.ds(q + 4, m, stride=8), :] = jnp.where(low, pltpu.roll(a, 64, 1), b)
+        rows[pl.ds(first + q, m, stride=8), :] = jnp.where(low, a, pltpu.roll(b, 64, 1))
+        rows[pl.ds(first + q + 4, m, stride=8), :] = jnp.where(low, pltpu.roll(a, 64, 1), b)
 
 
 def bounds(lower, upper, kind, free):
@@ -350,13 +350,16 @@
 
 
 def second_sum_kernel(msg, hot, weight, out):
-    sum_rows(msg, hot[...], out, 5, 13, 6)
+    sum_rows(msg, hot[...], out, 5, 13, 6, 2)
     tail = jnp.sum(msg[pl.ds(5, NB, stride=6), :], axis=0, keepdims=True)
     weight[...] = jnp.broadcast_to(new_weight(jnp.ones((1, 1), F32), tail[:, 1:2], tail[:, 0:1]), (8, LANES))
 
 
 def primal_step(grads, own, read, own_x, read_x, tau, own_out, rows):
-    receive_rows(grads, rows, 13)
+    skip = 13 - grads.shape[0] // 8
+    if skip:
+        rows[0 : 8 * skip] = jnp.zeros((8 * skip, LANES), F32)
+    receive_rows(grads, rows, 13 - skip, 8 * skip)
     c, low, high, kind = own
     x = own_x[...]
     low, high = bounds(low[...], high[...], kind[...], jnp.inf)
@@ -493,7 +496,7 @@
     hess_prod, put = call(hessian_kernel, [ROWS, ((4 * LANES, 2 * LANES), BF16)], read_x, rel, hess)
     y, msg = call(dual_kernel, [wide_block, ((6 * NB, LANES), F32)], *parts, put, take, y, b, kind, hess_prod, cons,
                   scratch=ROWS_SCRATCH)
-    weight, msg = call(second_sum_kernel, [scalar, cube], exchange(msg), hot)
+    weight, msg = call(second_sum_kernel, [scalar, ((8 * 11, LANES), F32)], exchange(msg), hot)
     final, prods = call(second_primal_kernel, [ROWS, PACKED], exchange_in_cube(msg), *own, read, own_x, read_x, weight, cons,
                         scratch=grads)
     parts = over_group(prods)

time: 136 us -> 136 us (level)
  no operation moved by 1% of the time
where the time goes in v7:
time: 136 us
  blocking collectives  88.4 us (65%)
  starting transfers between devices  20.9 us (15%)
  waiting for transfers between devices  10.7 us (8%)
  Pallas kernels  9.97 us (7%)
  local copies, waits for them, and re-layouts  5.01 us (4%)
    all_to_all x4, blocking collectives, exchange(): out = lax.all_to_all(rows.reshape(NB, 1, k * LANES), BLK, 0, 0, tiled=True)  74.3 us
    ppermute x9, starting transfers between devices, over_group(): parts.append(lax.ppermute(rows, GRP, [(i, i ^ k) for i in range(4)]))  15.8 us
    all_to_all x2, blocking collectives, exchange_in_cube(): lax.all_to_all(rows.reshape(8, 1, k * LANES), CUBE, 0, 0, tiled=True)  14.1 us
    ppermute x9, waiting for transfers between devices, over_group(): parts.append(lax.ppermute(rows, GRP, [(i, i ^ k) for i in range(4)]))  10.6 us
    pallas_call x11, Pallas kernels, call(): pl.pallas_call(kernel, out_shape=shapes, in_specs=[s] * smem + [w] * (len...  9.97 us
    all_to_all x1, starting transfers between devices, exchange(): out = lax.all_to_all(rows.reshape(NB, 1, k * LANES), BLK, 0, 0, tiled=True)  5.08 us
    unnamed x22, local copies, waits for them, and re-layouts  5.01 us
  transfers between devices with their start and end apart: 10, of which 7 were waited for; matrix products, arithmetic and copies ran while one was open for 0% of the time, Pallas kernels for 0%

profile of v7, /device:TPU:1, one launch (start us, length us, event | category | flops | bytes accessed | tf_op | source)
XLA Modules:
  0.0 135.8 jit_solution(8133807108877629429)
XLA Ops:
  0.6 1.8 %shard_map.148 = (f32[320,128]{1,0:T(8,128)}, f32[136,128]{1,0:T(8,128)}) custom-call(s32[1]{0:T(128)} %bitcast.me, s32[2,4]{1,0:T(2,128)} %bitcast.62, s32[1,6]{1,0:T(1,128)} %k_cols.1, s32[1,6]{1,0:T(1,128)} %k_rows.1, f32[64,128]{1,0:T(8,128)} %bitcast.44, f32[64,128]{1,0:T(8,128)} %bitcast.46, f32[64,128]{1,0:T(8,128)} %bitcast.49, f32[64,128]{1,0:T(8,128)} %bitcast.52, ...), custom_call_target="tpu_custom_call" | custom-call | flops 10000000000 | bytes 10000000 | tf_op jit(solution)/shard_map/pallas_call | solution.py:430
  2.5 23.5 %all_to_all.35 = f32[64,1,640]{2,1,0:T(1,128)S(1)} all-to-all(f32[64,1,640]{2,1,0:T(1,128)} %bitcast.58), channel_id=1, replica_groups=mesh['grp_0'=2,'grp_1'=2,'zh'=4,'zl'=2,'xh'=2,'xl'=2,'yl'=2] {'zh','zl',..., dimensions={0} | all-to-all | bytes 327680 | tf_op jit(solution)/shard_map/all_to_all | solution.py:449
  26.0 1.8 %shard_map.149 = f32[192,128]{1,0:T(8,128)} custom-call(f32[320,128]{1,0:T(8,128)S(1)} %bitcast.31), custom_call_target="tpu_custom_call" | custom-call | flops 10000000000 | bytes 10000000 | tf_op jit(solution)/shard_map/pallas_call | solution.py:430
  27.8 5.1 %all-to-all-start.1 = ((f32[64,1,384]{2,1,0:T(1,128)}), f32[64,1,384]{2,1,0:T(1,128)S(1)}, u32[]{:S(2)}, u32[]{:S(2)}) async-start(f32[64,1,384]{2,1,0:T(1,128)} %bitcast.12), calls=%async_computation.1 | async-start | bytes 196608 | tf_op jit(solution)/shard_map/all_to_all | solution.py:449
  32.9 4.5 %collective-permute-start.2 = (f32[136,128]{1,0:T(8,128)S(1)}, f32[136,128]{1,0:T(8,128)S(1)}, u32[]{:S(2)}, u32[]{:S(2)}) collective-permute-start(f32[136,128]{1,0:T(8,128)S(1)} %copy-done.3), channel_id=1, source_target_pairs={{0,192},{64,128},{128,64},{192,0},{1,193},{65,129},{129,65},{193,1... | collective-permute-start | bytes 208904 | tf_op jit(solution)/shard_map/ppermute | solution.py:461
  37.3 0.4 collective-permute-start.1
  37.7 0.1 collective-permute-start
  37.8 2.6 %collective-permute-done.2.p3 = f32[136,128]{1,0:T(8,128)S(1)} collective-permute-done((f32[136,128]{1,0:T(8,128)S(1)}, f32[136,128]{1,0:T(8,128)S(1)}, u32[]{:S(2)}, u32[]{:S(2)}) %collective-permute-start.2) | collective-permute-done | bytes 69664 | tf_op jit(solution)/shard_map/ppermute | solution.py:461
  40.5 2.0 %collective-permute-done.1.p2 = f32[136,128]{1,0:T(8,128)S(1)} collective-permute-done((f32[136,128]{1,0:T(8,128)S(1)}, f32[136,128]{1,0:T(8,128)S(1)}, u32[]{:S(2)}, u32[]{:S(2)}) %collective-permute-start.1) | collective-permute-done | bytes 69664 | tf_op jit(solution)/shard_map/ppermute | solution.py:461
  42.6 2.8 %copy-done = f32[1,6,512,512]{3,2,1,0:T(8,128)S(1)} copy-done((f32[1,6,512,512]{3,2,1,0:T(8,128)S(1)}, f32[1,6,512,512]{3,2,1,0:T(8,128)}, u32[]{:S(2)}) %copy-start) | copy-done | bytes 6291480
  45.4 2.2 %copy-done.1 = f32[1,4,512,512]{3,2,1,0:T(8,128)S(1)} copy-done((f32[1,4,512,512]{3,2,1,0:T(8,128)S(1)}, f32[1,4,512,512]{3,2,1,0:T(8,128)}, u32[]{:S(2)}) %copy-start.1) | copy-done | bytes 4194328
  47.6 1.4 shard_map.150
  48.9 20.1 %all_to_all.36 = f32[64,1,640]{2,1,0:T(1,128)S(1)} all-to-all(f32[64,1,640]{2,1,0:T(1,128)S(1)} %bitcast.33), channel_id=1, replica_groups=mesh['grp_0'=2,'grp_1'=2,'zh'=4,'zl'=2,'xh'=2,'xl'=2,'yl'=2] {'zh','zl',..., dimensions={0} | all-to-all | bytes 327680 | tf_op jit(solution)/shard_map/all_to_all | solution.py:449
  69.1 0.3 shard_map.151
  69.4 7.0 %all_to_all.37 = f32[8,1,1664]{2,1,0:T(1,128)S(1)} all-to-all(f32[8,1,1664]{2,1,0:T(1,128)S(1)} %bitcast.37), channel_id=1, replica_groups=mesh['grp_0'=2,'grp_1'=2,'zh'=4,'zl'=2,'xh'=2,'xl'=2,'yl'=2] {'zl','xl',..., dimensions={0} | all-to-all | bytes 106496 | tf_op jit(solution)/shard_map/all_to_all | solution.py:455
  76.5 0.7 shard_map.152
  77.1 5.4 %collective-permute-start.5 = (f32[32,128]{1,0:T(8,128)S(1)}, f32[32,128]{1,0:T(8,128)S(1)}, u32[]{:S(2)}, u32[]{:S(2)}) collective-permute-start(f32[32,128]{1,0:T(8,128)S(1)} %get-tuple-element.34.p0), channel_id=1, source_target_pairs={{0,192},{64,128},{128,64},{192,0},{1,193},{65,129},{129,65},{193,1... | collective-permute-start | bytes 49160 | tf_op jit(solution)/shard_map/ppermute | solution.py:461
  82.5 0.7 collective-permute-start.4
  83.3 0.6 shard_map.153
  83.9 2.7 %collective-permute-done.4.p2 = f32[32,128]{1,0:T(8,128)S(1)} collective-permute-done((f32[32,128]{1,0:T(8,128)S(1)}, f32[32,128]{1,0:T(8,128)S(1)}, u32[]{:S(2)}, u32[]{:S(2)}) %collective-permute-start.4) | collective-permute-done | bytes 16416 | tf_op jit(solution)/shard_map/ppermute | solution.py:461
  86.6 1.4 %shard_map.154 = (f32[64,256]{1,0:T(8,128)S(1)}, f32[384,128]{1,0:T(8,128)S(1)}) custom-call(f32[32,128]{1,0:T(8,128)S(1)} %get-tuple-element.34.p0, f32[32,128]{1,0:T(8,128)S(1)} %collective-permute-done.3.p1, f32[32,128]{1,0:T(8,128)S(1)} %collective-permute-done.4.p2, f32[32,128]{1,0:T(8,128)S(1)} %collective-permute-done.5.p3, ...), custom_call_target="tpu_custom_call" | custom-call | flops 10000000000 | bytes 10000000 | tf_op jit(solution)/shard_map/pallas_call | solution.py:430
  88.0 16.3 %all_to_all.38 = f32[64,1,768]{2,1,0:T(1,128)S(1)} all-to-all(f32[64,1,768]{2,1,0:T(1,128)S(1)} %bitcast.29), channel_id=1, replica_groups=mesh['grp_0'=2,'grp_1'=2,'zh'=4,'zl'=2,'xh'=2,'xl'=2,'yl'=2] {'zh','zl',..., dimensions={0} | all-to-all | bytes 393216 | tf_op jit(solution)/shard_map/all_to_all | solution.py:449
  104.4 0.3 shard_map.155
  104.7 7.1 %all_to_all.39 = f32[8,1,1408]{2,1,0:T(1,128)S(1)} all-to-all(f32[8,1,1408]{2,1,0:T(1,128)S(1)} %bitcast.39), channel_id=1, replica_groups=mesh['grp_0'=2,'grp_1'=2,'zh'=4,'zl'=2,'xh'=2,'xl'=2,'yl'=2] {'zl','xl',..., dimensions={0} | all-to-all | bytes 90112 | tf_op jit(solution)/shard_map/all_to_all | solution.py:455
  111.8 0.7 shard_map.156
  112.5 3.8 %collective-permute-start.8 = (f32[32,128]{1,0:T(8,128)S(1)}, f32[32,128]{1,0:T(8,128)S(1)}, u32[]{:S(2)}, u32[]{:S(2)}) collective-permute-start(f32[32,128]{1,0:T(8,128)S(1)} %get-tuple-element.47.p0), channel_id=1, source_target_pairs={{0,192},{64,128},{128,64},{192,0},{1,193},{65,129},{129,65},{193,1... | collective-permute-start | bytes 49160 | tf_op jit(solution)/shard_map/ppermute | solution.py:461
  116.3 0.9 collective-permute-start.7
  117.2 0.5 collective-permute-done.8.p3
  117.7 2.7 %collective-permute-done.7.p2 = f32[32,128]{1,0:T(8,128)S(1)} collective-permute-done((f32[32,128]{1,0:T(8,128)S(1)}, f32[32,128]{1,0:T(8,128)S(1)}, u32[]{:S(2)}, u32[]{:S(2)}) %collective-permute-start.7) | collective-permute-done | bytes 16416 | tf_op jit(solution)/shard_map/ppermute | solution.py:461
  120.4 0.3 shard_map.157
  120.7 14.3 %all_to_all.40 = f32[64,1,128]{2,1,0:T(1,128)S(1)} all-to-all(f32[64,1,128]{2,1,0:T(1,128)S(1)} %bitcast.40), channel_id=1, replica_groups=mesh['grp_0'=2,'grp_1'=2,'zh'=4,'zl'=2,'xh'=2,'xl'=2,'yl'=2] {'zh','zl',..., dimensions={0} | all-to-all | bytes 65536 | tf_op jit(solution)/shard_map/all_to_all | solution.py:449
  135.0 0.8 shard_map.158
  (28 shorter events, 0.3 us)
Async XLA Ops:
  26.0 6.9 %copy-start.3 = (f32[136,128]{1,0:T(8,128)S(1)}, f32[136,128]{1,0:T(8,128)}, u32[]{:S(2)}) copy-start(f32[136,128]{1,0:T(8,128)} %get-tuple-element.30.p0) | copy-start | bytes 208900
  27.8 14.8 %all-to-all-start.1 = ((f32[64,1,384]{2,1,0:T(1,128)}), f32[64,1,384]{2,1,0:T(1,128)S(1)}, u32[]{:S(2)}, u32[]{:S(2)}) async-start(f32[64,1,384]{2,1,0:T(1,128)} %bitcast.12), calls=%async_computation.1 | async-start | bytes 196608 | tf_op jit(solution)/shard_map/all_to_all | solution.py:449
  32.9 7.6 %collective-permute-start.2 = (f32[136,128]{1,0:T(8,128)S(1)}, f32[136,128]{1,0:T(8,128)S(1)}, u32[]{:S(2)}, u32[]{:S(2)}) collective-permute-start(f32[136,128]{1,0:T(8,128)S(1)} %copy-done.3), channel_id=1, source_target_pairs={{0,192},{64,128},{128,64},{192,0},{1,193},{65,129},{129,65},{193,1... | collective-permute-start | bytes 208904 | tf_op jit(solution)/shard_map/ppermute | solution.py:461
  37.3 5.1 %collective-permute-start.1 = (f32[136,128]{1,0:T(8,128)S(1)}, f32[136,128]{1,0:T(8,128)S(1)}, u32[]{:S(2)}, u32[]{:S(2)}) collective-permute-start(f32[136,128]{1,0:T(8,128)S(1)} %copy-done.3), channel_id=1, source_target_pairs={{0,128},{64,192},{128,0},{192,64},{1,129},{65,193},{129,1},{193,65... | collective-permute-start | bytes 208904 | tf_op jit(solution)/shard_map/ppermute | solution.py:461
  37.7 4.8 %collective-permute-start = (f32[136,128]{1,0:T(8,128)S(1)}, f32[136,128]{1,0:T(8,128)S(1)}, u32[]{:S(2)}, u32[]{:S(2)}) collective-permute-start(f32[136,128]{1,0:T(8,128)S(1)} %copy-done.3), channel_id=1, source_target_pairs={{0,64},{64,0},{128,192},{192,128},{1,65},{65,1},{129,193},{193,129... | collective-permute-start | bytes 208904 | tf_op jit(solution)/shard_map/ppermute | solution.py:461
  42.6 2.8 %copy-start = (f32[1,6,512,512]{3,2,1,0:T(8,128)S(1)}, f32[1,6,512,512]{3,2,1,0:T(8,128)}, u32[]{:S(2)}) copy-start(f32[1,6,512,512]{3,2,1,0:T(8,128)} %tiles.7) | copy-start | bytes 18874372
  45.4 2.2 %copy-start.1 = (f32[1,4,512,512]{3,2,1,0:T(8,128)S(1)}, f32[1,4,512,512]{3,2,1,0:T(8,128)}, u32[]{:S(2)}) copy-start(f32[1,4,512,512]{3,2,1,0:T(8,128)} %tiles.5) | copy-start | bytes 12582916
  47.6 28.9 %slice-start = ((s8[6291456]{0:T(1024)(128)(4,1)}), s8[2097152]{0:T(1024)(128)(4,1)S(1)}, s32[]{:S(2)}) async-start(s8[6291456]{0:T(1024)(128)(4,1)} %bitcast.42), calls=%async_computation.7 | async-start | bytes 4194304
  48.9 27.5 %slice-start.1 = ((s8[6291456]{0:T(1024)(128)(4,1)}), s8[4194304]{0:T(1024)(128)(4,1)S(1)}, s32[]{:S(2)}) async-start(s8[6291456]{0:T(1024)(128)(4,1)} %bitcast.42), calls=%async_computation.8 | async-start | bytes 8388608
  69.1 7.3 %copy-start.4 = (f32[8192]{0:T(1024)S(1)}, f32[8192]{0:T(1024)}, u32[]{:S(2)}) copy-start(f32[8192]{0:T(1024)} %param.13) | copy-start | bytes 98308
  69.1 7.4 %copy-start.5 = (f32[8192]{0:T(1024)S(1)}, f32[8192]{0:T(1024)}, u32[]{:S(2)}) copy-start(f32[8192]{0:T(1024)} %param.15) | copy-start | bytes 98308
  69.1 7.4 %copy-start.6 = (f32[8192]{0:T(1024)S(1)}, f32[8192]{0:T(1024)}, u32[]{:S(2)}) copy-start(f32[8192]{0:T(1024)} %param.16) | copy-start | bytes 98308
  69.1 7.4 %copy-start.7 = (f32[8192]{0:T(1024)S(1)}, f32[8192]{0:T(1024)}, u32[]{:S(2)}) copy-start(f32[8192]{0:T(1024)} %param.17) | copy-start | bytes 98308
  69.1 7.4 %copy-start.8 = (s32[8192]{0:T(1024)S(1)}, s32[8192]{0:T(1024)}, u32[]{:S(2)}) copy-start(s32[8192]{0:T(1024)} %param.18) | copy-start | bytes 98308
  76.5 6.8 %copy-start.2 = (f32[1,4,512,512]{3,2,1,0:T(8,128)S(1)}, f32[1,4,512,512]{3,2,1,0:T(8,128)}, u32[]{:S(2)}) copy-start(f32[1,4,512,512]{3,2,1,0:T(8,128)} %tiles.5) | copy-start | bytes 12582916
  77.1 6.8 %collective-permute-start.5 = (f32[32,128]{1,0:T(8,128)S(1)}, f32[32,128]{1,0:T(8,128)S(1)}, u32[]{:S(2)}, u32[]{:S(2)}) collective-permute-start(f32[32,128]{1,0:T(8,128)S(1)} %get-tuple-element.34.p0), channel_id=1, source_target_pairs={{0,192},{64,128},{128,64},{192,0},{1,193},{65,129},{129,65},{193,1... | collective-permute-start | bytes 49160 | tf_op jit(solution)/shard_map/ppermute | solution.py:461
  82.5 4.1 %collective-permute-start.4 = (f32[32,128]{1,0:T(8,128)S(1)}, f32[32,128]{1,0:T(8,128)S(1)}, u32[]{:S(2)}, u32[]{:S(2)}) collective-permute-start(f32[32,128]{1,0:T(8,128)S(1)} %get-tuple-element.34.p0), channel_id=1, source_target_pairs={{0,128},{64,192},{128,0},{192,64},{1,129},{65,193},{129,1},{193,65... | collective-permute-start | bytes 49160 | tf_op jit(solution)/shard_map/ppermute | solution.py:461
  83.2 3.4 %collective-permute-start.3 = (f32[32,128]{1,0:T(8,128)S(1)}, f32[32,128]{1,0:T(8,128)S(1)}, u32[]{:S(2)}, u32[]{:S(2)}) collective-permute-start(f32[32,128]{1,0:T(8,128)S(1)} %get-tuple-element.34.p0), channel_id=1, source_target_pairs={{0,64},{64,0},{128,192},{192,128},{1,65},{65,1},{129,193},{193,129... | collective-permute-start | bytes 49160 | tf_op jit(solution)/shard_map/ppermute | solution.py:461
  112.5 5.3 %collective-permute-start.8 = (f32[32,128]{1,0:T(8,128)S(1)}, f32[32,128]{1,0:T(8,128)S(1)}, u32[]{:S(2)}, u32[]{:S(2)}) collective-permute-start(f32[32,128]{1,0:T(8,128)S(1)} %get-tuple-element.47.p0), channel_id=1, source_target_pairs={{0,192},{64,128},{128,64},{192,0},{1,193},{65,129},{129,65},{193,1... | collective-permute-start | bytes 49160 | tf_op jit(solution)/shard_map/ppermute | solution.py:461
  116.3 4.1 %collective-permute-start.7 = (f32[32,128]{1,0:T(8,128)S(1)}, f32[32,128]{1,0:T(8,128)S(1)}, u32[]{:S(2)}, u32[]{:S(2)}) collective-permute-start(f32[32,128]{1,0:T(8,128)S(1)} %get-tuple-element.47.p0), channel_id=1, source_target_pairs={{0,128},{64,192},{128,0},{192,64},{1,129},{65,193},{129,1},{193,65... | collective-permute-start | bytes 49160 | tf_op jit(solution)/shard_map/ppermute | solution.py:461
  117.2 3.2 %collective-permute-start.6 = (f32[32,128]{1,0:T(8,128)S(1)}, f32[32,128]{1,0:T(8,128)S(1)}, u32[]{:S(2)}, u32[]{:S(2)}) collective-permute-start(f32[32,128]{1,0:T(8,128)S(1)} %get-tuple-element.47.p0), channel_id=1, source_target_pairs={{0,64},{64,0},{128,192},{192,128},{1,65},{65,1},{129,193},{193,129... | collective-permute-start | bytes 49160 | tf_op jit(solution)/shard_map/ppermute | solution.py:461

commit v8 on v6

--- a/solution.py
+++ b/solution.py
@@ -259,14 +259,16 @@
     refs = (q_index, k_cols, k_rows, primal, objective, lower, upper, bound_kind, dual, rhs, row_kind)
     sems = scratch[-1]
     copies = [pltpu.make_async_copy(r, s, sems.at[i]) for i, (r, s) in enumerate(zip(refs, scratch))]
-    for c in copies:
-        c.start()
+    for i in (3, 4, 5, 6, 7, 8, 9, 10, 0, 1, 2):
+        copies[i].start()
     qi, kc, kr, p, ob, lo, up, bk, du, rh, rk = scratch[:-1]
-    for c in copies:
-        c.wait()
+    for i in (3, 4, 5, 6, 7):
+        copies[i].wait()
     low, high = bounds(lo[...], up[...], bk[...], FREE)
     for k, v in enumerate((*spread_two(p[...], ob[...]), *spread_two(low, high))):
         out[pl.ds(k, NB, stride=FIRST), :] = v
+    for i in (0, 1, 2, 8, 9, 10):
+        copies[i].wait()
     ln = lane(8)
     ids = jnp.zeros((8, LANES), F32)
     for j in range(NQ):

time: 136 us -> 136 us (level)
  no operation moved by 1% of the time
where the time goes in v8:
time: 136 us
  blocking collectives  88.4 us (65%)
  starting transfers between devices  20.9 us (15%)
  waiting for transfers between devices  10.7 us (8%)
  Pallas kernels  10.1 us (7%)
  local copies, waits for them, and re-layouts  5.01 us (4%)
    all_to_all x4, blocking collectives, exchange(): out = lax.all_to_all(rows.reshape(NB, 1, k * LANES), BLK, 0, 0, tiled=True)  74.3 us
    ppermute x9, starting transfers between devices, over_group(): parts.append(lax.ppermute(rows, GRP, [(i, i ^ k) for i in range(4)]))  15.8 us
    all_to_all x2, blocking collectives, exchange_in_cube(): lax.all_to_all(rows.reshape(8, 1, k * LANES), CUBE, 0, 0, tiled=True)  14.2 us
    ppermute x9, waiting for transfers between devices, over_group(): parts.append(lax.ppermute(rows, GRP, [(i, i ^ k) for i in range(4)]))  10.6 us
    pallas_call x11, Pallas kernels, call(): pl.pallas_call(kernel, out_shape=shapes, in_specs=[s] * smem + [w] * (len...  10.1 us
    all_to_all x1, starting transfers between devices, exchange(): out = lax.all_to_all(rows.reshape(NB, 1, k * LANES), BLK, 0, 0, tiled=True)  5.08 us
    unnamed x22, local copies, waits for them, and re-layouts  5.01 us
  transfers between devices with their start and end apart: 10, of which 7 were waited for; matrix products, arithmetic and copies ran while one was open for 0% of the time, Pallas kernels for 0%

profile of v8, /device:TPU:1, one launch (start us, length us, event | category | flops | bytes accessed | tf_op | source)
XLA Modules:
  0.0 135.9 jit_solution(8274381673581726831)
XLA Ops:
  0.6 1.9 %shard_map.148 = (f32[320,128]{1,0:T(8,128)}, f32[136,128]{1,0:T(8,128)}) custom-call(s32[1]{0:T(128)} %bitcast.me, s32[2,4]{1,0:T(2,128)} %bitcast.62, s32[1,6]{1,0:T(1,128)} %k_cols.1, s32[1,6]{1,0:T(1,128)} %k_rows.1, f32[64,128]{1,0:T(8,128)} %bitcast.44, f32[64,128]{1,0:T(8,128)} %bitcast.46, f32[64,128]{1,0:T(8,128)} %bitcast.49, f32[64,128]{1,0:T(8,128)} %bitcast.52, ...), custom_call_target="tpu_custom_call" | custom-call | flops 10000000000 | bytes 10000000 | tf_op jit(solution)/shard_map/pallas_call | solution.py:429
  2.6 23.5 %all_to_all.35 = f32[64,1,640]{2,1,0:T(1,128)S(1)} all-to-all(f32[64,1,640]{2,1,0:T(1,128)} %bitcast.58), channel_id=1, replica_groups=mesh['grp_0'=2,'grp_1'=2,'zh'=4,'zl'=2,'xh'=2,'xl'=2,'yl'=2] {'zh','zl',..., dimensions={0} | all-to-all | bytes 327680 | tf_op jit(solution)/shard_map/all_to_all | solution.py:448
  26.1 1.8 %shard_map.149 = f32[192,128]{1,0:T(8,128)} custom-call(f32[320,128]{1,0:T(8,128)S(1)} %bitcast.31), custom_call_target="tpu_custom_call" | custom-call | flops 10000000000 | bytes 10000000 | tf_op jit(solution)/shard_map/pallas_call | solution.py:429
  27.9 5.1 %all-to-all-start.1 = ((f32[64,1,384]{2,1,0:T(1,128)}), f32[64,1,384]{2,1,0:T(1,128)S(1)}, u32[]{:S(2)}, u32[]{:S(2)}) async-start(f32[64,1,384]{2,1,0:T(1,128)} %bitcast.12), calls=%async_computation.1 | async-start | bytes 196608 | tf_op jit(solution)/shard_map/all_to_all | solution.py:448
  33.0 4.5 %collective-permute-start.2 = (f32[136,128]{1,0:T(8,128)S(1)}, f32[136,128]{1,0:T(8,128)S(1)}, u32[]{:S(2)}, u32[]{:S(2)}) collective-permute-start(f32[136,128]{1,0:T(8,128)S(1)} %copy-done.3), channel_id=1, source_target_pairs={{0,192},{64,128},{128,64},{192,0},{1,193},{65,129},{129,65},{193,1... | collective-permute-start | bytes 208904 | tf_op jit(solution)/shard_map/ppermute | solution.py:460
  37.4 0.3 collective-permute-start.1
  37.8 0.1 collective-permute-start
  37.9 2.6 %collective-permute-done.2.p3 = f32[136,128]{1,0:T(8,128)S(1)} collective-permute-done((f32[136,128]{1,0:T(8,128)S(1)}, f32[136,128]{1,0:T(8,128)S(1)}, u32[]{:S(2)}, u32[]{:S(2)}) %collective-permute-start.2) | collective-permute-done | bytes 69664 | tf_op jit(solution)/shard_map/ppermute | solution.py:460
  40.6 2.0 %collective-permute-done.1.p2 = f32[136,128]{1,0:T(8,128)S(1)} collective-permute-done((f32[136,128]{1,0:T(8,128)S(1)}, f32[136,128]{1,0:T(8,128)S(1)}, u32[]{:S(2)}, u32[]{:S(2)}) %collective-permute-start.1) | collective-permute-done | bytes 69664 | tf_op jit(solution)/shard_map/ppermute | solution.py:460
  42.7 2.8 %copy-done = f32[1,6,512,512]{3,2,1,0:T(8,128)S(1)} copy-done((f32[1,6,512,512]{3,2,1,0:T(8,128)S(1)}, f32[1,6,512,512]{3,2,1,0:T(8,128)}, u32[]{:S(2)}) %copy-start) | copy-done | bytes 6291480
  45.5 2.2 %copy-done.1 = f32[1,4,512,512]{3,2,1,0:T(8,128)S(1)} copy-done((f32[1,4,512,512]{3,2,1,0:T(8,128)S(1)}, f32[1,4,512,512]{3,2,1,0:T(8,128)}, u32[]{:S(2)}) %copy-start.1) | copy-done | bytes 4194328
  47.7 1.4 shard_map.150
  49.0 20.1 %all_to_all.36 = f32[64,1,640]{2,1,0:T(1,128)S(1)} all-to-all(f32[64,1,640]{2,1,0:T(1,128)S(1)} %bitcast.33), channel_id=1, replica_groups=mesh['grp_0'=2,'grp_1'=2,'zh'=4,'zl'=2,'xh'=2,'xl'=2,'yl'=2] {'zh','zl',..., dimensions={0} | all-to-all | bytes 327680 | tf_op jit(solution)/shard_map/all_to_all | solution.py:448
  69.2 0.3 shard_map.151
  69.5 7.0 %all_to_all.37 = f32[8,1,1664]{2,1,0:T(1,128)S(1)} all-to-all(f32[8,1,1664]{2,1,0:T(1,128)S(1)} %bitcast.39), channel_id=1, replica_groups=mesh['grp_0'=2,'grp_1'=2,'zh'=4,'zl'=2,'xh'=2,'xl'=2,'yl'=2] {'zl','xl',..., dimensions={0} | all-to-all | bytes 106496 | tf_op jit(solution)/shard_map/all_to_all | solution.py:454
  76.6 0.7 shard_map.152
  77.2 5.4 %collective-permute-start.5 = (f32[32,128]{1,0:T(8,128)S(1)}, f32[32,128]{1,0:T(8,128)S(1)}, u32[]{:S(2)}, u32[]{:S(2)}) collective-permute-start(f32[32,128]{1,0:T(8,128)S(1)} %get-tuple-element.34.p0), channel_id=1, source_target_pairs={{0,192},{64,128},{128,64},{192,0},{1,193},{65,129},{129,65},{193,1... | collective-permute-start | bytes 49160 | tf_op jit(solution)/shard_map/ppermute | solution.py:460
  82.6 0.7 collective-permute-start.4
  83.3 0.6 shard_map.153
  84.0 2.7 %collective-permute-done.4.p2 = f32[32,128]{1,0:T(8,128)S(1)} collective-permute-done((f32[32,128]{1,0:T(8,128)S(1)}, f32[32,128]{1,0:T(8,128)S(1)}, u32[]{:S(2)}, u32[]{:S(2)}) %collective-permute-start.4) | collective-permute-done | bytes 16416 | tf_op jit(solution)/shard_map/ppermute | solution.py:460
  86.7 1.4 %shard_map.154 = (f32[64,256]{1,0:T(8,128)S(1)}, f32[384,128]{1,0:T(8,128)S(1)}) custom-call(f32[32,128]{1,0:T(8,128)S(1)} %get-tuple-element.34.p0, f32[32,128]{1,0:T(8,128)S(1)} %collective-permute-done.3.p1, f32[32,128]{1,0:T(8,128)S(1)} %collective-permute-done.4.p2, f32[32,128]{1,0:T(8,128)S(1)} %collective-permute-done.5.p3, ...), custom_call_target="tpu_custom_call" | custom-call | flops 10000000000 | bytes 10000000 | tf_op jit(solution)/shard_map/pallas_call | solution.py:429
  88.1 16.3 %all_to_all.38 = f32[64,1,768]{2,1,0:T(1,128)S(1)} all-to-all(f32[64,1,768]{2,1,0:T(1,128)S(1)} %bitcast.29), channel_id=1, replica_groups=mesh['grp_0'=2,'grp_1'=2,'zh'=4,'zl'=2,'xh'=2,'xl'=2,'yl'=2] {'zh','zl',..., dimensions={0} | all-to-all | bytes 393216 | tf_op jit(solution)/shard_map/all_to_all | solution.py:448
  104.4 0.3 shard_map.155
  104.8 7.2 %all_to_all.39 = f32[8,1,1664]{2,1,0:T(1,128)S(1)} all-to-all(f32[8,1,1664]{2,1,0:T(1,128)S(1)} %bitcast.38), channel_id=1, replica_groups=mesh['grp_0'=2,'grp_1'=2,'zh'=4,'zl'=2,'xh'=2,'xl'=2,'yl'=2] {'zl','xl',..., dimensions={0} | all-to-all | bytes 106496 | tf_op jit(solution)/shard_map/all_to_all | solution.py:454
  111.9 0.7 shard_map.156
  112.6 3.8 %collective-permute-start.8 = (f32[32,128]{1,0:T(8,128)S(1)}, f32[32,128]{1,0:T(8,128)S(1)}, u32[]{:S(2)}, u32[]{:S(2)}) collective-permute-start(f32[32,128]{1,0:T(8,128)S(1)} %get-tuple-element.47.p0), channel_id=1, source_target_pairs={{0,192},{64,128},{128,64},{192,0},{1,193},{65,129},{129,65},{193,1... | collective-permute-start | bytes 49160 | tf_op jit(solution)/shard_map/ppermute | solution.py:460
  116.4 0.9 collective-permute-start.7
  117.3 0.5 collective-permute-done.8.p3
  117.8 2.7 %collective-permute-done.7.p2 = f32[32,128]{1,0:T(8,128)S(1)} collective-permute-done((f32[32,128]{1,0:T(8,128)S(1)}, f32[32,128]{1,0:T(8,128)S(1)}, u32[]{:S(2)}, u32[]{:S(2)}) %collective-permute-start.7) | collective-permute-done | bytes 16416 | tf_op jit(solution)/shard_map/ppermute | solution.py:460
  120.5 0.3 shard_map.157
  120.8 14.3 %all_to_all.40 = f32[64,1,128]{2,1,0:T(1,128)S(1)} all-to-all(f32[64,1,128]{2,1,0:T(1,128)S(1)} %bitcast.40), channel_id=1, replica_groups=mesh['grp_0'=2,'grp_1'=2,'zh'=4,'zl'=2,'xh'=2,'xl'=2,'yl'=2] {'zh','zl',..., dimensions={0} | all-to-all | bytes 65536 | tf_op jit(solution)/shard_map/all_to_all | solution.py:448
  135.2 0.8 shard_map.158
  (28 shorter events, 0.3 us)
Async XLA Ops:
  26.1 6.9 %copy-start.3 = (f32[136,128]{1,0:T(8,128)S(1)}, f32[136,128]{1,0:T(8,128)}, u32[]{:S(2)}) copy-start(f32[136,128]{1,0:T(8,128)} %get-tuple-element.30.p0) | copy-start | bytes 208900
  27.9 14.8 %all-to-all-start.1 = ((f32[64,1,384]{2,1,0:T(1,128)}), f32[64,1,384]{2,1,0:T(1,128)S(1)}, u32[]{:S(2)}, u32[]{:S(2)}) async-start(f32[64,1,384]{2,1,0:T(1,128)} %bitcast.12), calls=%async_computation.1 | async-start | bytes 196608 | tf_op jit(solution)/shard_map/all_to_all | solution.py:448
  33.0 7.6 %collective-permute-start.2 = (f32[136,128]{1,0:T(8,128)S(1)}, f32[136,128]{1,0:T(8,128)S(1)}, u32[]{:S(2)}, u32[]{:S(2)}) collective-permute-start(f32[136,128]{1,0:T(8,128)S(1)} %copy-done.3), channel_id=1, source_target_pairs={{0,192},{64,128},{128,64},{192,0},{1,193},{65,129},{129,65},{193,1... | collective-permute-start | bytes 208904 | tf_op jit(solution)/shard_map/ppermute | solution.py:460
  37.4 5.1 %collective-permute-start.1 = (f32[136,128]{1,0:T(8,128)S(1)}, f32[136,128]{1,0:T(8,128)S(1)}, u32[]{:S(2)}, u32[]{:S(2)}) collective-permute-start(f32[136,128]{1,0:T(8,128)S(1)} %copy-done.3), channel_id=1, source_target_pairs={{0,128},{64,192},{128,0},{192,64},{1,129},{65,193},{129,1},{193,65... | collective-permute-start | bytes 208904 | tf_op jit(solution)/shard_map/ppermute | solution.py:460
  37.8 4.8 %collective-permute-start = (f32[136,128]{1,0:T(8,128)S(1)}, f32[136,128]{1,0:T(8,128)S(1)}, u32[]{:S(2)}, u32[]{:S(2)}) collective-permute-start(f32[136,128]{1,0:T(8,128)S(1)} %copy-done.3), channel_id=1, source_target_pairs={{0,64},{64,0},{128,192},{192,128},{1,65},{65,1},{129,193},{193,129... | collective-permute-start | bytes 208904 | tf_op jit(solution)/shard_map/ppermute | solution.py:460
  42.7 2.8 %copy-start = (f32[1,6,512,512]{3,2,1,0:T(8,128)S(1)}, f32[1,6,512,512]{3,2,1,0:T(8,128)}, u32[]{:S(2)}) copy-start(f32[1,6,512,512]{3,2,1,0:T(8,128)} %tiles.7) | copy-start | bytes 18874372
  45.5 2.2 %copy-start.1 = (f32[1,4,512,512]{3,2,1,0:T(8,128)S(1)}, f32[1,4,512,512]{3,2,1,0:T(8,128)}, u32[]{:S(2)}) copy-start(f32[1,4,512,512]{3,2,1,0:T(8,128)} %tiles.5) | copy-start | bytes 12582916
  47.6 28.9 %slice-start = ((s8[6291456]{0:T(1024)(128)(4,1)}), s8[2097152]{0:T(1024)(128)(4,1)S(1)}, s32[]{:S(2)}) async-start(s8[6291456]{0:T(1024)(128)(4,1)} %bitcast.42), calls=%async_computation.7 | async-start | bytes 4194304
  49.0 27.5 %slice-start.1 = ((s8[6291456]{0:T(1024)(128)(4,1)}), s8[4194304]{0:T(1024)(128)(4,1)S(1)}, s32[]{:S(2)}) async-start(s8[6291456]{0:T(1024)(128)(4,1)} %bitcast.42), calls=%async_computation.8 | async-start | bytes 8388608
  69.2 7.3 %copy-start.4 = (f32[8192]{0:T(1024)S(1)}, f32[8192]{0:T(1024)}, u32[]{:S(2)}) copy-start(f32[8192]{0:T(1024)} %param.13) | copy-start | bytes 98308
  69.2 7.4 %copy-start.5 = (f32[8192]{0:T(1024)S(1)}, f32[8192]{0:T(1024)}, u32[]{:S(2)}) copy-start(f32[8192]{0:T(1024)} %param.15) | copy-start | bytes 98308
  69.2 7.4 %copy-start.6 = (f32[8192]{0:T(1024)S(1)}, f32[8192]{0:T(1024)}, u32[]{:S(2)}) copy-start(f32[8192]{0:T(1024)} %param.16) | copy-start | bytes 98308
  69.2 7.4 %copy-start.7 = (f32[8192]{0:T(1024)S(1)}, f32[8192]{0:T(1024)}, u32[]{:S(2)}) copy-start(f32[8192]{0:T(1024)} %param.17) | copy-start | bytes 98308
  69.2 7.4 %copy-start.8 = (s32[8192]{0:T(1024)S(1)}, s32[8192]{0:T(1024)}, u32[]{:S(2)}) copy-start(s32[8192]{0:T(1024)} %param.18) | copy-start | bytes 98308
  76.6 6.8 %copy-start.2 = (f32[1,4,512,512]{3,2,1,0:T(8,128)S(1)}, f32[1,4,512,512]{3,2,1,0:T(8,128)}, u32[]{:S(2)}) copy-start(f32[1,4,512,512]{3,2,1,0:T(8,128)} %tiles.5) | copy-start | bytes 12582916
  77.2 6.8 %collective-permute-start.5 = (f32[32,128]{1,0:T(8,128)S(1)}, f32[32,128]{1,0:T(8,128)S(1)}, u32[]{:S(2)}, u32[]{:S(2)}) collective-permute-start(f32[32,128]{1,0:T(8,128)S(1)} %get-tuple-element.34.p0), channel_id=1, source_target_pairs={{0,192},{64,128},{128,64},{192,0},{1,193},{65,129},{129,65},{193,1... | collective-permute-start | bytes 49160 | tf_op jit(solution)/shard_map/ppermute | solution.py:460
  82.6 4.1 %collective-permute-start.4 = (f32[32,128]{1,0:T(8,128)S(1)}, f32[32,128]{1,0:T(8,128)S(1)}, u32[]{:S(2)}, u32[]{:S(2)}) collective-permute-start(f32[32,128]{1,0:T(8,128)S(1)} %get-tuple-element.34.p0), channel_id=1, source_target_pairs={{0,128},{64,192},{128,0},{192,64},{1,129},{65,193},{129,1},{193,65... | collective-permute-start | bytes 49160 | tf_op jit(solution)/shard_map/ppermute | solution.py:460
  83.3 3.4 %collective-permute-start.3 = (f32[32,128]{1,0:T(8,128)S(1)}, f32[32,128]{1,0:T(8,128)S(1)}, u32[]{:S(2)}, u32[]{:S(2)}) collective-permute-start(f32[32,128]{1,0:T(8,128)S(1)} %get-tuple-element.34.p0), channel_id=1, source_target_pairs={{0,64},{64,0},{128,192},{192,128},{1,65},{65,1},{129,193},{193,129... | collective-permute-start | bytes 49160 | tf_op jit(solution)/shard_map/ppermute | solution.py:460
  112.6 5.3 %collective-permute-start.8 = (f32[32,128]{1,0:T(8,128)S(1)}, f32[32,128]{1,0:T(8,128)S(1)}, u32[]{:S(2)}, u32[]{:S(2)}) collective-permute-start(f32[32,128]{1,0:T(8,128)S(1)} %get-tuple-element.47.p0), channel_id=1, source_target_pairs={{0,192},{64,128},{128,64},{192,0},{1,193},{65,129},{129,65},{193,1... | collective-permute-start | bytes 49160 | tf_op jit(solution)/shard_map/ppermute | solution.py:460
  116.4 4.1 %collective-permute-start.7 = (f32[32,128]{1,0:T(8,128)S(1)}, f32[32,128]{1,0:T(8,128)S(1)}, u32[]{:S(2)}, u32[]{:S(2)}) collective-permute-start(f32[32,128]{1,0:T(8,128)S(1)} %get-tuple-element.47.p0), channel_id=1, source_target_pairs={{0,128},{64,192},{128,0},{192,64},{1,129},{65,193},{129,1},{193,65... | collective-permute-start | bytes 49160 | tf_op jit(solution)/shard_map/ppermute | solution.py:460
  117.3 3.2 %collective-permute-start.6 = (f32[32,128]{1,0:T(8,128)S(1)}, f32[32,128]{1,0:T(8,128)S(1)}, u32[]{:S(2)}, u32[]{:S(2)}) collective-permute-start(f32[32,128]{1,0:T(8,128)S(1)} %get-tuple-element.47.p0), channel_id=1, source_target_pairs={{0,64},{64,0},{128,192},{192,128},{1,65},{65,1},{129,193},{193,129... | collective-permute-start | bytes 49160 | tf_op jit(solution)/shard_map/ppermute | solution.py:460
